TPU v7x, 128 devices: a whole 4x4x4 slice. The times are simulated.
128 devices in a mesh: mx: 4 (over z), my: 4 (over y_hi, core), col: 8 (over y_lo, x).
Axes of the slice: x: 4, y: 4 (y_hi: 2, y_lo: 2; y = y_hi * 2 + y_lo), z: 4, core: 2. Of those that a mesh axis runs over, the one named last changes fastest.
Arguments:
- spectrum: float32 [2, 16, 128, 32, 512], P(None, 'col', None, 'mx', 'my'), may hold values from -6 to 6
- core_tensor: float32 [2, 64, 64, 16, 16, 16], P(None, 'col', None, ('mx', 'my')), may hold values from -0.01171875 to 0.01171875
- input_factor: float32 [128, 64], replicated, may hold values from -0.5 to 0.5
- output_factor: float32 [128, 64], replicated, may hold values from -0.75 to 0.75
- first_factor: float32 [32, 16], P('mx'), may hold values from -5 to 5
- second_factor: float32 [32, 16], P('my'), may hold values from -5 to 5
- third_factor: float32 [16, 16], replicated, may hold values from -5 to 5
Outputs:
- mixed_modes: float32 [2, 16, 128, 32, 512], P(None, 'col', None, 'mx', 'my')
All inputs are finite; a program needn't handle non-finite values.
Results may differ from a plain program's by a relative error of at most 0.00007.
Values sent between devices are 32-bit elements; how exact they have to be, the bound alone decides.
No kernel may reach another device: no remote copies, remote signals or barrier semaphores. Data moves between devices by JAX's collectives and lax.ppermute only.
A program may use at most 128 MiB of HBM per device.

v0:
```python
import jax
import jax.numpy as jnp
from jax import lax
from jax.sharding import PartitionSpec as P

precise = lax.Precision.HIGHEST


def per_device(
    spectrum, core_tensor, input_factor, output_factor, first_factor, second_factor, third_factor
):
    rank_local = core_tensor.shape[1]
    rank_out = core_tensor.shape[2]
    rows_first = first_factor.shape[0]
    rank_second = second_factor.shape[1]
    modes_third = third_factor.shape[0]
    core_third = jnp.einsum("cpqstu,zu->cpqstz", core_tensor, third_factor, precision=precise)
    core_third = core_third.reshape(
        2, rank_local, rank_out, core_tensor.shape[3], rank_second * modes_third
    )
    core_gathered = lax.all_gather(core_third, ("mx", "my"), axis=3, tiled=True)
    weight_first = jnp.einsum("cpqsm,ks->cpqkm", core_gathered, first_factor, precision=precise)
    weight_first = weight_first.reshape(
        2, rank_local, rank_out, rows_first, rank_second, modes_third
    )
    mode_weight = jnp.einsum("cpqktz,yt->cpqkyz", weight_first, second_factor, precision=precise)
    mode_weight = mode_weight.reshape(2, rank_local, rank_out, rows_first, -1)
    projected = jnp.einsum("cbikm,ir->cbrkm", spectrum, input_factor, precision=precise)
    rank_spectrum = lax.all_to_all(projected, "col", split_axis=2, concat_axis=1, tiled=True)
    real_part = jnp.einsum(
        "brkm,rqkm->bqkm", rank_spectrum[0], mode_weight[0], precision=precise
    ) - jnp.einsum("brkm,rqkm->bqkm", rank_spectrum[1], mode_weight[1], precision=precise)
    imag_part = jnp.einsum(
        "brkm,rqkm->bqkm", rank_spectrum[0], mode_weight[1], precision=precise
    ) + jnp.einsum("brkm,rqkm->bqkm", rank_spectrum[1], mode_weight[0], precision=precise)
    mode_values = jnp.stack([real_part, imag_part])
    summed_values = lax.psum_scatter(mode_values, "col", scatter_dimension=1, tiled=True)
    mixed_modes = jnp.einsum("oq,cbqkm->cbokm", output_factor, summed_values, precision=precise)
    return mixed_modes


def solution(mesh):
    placed = (
        P(None, "col", None, "mx", "my"),
        P(None, "col", None, ("mx", "my"), None, None),
        P(),
        P(),
        P("mx", None),
        P("my", None),
        P(),
    )
    return jax.shard_map(
        per_device,
        mesh=mesh,
        in_specs=placed,
        out_specs=P(None, "col", None, "mx", "my"),
        check_vma=False,
    )
```

profile of v0, /device:TPU:1, one launch (start us, length us, event | category | flops | bytes accessed | tf_op | source)
XLA Modules:
  0.0 377.2 jit_solution(9555578541024835973)
XLA Ops:
  6.5 1.6 copy-done
  8.1 3.9 %fusion.22 = f32[2,8,64,16,16]{2,4,3,1,0:T(8,128)} fusion(f32[2,8,64,1,16,16]{2,5,4,3,1,0:T(8,128)S(1)} %copy-done, f32[16,16]{1,0:T(8,128)} %param.13), kind=kOutput, calls=%fused_computation.17 | convolution fusion | flops 50331648 | bytes 2098176 | tf_op jit(solution)/shard_map/cpqstu,zu->cpqstz/dot_general | solution.py:17
  12.1 3.2 copy.51
  15.3 3.1 fusion.26
  19.0 20.6 %all_to_all.15 = f32[2,2,64,8,128]{4,3,1,0,2:T(8,128)S(1)} all-to-all(f32[2,2,64,8,128]{4,3,1,0,2:T(8,128)S(1)} %copy.57), channel_id=1, replica_groups=mesh['mx'=4,'my'=4,'col'=8] {'col'}, dimensions={2} | all-to-all | bytes 2097152 | tf_op jit(solution)/shard_map/all_to_all | solution.py:29
  39.9 3.2 copy.61
  43.1 3.1 copy.65
  46.2 90.1 %all-gather.2.cloned.1.call-done = f32[2,8,64,16,256]{4,2,1,0,3:T(8,128)} async-done(((f32[2,8,64,1,256]{4,2,1,0,3:T(8,128)}), f32[2,8,64,16,256]{4,2,1,0,3:T(8,128)}) %all-gather.2.cloned.1.call-update) | async-done | bytes 16777232 | tf_op jit(solution)/shard_map/all_gather | solution.py:21
  136.3 25.8 %fusion.16 = f32[2,8,64,8,256]{4,3,2,1,0:T(8,128)} fusion(f32[2,8,64,16,256]{4,2,1,0,3:T(8,128)} %all-gather.2.cloned.1.call-done, f32[8,16]{1,0:T(8,128)S(1)} %copy-done.6), kind=kOutput, calls=%fused_computation.15 | convolution fusion | flops 402653184 | bytes 25166336 | tf_op jit(solution)/shard_map/cpqsm,ks->cpqkm/dot_general | solution.py:22
  162.1 12.2 %copy.53 = f32[2,8,64,8,256]{2,4,3,1,0:T(8,128)} copy(f32[2,8,64,8,256]{4,3,2,1,0:T(8,128)} %fusion.16) | data formatting | bytes 16777216 | tf_op jit(solution)/shard_map/cpqsm,ks->cpqkm/transpose | solution.py:22
  174.3 17.9 %fusion.19 = f32[2,8,64,8,8,16]{2,4,5,3,1,0:T(8,128)S(1)} fusion(f32[2,8,64,8,16,16]{2,5,4,3,1,0:T(8,128)} %bitcast.59, f32[8,16]{1,0:T(8,128)S(1)} %copy-done.7), kind=kOutput, calls=%fused_computation.16 | convolution fusion | flops 201326592 | bytes 12583424 | tf_op jit(solution)/shard_map/cpqktz,yt->cpqkyz/dot_general | solution.py:26
  192.2 1.1 fusion.35
  193.3 0.9 copy.55
  194.2 0.9 copy.62
  195.2 1.2 copy-done.2
  196.4 14.4 %fusion.4 = f32[8,128,64,16]{2,3,1,0:T(8,128)S(1)} fusion(f32[16,8,8,128]{0,1,3,2:T(8,128)S(1)} %copy-done.2, f32[8,64,8,128]{1,3,2,0:T(8,128)S(1)} %bitcast.60), kind=kOutput, calls=%fused_computation.7 | convolution fusion | flops 100663296 | bytes 6815744 | tf_op jit(solution)/shard_map/brkm,rqkm->bqkm/dot_general | solution.py:33
  210.8 14.6 %fusion.6 = f32[8,128,64,16]{2,3,1,0:T(8,128)S(1)} fusion(f32[16,8,8,128]{0,1,3,2:T(8,128)S(1)} %copy-done.3, f32[8,64,8,128]{1,3,2,0:T(8,128)S(1)} %bitcast.61), kind=kOutput, calls=%fused_computation.9 | convolution fusion | flops 100663296 | bytes 6815744 | tf_op jit(solution)/shard_map/brkm,rqkm->bqkm/dot_general | solution.py:32
  225.4 14.3 %add_bitcast_fusion = f32[1,16,64,8,128]{2,1,4,3,0:T(8,128)S(1)} fusion(f32[8,128,64,16]{2,3,1,0:T(8,128)S(1)} %fusion.4, f32[16,8,8,128]{0,1,3,2:T(8,128)S(1)} %copy-done.3, f32[8,64,8,128]{1,3,2,0:T(8,128)S(1)} %bitcast.57), kind=kOutput, calls=%fused_computation.5 | convolution fusion | flops 101711872 | bytes 11010048 | tf_op jit(solution)/shard_map/brkm,rqkm->bqkm/dot_general | solution.py:35
  239.8 14.4 %subtract_bitcast_fusion = f32[1,16,64,8,128]{2,1,4,3,0:T(8,128)S(1)} fusion(f32[8,128,64,16]{2,3,1,0:T(8,128)S(1)} %fusion.6, f32[16,8,8,128]{0,1,3,2:T(8,128)S(1)} %copy-done.2, f32[8,64,8,128]{1,3,2,0:T(8,128)S(1)} %bitcast.58), kind=kOutput, calls=%fused_computation.6 | convolution fusion | flops 101711872 | bytes 11010048 | tf_op jit(solution)/shard_map/brkm,rqkm->bqkm/dot_general | solution.py:30
  254.2 6.1 %pad_maximum_fusion = f32[2,16,64,8,128]{2,1,4,3,0:T(8,128)} fusion(f32[1,16,64,8,128]{2,1,4,3,0:T(8,128)S(1)} %add_bitcast_fusion, f32[1,16,64,8,128]{2,1,4,3,0:T(8,128)S(1)} %subtract_bitcast_fusion), kind=kLoop, calls=%fused_computation | loop fusion | flops 2097152 | bytes 16777216 | tf_op jit(solution)/shard_map/stack | solution.py:36
  260.3 11.0 %copy.70 = f32[2,16,64,8,128]{4,3,2,0,1:T(8,128)} copy(f32[2,16,64,8,128]{2,1,4,3,0:T(8,128)} %pad_maximum_fusion) | data formatting | bytes 16777216 | tf_op jit(solution)/shard_map/stack | solution.py:36
  271.3 89.9 %reduce-scatter.2.cloned.1.call-done = f32[2,2,64,8,128]{4,3,2,0,1:T(8,128)} async-done(((f32[2,16,64,8,128]{4,3,2,0,1:T(8,128)}), f32[2,2,64,8,128]{4,3,2,0,1:T(8,128)}) %reduce-scatter.2.cloned.1.call-update) | async-done | bytes 1048592 | tf_op jit(solution)/shard_map/reduce_scatter | solution.py:37
  361.2 6.0 %convolution_bitcast_fusion = f32[2,2,128,8,128]{2,4,3,1,0:T(8,128)} fusion(f32[2,2,64,8,128]{4,3,2,0,1:T(8,128)} %reduce-scatter.2.cloned.1.call-done, f32[128,64]{0,1:T(8,128)S(1)} %copy-done.5), kind=kOutput, calls=%fused_computation.21 | convolution fusion | flops 402653184 | bytes 3178496 | tf_op jit(solution)/shard_map/oq,cbqkm->cbokm/dot_general | solution.py:38
  367.2 2.9 copy.72
  (23 shorter events, 1.0 us)
Async XLA Ops:
  6.5 1.6 copy-start
  6.5 8.8 %copy-start.4 = (f32[128,64]{0,1:T(8,128)S(1)}, f32[128,64]{0,1:T(8,128)}, u32[]{:S(2)}) copy-start(f32[128,64]{0,1:T(8,128)} %param.9) | copy-start | bytes 98308
  6.5 129.7 %all-gather.2.cloned.1.call-start = ((), (), s32[]{:S(2)}) async-start(), calls=%async_computation.2 | async-start | bytes 17825792 | tf_op jit(solution)/shard_map/all_gather | solution.py:21
  15.2 346.0 %reduce-scatter.2.cloned.1.call-start = ((), (), s32[]{:S(2)}) async-start(), calls=%async_computation.3 | async-start | bytes 9437184 | tf_op jit(solution)/shard_map/reduce_scatter | solution.py:37
  39.9 96.3 %copy-start.6 = (f32[8,16]{1,0:T(8,128)S(1)}, f32[8,16]{1,0:T(8,128)}, u32[]{:S(2)}) copy-start(f32[8,16]{1,0:T(8,128)} %param.11) | copy-start | bytes 1540
  162.1 12.2 %copy-start.7 = (f32[8,16]{1,0:T(8,128)S(1)}, f32[8,16]{1,0:T(8,128)}, u32[]{:S(2)}) copy-start(f32[8,16]{1,0:T(8,128)} %param.12) | copy-start | bytes 1540
  194.2 2.2 copy-start.2
  196.4 14.4 %copy-start.3 = (f32[16,8,8,128]{0,1,3,2:T(8,128)S(1)}, f32[16,8,8,128]{0,1,3,2:T(8,128)}, u32[]{:S(2)}) copy-start(f32[16,8,8,128]{0,1,3,2:T(8,128)} %copy.65) | copy-start | bytes 1572868
  271.3 89.9 %copy-start.5 = (f32[128,64]{0,1:T(8,128)S(1)}, f32[128,64]{0,1:T(8,128)}, u32[]{:S(2)}) copy-start(f32[128,64]{0,1:T(8,128)} %param.10) | copy-start | bytes 98308
  271.3 98.8 %copy-start.1 = (f32[2,8,64,1,16,16]{2,5,4,3,1,0:T(8,128)S(1)}, f32[2,8,64,1,16,16]{2,5,4,3,1,0:T(8,128)}, u32[]{:S(2)}) copy-start(f32[2,8,64,1,16,16]{2,5,4,3,1,0:T(8,128)} %param.8) | copy-start | bytes 3145732
Sparse Core Ops, SparseCore 0:
  15.4 120.8 all-gather.1
  271.4 89.7 reduce-scatter.1
where the time goes:
time: 383 us; the launch traced here: 377 us
  waiting for transfers between devices  180 us (47%)
  matrix products  114 us (30%)
  local copies, waits for them, and re-layouts  42.2 us (11%)
  blocking collectives  20.6 us (5%)
  between operations  13.8 us (4%)
  other arithmetic  6.1 us (2%)
    all_gather x1, waiting for transfers between devices, per_device(): core_gathered = lax.all_gather(core_third, ('mx', 'my'), axis=3, tiled=True)  90.1 us
    reduce_scatter x1, waiting for transfers between devices, per_device(): lax.psum_scatter(mode_values, 'col', scatter_dimension=1, tiled=True)  89.9 us
    dot_general x1, matrix products, per_device(): jnp.einsum('cpqsm,ks->cpqkm', core_gathered, first_factor, precision=prec...  25.8 us
    all_to_all x1, blocking collectives, per_device(): lax.all_to_all(projected, 'col', split_axis=2, concat_axis=1, tiled=True)  20.6 us
    dot_general x1, matrix products, per_device(): jnp.einsum('cpqktz,yt->cpqkyz', weight_first, second_factor, precision=pr...  17.9 us
    dot_general x1, matrix products, per_device(): jnp.einsum('brkm,rqkm->bqkm', rank_spectrum[1], mode_weight[1], precision...  14.6 us
    dot_general x1, matrix products, per_device(): jnp.einsum('brkm,rqkm->bqkm', rank_spectrum[0], mode_weight[1], precision...  14.4 us
    dot_general x1, matrix products, per_device(): jnp.einsum('brkm,rqkm->bqkm', rank_spectrum[0], mode_weight[0], precision...  14.4 us
  transfers between devices with their start and end apart: 2, of which 2 were waited for; matrix products, arithmetic and copies ran while one was open for 3% of the time, Pallas kernels for 0%

commit v1 on v0

v1 whole, which is shorter than its diff:
```python
import functools

import jax
import jax.numpy as jnp
from jax import lax
from jax.experimental import pallas as pl
from jax.experimental.pallas import tpu as pltpu
from jax.sharding import PartitionSpec as P

precise = lax.Precision.HIGHEST
LANES = 128


def dot(a, b, contract=(1, 0)):
    return lax.dot_general(
        a, b, (((contract[0],), (contract[1],)), ((), ())),
        precision=precise, preferred_element_type=jnp.float32,
    )


def iota(shape, dim):
    return lax.broadcasted_iota(jnp.int32, shape, dim)


def core_kernel(core_ref, second_ref, third_ref, out_ref, mat_ref):
    @pl.when(pl.program_id(0) == 0)
    def _():
        def picks(width):
            row, col = iota((512, width), 0), iota((512, width), 1)
            c, b, a, r = row & 7, (row >> 3) & 3, (row >> 5) & 3, row >> 7
            return col, 8 * b + 2 * r + (a >> 1), (a & 1) * 8 + c

        col, ky, _ = picks(second_ref.shape[0])
        rows_y = dot((col == ky).astype(jnp.float32), second_ref[...])
        col, _, kz = picks(third_ref.shape[0])
        rows_z = dot((col == kz).astype(jnp.float32), third_ref[...])
        of_t = (iota((16, 256), 1) >> 4 == iota((16, 256), 0)).astype(jnp.float32)
        of_u = (iota((16, 256), 1) & 15 == iota((16, 256), 0)).astype(jnp.float32)
        mat_ref[...] = dot(rows_y, of_t) * dot(rows_z, of_u)

    both = jnp.concatenate([core_ref[0, 0], core_ref[0, 1], core_ref[1, 0], core_ref[1, 1]], axis=1)
    out = dot(mat_ref[...], both)
    for part in range(2):
        for r in range(4):
            out_ref[pl.ds(part * 4 + r, 128, stride=8), :] = out[
                r * 128 : (r + 1) * 128, part * LANES : (part + 1) * LANES
            ]


def core_chunks(core, second, third):
    return pl.pallas_call(
        core_kernel,
        grid=(4,),
        in_specs=[
            pl.BlockSpec((2, 2, 256, 64), lambda i: (0, i, 0, 0)),
            pl.BlockSpec(second.shape, lambda i: (0, 0)),
            pl.BlockSpec(third.shape, lambda i: (0, 0)),
        ],
        out_specs=pl.BlockSpec((1024, LANES), lambda i: (0, i)),
        out_shape=jax.ShapeDtypeStruct((1024, 512), jnp.float32),
        scratch_shapes=[pltpu.VMEM((512, 256), jnp.float32)],
        name="core_chunks",
    )(core, second, third)


def spectrum_kernel(spec_ref, factor_ref, out_ref):
    factor = factor_ref[...]
    for k in range(8):
        halves = [dot(factor, spec_ref[0, b, pl.ds(k, 128, stride=8), :]) for b in range(2)]
        turned = jnp.concatenate(halves, axis=0).T
        for r in range(4):
            out_ref[pl.ds(k * 4 + r, 32, stride=32), :] = turned[r * 32 : (r + 1) * 32]


def spectrum_chunks(spec, factor):
    return pl.pallas_call(
        spectrum_kernel,
        grid=(2,),
        in_specs=[
            pl.BlockSpec((1, 2, 1024, LANES), lambda i: (i, 0, 0, 0)),
            pl.BlockSpec((64, 128), lambda i: (0, 0)),
        ],
        out_specs=pl.BlockSpec((1024, LANES), lambda i: (0, i)),
        out_shape=jax.ShapeDtypeStruct((1024, 256), jnp.float32),
        name="spectrum_chunks",
    )(spec, factor)


def mode_kernel(core_ref, spec_ref, first_ref, out_ref, w_ref, x_ref, v_ref):
    of_s = (iota((128, 16), 0) >> 3 == iota((128, 16), 1)).astype(jnp.float32)
    of_k = ((iota((32, 256), 1) >> 2) & 31 == iota((32, 256), 0)).astype(jnp.float32)
    row, col = iota((128, 256), 0), iota((128, 256), 1)
    same = (((row >> 2) & 1) == (col >> 7)) & ((row & 3) == (col & 3))
    expand = jnp.where(same, dot(dot(of_s, first_ref[...], (1, 1)), of_k), 0.0)

    for src in range(8):
        for pair in range(4):
            block = core_ref[:, src, :, pair * LANES : (pair + 1) * LANES].reshape(128, LANES)
            w = dot(block.T, expand)
            for half in range(2):
                rows = w[half * 64 : (half + 1) * 64]
                p = src * 8 + pair * 2 + half
                w_ref[p, 0] = rows[:, :LANES]
                w_ref[p, 1] = rows[:, LANES:]
                w_ref[p, 2] = rows[:, :LANES] + rows[:, LANES:]

    for src in range(8):
        parts = [
            spec_ref[:, src, :, part * LANES : (part + 1) * LANES].reshape(128, LANES).T
            for part in range(2)
        ]
        parts.append(parts[0] + parts[1])
        for part in range(3):
            for b in range(2):
                x_ref[src * 2 + b, part] = parts[part][b * 64 : (b + 1) * 64]

    @pl.loop(0, 16)
    def _(step):
        samples, q0 = step // 4 * 4, pl.multiple_of(step % 4 * 16, 16)

        def one(p, sums):
            w = [w_ref[p, part, pl.ds(q0, 16), :] for part in range(3)]
            return tuple(
                sums[b * 3 + part] + x_ref[samples + b, part, pl.ds(p, 1), :] * w[part]
                for b in range(4)
                for part in range(3)
            )

        zero = jnp.zeros((16, LANES), jnp.float32)
        sums = lax.fori_loop(0, 64, one, (zero,) * 12, unroll=8)
        for b in range(4):
            rr, ii, mixed = sums[b * 3 : b * 3 + 3]
            v_ref[samples + b, 0, pl.ds(q0, 16), :] = rr - ii
            v_ref[samples + b, 1, pl.ds(q0, 16), :] = mixed - rr - ii

    for src in range(8):
        for part in range(2):
            both = jnp.concatenate([v_ref[src * 2, part], v_ref[src * 2 + 1, part]], axis=0)
            out_ref[:, src, :, part * LANES : (part + 1) * LANES] = both.T.reshape(4, 32, LANES)


def mode_products(core, spec, first):
    return pl.pallas_call(
        mode_kernel,
        out_shape=jax.ShapeDtypeStruct((4, 8, 32, 256), jnp.float32),
        scratch_shapes=[
            pltpu.VMEM((64, 3, 64, LANES), jnp.float32),
            pltpu.VMEM((16, 3, 64, LANES), jnp.float32),
            pltpu.VMEM((16, 2, 64, LANES), jnp.float32),
        ],
        name="mode_products",
    )(core, spec, first)


def output_kernel(value_ref, factor_ref, out_ref):
    factor = factor_ref[...].T
    for k in range(8):
        rows = [value_ref[pl.ds(k * 4 + r, 32, stride=32), :] for r in range(4)]
        turned = jnp.concatenate(rows, axis=0).T
        for b in range(2):
            out_ref[0, b, pl.ds(k, 128, stride=8), :] = dot(factor, turned[b * 64 : (b + 1) * 64])


def output_modes(values, factor):
    return pl.pallas_call(
        output_kernel,
        grid=(2,),
        in_specs=[
            pl.BlockSpec((1024, LANES), lambda i: (0, i)),
            pl.BlockSpec((64, 128), lambda i: (0, 0)),
        ],
        out_specs=pl.BlockSpec((1, 2, 1024, LANES), lambda i: (i, 0, 0, 0)),
        out_shape=jax.ShapeDtypeStruct((2, 2, 1024, LANES), jnp.float32),
        name="output_modes",
    )(values, factor)


def swap(chunks, axes):
    return lax.all_to_all(chunks, axes, split_axis=0, concat_axis=0, tiled=True)


def per_device(
    spectrum, core_tensor, input_factor, output_factor, first_factor, second_factor, third_factor
):
    second = lax.all_gather(second_factor, "my", axis=0, tiled=True)
    first = lax.all_gather(first_factor, "mx", axis=0, tiled=True)
    core = jnp.transpose(core_tensor, (0, 1, 3, 4, 5, 2)).reshape(2, 8, 256, 64)
    core = core_chunks(core, second, third_factor)
    core = swap(core.reshape(128, 8, 512), ("mx", "my", "col"))
    spec = spectrum_chunks(spectrum.reshape(2, 2, 1024, LANES), input_factor.T)
    spec = swap(spec.reshape(32, 32, 256), ("mx", "col"))
    values = mode_products(core.reshape(16, 8, 8, 512), spec.reshape(4, 8, 32, 256), first)
    values = swap(values.reshape(32, 32, 256), ("mx", "col"))
    out = output_modes(values.reshape(1024, 256), output_factor.T)
    return out.reshape(spectrum.shape)


def solution(mesh):
    placed = (
        P(None, "col", None, "mx", "my"),
        P(None, "col", None, ("mx", "my"), None, None),
        P(),
        P(),
        P("mx", None),
        P("my", None),
        P(),
    )
    return jax.shard_map(
        per_device,
        mesh=mesh,
        in_specs=placed,
        out_specs=P(None, "col", None, "mx", "my"),
        check_vma=False,
    )
```

time: 383 us -> 121 us (0.32); the launches traced: 377 us -> 120 us
  waiting for transfers between devices: 180 us -> 12.6 us
  matrix products: 114 us -> 0 us
  local copies, waits for them, and re-layouts: 42.2 us -> 2.35 us
  Pallas kernels: 0 us -> 33.7 us
  blocking collectives: 20.6 us -> 50.2 us
  starting transfers between devices: 0.04 us -> 20.7 us
  between operations: 13.8 us -> 0.05 us
  other arithmetic: 6.1 us -> 0 us
    dot_general x9 -> x0, matrix products: 114 us -> none  [the longest x1 25.8 us: per_device(): jnp.einsum('cpqsm,ks->cpqkm', core_gathered, first_factor, precision=prec...]
    all_gather x1 -> x0, waiting for transfers between devices: 90.1 us -> none  [per_device(): core_gathered = lax.all_gather(core_third, ('mx', 'my'), axis=3, tiled=True)]
    reduce_scatter x1 -> x0, waiting for transfers between devices: 89.9 us -> none  [per_device(): lax.psum_scatter(mode_values, 'col', scatter_dimension=1, tiled=True)]
    pallas_call x0 -> x4, Pallas kernels: none -> 33.7 us  [the longest x1 15.4 us: mode_products(): pl.pallas_call(mode_kernel, out_shape=jax.ShapeDtypeStruct((4, 8, 32, 256...]
    all_gather x0 -> x2, blocking collectives: none -> 30.4 us  [the longest x1 17.7 us: per_device(): first = lax.all_gather(first_factor, 'mx', axis=0, tiled=True)]
    all_to_all x0 -> x2, starting transfers between devices: none -> 20.7 us  [swap(): return lax.all_to_all(chunks, axes, split_axis=0, concat_axis=0, tiled=True)]
    transpose x3 -> x0, local copies, waits for them, and re-layouts: 15.7 us -> none  [the longest x1 12.2 us: per_device(): jnp.einsum('cpqsm,ks->cpqkm', core_gathered, first_factor, precision=prec...]
    all_to_all x0 -> x2, waiting for transfers between devices: none -> 12.6 us  [swap(): return lax.all_to_all(chunks, axes, split_axis=0, concat_axis=0, tiled=True)]
  transfers between devices with their start and end apart: 2 -> 2, of which waited for: 2 -> 1; matrix products, arithmetic and copies ran while one was open for 3% -> 0% of each run, Pallas kernels for 0% -> 6%
where the time goes in v1:
time: 121 us; the launch traced here: 120 us
  blocking collectives  50.2 us (41%)
  Pallas kernels  33.7 us (28%)
  starting transfers between devices  20.7 us (17%)
  waiting for transfers between devices  12.6 us (10%)
  local copies, waits for them, and re-layouts  2.35 us (2%)
    all_to_all x2, starting transfers between devices, swap(): return lax.all_to_all(chunks, axes, split_axis=0, concat_axis=0, tiled=True)  20.7 us
    all_to_all x1, blocking collectives, swap(): return lax.all_to_all(chunks, axes, split_axis=0, concat_axis=0, tiled=True)  19.8 us
    all_gather x1, blocking collectives, per_device(): first = lax.all_gather(first_factor, 'mx', axis=0, tiled=True)  17.7 us
    pallas_call x1, Pallas kernels, mode_products(): pl.pallas_call(mode_kernel, out_shape=jax.ShapeDtypeStruct((4, 8, 32, 256...  15.4 us
    all_gather x1, blocking collectives, per_device(): second = lax.all_gather(second_factor, 'my', axis=0, tiled=True)  12.7 us
    all_to_all x2, waiting for transfers between devices, swap(): return lax.all_to_all(chunks, axes, split_axis=0, concat_axis=0, tiled=True)  12.6 us
    pallas_call x1, Pallas kernels, output_modes(): pl.pallas_call(output_kernel, grid=(2,), in_specs=[pl.BlockSpec((1024, LA...  6.99 us
    pallas_call x1, Pallas kernels, core_chunks(): pl.pallas_call(core_kernel, grid=(4,), in_specs=[pl.BlockSpec((2, 2, 256,...  6.8 us
  transfers between devices with their start and end apart: 2, of which 1 were waited for; matrix products, arithmetic and copies ran while one was open for 0% of the time, Pallas kernels for 6%

profile of v1, /device:TPU:1, one launch (start us, length us, event | category | flops | bytes accessed | tf_op | source)
XLA Modules:
  0.0 119.7 jit_solution(8938973831846448677)
XLA Ops:
  0.0 0.0 copy-start.2
  0.0 4.5 %spectrum_chunks.1 = f32[1024,256]{1,0:T(8,128)} custom-call(f32[2,2,1024,128]{3,2,1,0:T(8,128)} %bitcast.19, f32[64,128]{1,0:T(8,128)} %bitcast.21), custom_call_target="tpu_custom_call" | custom-call | tf_op jit(solution)/shard_map/spectrum_chunks/pallas_call | solution.py:76
  4.5 9.7 %all-to-all-start.1 = ((f32[32,32,256]{2,1,0:T(8,128)}), f32[32,32,256]{2,1,0:T(8,128)S(1)}, u32[]{:S(2)}, u32[]{:S(2)}) async-start(f32[32,32,256]{2,1,0:T(8,128)} %bitcast.15), calls=%async_computation.1 | async-start | bytes 2097152 | tf_op jit(solution)/shard_map/all_to_all | solution.py:179
  14.3 0.0 copy-done.2
  14.3 12.7 %all_gather.6.second_ref = f32[32,16]{1,0:T(8,128)} all-gather(f32[8,16]{1,0:T(8,128)S(1)} %copy-done.2), channel_id=1, replica_groups=mesh['mx'=4,'my'=4,'col'=8] {'my'}, dimensions={0}, use_global_device_ids=true | all-gather | bytes 2560 | tf_op jit(solution)/shard_map/all_gather | solution.py:185
  27.0 6.8 %core_chunks.1 = f32[1024,512]{1,0:T(8,128)} custom-call(f32[2,8,256,64]{3,2,1,0:T(8,128)} %bitcast.20, f32[32,16]{1,0:T(8,128)} %all_gather.6.second_ref, f32[16,16]{1,0:T(8,128)} %third_ref.1), custom_call_target="tpu_custom_call" | custom-call | tf_op jit(solution)/shard_map/core_chunks/pallas_call | solution.py:51
  33.8 0.0 all-to-all-done.1
  33.8 0.0 copy-start.1
  33.8 0.0 copy-start.3
  33.8 1.0 copy-done.1
  34.8 11.0 %all-to-all-start = ((f32[128,8,512]{2,1,0:T(8,128)}), f32[128,8,512]{2,1,0:T(8,128)S(1)}, u32[]{:S(2)}, u32[]{:S(2)}) async-start(f32[128,8,512]{2,1,0:T(8,128)} %bitcast.13), calls=%async_computation | async-start | bytes 4194304 | tf_op jit(solution)/shard_map/all_to_all | solution.py:179
  45.8 0.0 copy-done.3
  45.8 17.7 %all_gather.7.first_ref = f32[32,16]{1,0:T(8,128)} all-gather(f32[8,16]{1,0:T(8,128)S(1)} %copy-done.3), channel_id=1, replica_groups=mesh['mx'=4,'my'=4,'col'=8] {'mx'}, dimensions={0}, use_global_device_ids=true | all-gather | bytes 2560 | tf_op jit(solution)/shard_map/all_gather | solution.py:186
  63.5 12.6 %all-to-all-done = f32[128,8,512]{2,1,0:T(8,128)S(1)} async-done(((f32[128,8,512]{2,1,0:T(8,128)}), f32[128,8,512]{2,1,0:T(8,128)S(1)}, u32[]{:S(2)}, u32[]{:S(2)}) %all-to-all-start) | async-done | bytes 2097184 | tf_op jit(solution)/shard_map/all_to_all | solution.py:179
  76.1 0.0 copy-start
  76.1 1.3 %copy-done = f32[128,8,512]{2,1,0:T(8,128)} copy-done((f32[128,8,512]{2,1,0:T(8,128)}, f32[128,8,512]{2,1,0:T(8,128)S(1)}, u32[]{:S(2)}) %copy-start) | copy-done | bytes 2097176
  77.5 15.4 %mode_products.1 = f32[4,8,32,256]{3,2,1,0:T(8,128)} custom-call(f32[16,8,8,512]{3,2,1,0:T(8,128)} %bitcast.14, f32[4,8,32,256]{3,2,1,0:T(8,128)} %bitcast.17, f32[32,16]{1,0:T(8,128)} %all_gather.7.first_ref), custom_call_target="tpu_custom_call" | custom-call | tf_op jit(solution)/shard_map/mode_products/pallas_call | solution.py:143
  92.9 19.8 %all_to_all.15 = f32[32,32,256]{2,1,0:T(8,128)} all-to-all(f32[32,32,256]{2,1,0:T(8,128)} %bitcast.18), channel_id=1, replica_groups=mesh['mx'=4,'my'=4,'col'=8] {'mx','col'}, dimensions={0} | all-to-all | bytes 2097152 | tf_op jit(solution)/shard_map/all_to_all | solution.py:179
  112.7 7.0 %output_modes.1 = f32[2,2,1024,128]{3,2,1,0:T(8,128)} custom-call(f32[1024,256]{1,0:T(8,128)} %bitcast.16, f32[64,128]{1,0:T(8,128)} %bitcast.22), custom_call_target="tpu_custom_call" | custom-call | tf_op jit(solution)/shard_map/output_modes/pallas_call | solution.py:165
Async XLA Ops:
  0.0 14.3 %copy-start.2 = (f32[8,16]{1,0:T(8,128)S(1)}, f32[8,16]{1,0:T(8,128)}, u32[]{:S(2)}) copy-start(f32[8,16]{1,0:T(8,128)} %param.12) | copy-start | bytes 1540
  4.5 29.3 %all-to-all-start.1 = ((f32[32,32,256]{2,1,0:T(8,128)}), f32[32,32,256]{2,1,0:T(8,128)S(1)}, u32[]{:S(2)}, u32[]{:S(2)}) async-start(f32[32,32,256]{2,1,0:T(8,128)} %bitcast.15), calls=%async_computation.1 | async-start | bytes 2097152 | tf_op jit(solution)/shard_map/all_to_all | solution.py:179
  33.8 1.0 copy-start.1
  33.8 12.0 %copy-start.3 = (f32[8,16]{1,0:T(8,128)S(1)}, f32[8,16]{1,0:T(8,128)}, u32[]{:S(2)}) copy-start(f32[8,16]{1,0:T(8,128)} %param.11) | copy-start | bytes 1540
  34.8 41.3 %all-to-all-start = ((f32[128,8,512]{2,1,0:T(8,128)}), f32[128,8,512]{2,1,0:T(8,128)S(1)}, u32[]{:S(2)}, u32[]{:S(2)}) async-start(f32[128,8,512]{2,1,0:T(8,128)} %bitcast.13), calls=%async_computation | async-start | bytes 4194304 | tf_op jit(solution)/shard_map/all_to_all | solution.py:179
  76.1 1.3 %copy-start = (f32[128,8,512]{2,1,0:T(8,128)}, f32[128,8,512]{2,1,0:T(8,128)S(1)}, u32[]{:S(2)}) copy-start(f32[128,8,512]{2,1,0:T(8,128)S(1)} %all-to-all-done) | copy-start | bytes 6291460

commit v2 on v1

--- a/solution.py
+++ b/solution.py
@@ -7,39 +7,63 @@
 from jax.experimental.pallas import tpu as pltpu
 from jax.sharding import PartitionSpec as P
 
-precise = lax.Precision.HIGHEST
 LANES = 128
-
-
-def dot(a, b, contract=(1, 0)):
-    return lax.dot_general(
-        a, b, (((contract[0],), (contract[1],)), ((), ())),
-        precision=precise, preferred_element_type=jnp.float32,
-    )
+VMEM_SMALL = 16 * 2**20
+VMEM_LARGE = 32 * 2**20
+
+
+def dot(a, b):
+    return jnp.dot(a, b, preferred_element_type=jnp.float32)
+
+
+def split(x):
+    high = x.astype(jnp.bfloat16)
+    return high, (x - high.astype(jnp.float32)).astype(jnp.bfloat16)
+
+
+def split3(x):
+    high, rest = x.astype(jnp.bfloat16), None
+    rest = x - high.astype(jnp.float32)
+    return (high, *split(rest))
 
 
 def iota(shape, dim):
     return lax.broadcasted_iota(jnp.int32, shape, dim)
 
 
-def core_kernel(core_ref, second_ref, third_ref, out_ref, mat_ref):
+def pick(chosen, table):
+    one = chosen.astype(jnp.bfloat16)
+    high, mid, low = split3(table)
+    return (dot(one, high) + dot(one, mid)) + dot(one, low)
+
+
+def pick_lanes(table, chosen):
+    one = chosen.astype(jnp.bfloat16)
+    high, mid, low = split3(table)
+    return (dot(high, one) + dot(mid, one)) + dot(low, one)
+
+
+def core_kernel(core_ref, factors_ref, third_ref, out_ref, mat_ref):
     @pl.when(pl.program_id(0) == 0)
     def _():
-        def picks(width):
+        def place(width):
             row, col = iota((512, width), 0), iota((512, width), 1)
             c, b, a, r = row & 7, (row >> 3) & 3, (row >> 5) & 3, row >> 7
             return col, 8 * b + 2 * r + (a >> 1), (a & 1) * 8 + c
 
-        col, ky, _ = picks(second_ref.shape[0])
-        rows_y = dot((col == ky).astype(jnp.float32), second_ref[...])
-        col, _, kz = picks(third_ref.shape[0])
-        rows_z = dot((col == kz).astype(jnp.float32), third_ref[...])
-        of_t = (iota((16, 256), 1) >> 4 == iota((16, 256), 0)).astype(jnp.float32)
-        of_u = (iota((16, 256), 1) & 15 == iota((16, 256), 0)).astype(jnp.float32)
-        mat_ref[...] = dot(rows_y, of_t) * dot(rows_z, of_u)
+        of_t = iota((16, 256), 1) >> 4 == iota((16, 256), 0)
+        of_u = iota((16, 256), 1) & 15 == iota((16, 256), 0)
+        second = pick_lanes(factors_ref[:32, 16:32], of_t)
+        third = pick_lanes(third_ref[...], of_u)
+        col, ky, _ = place(32)
+        by_y = pick(col == ky, second)
+        col, _, kz = place(16)
+        mat = by_y * pick(col == kz, third)
+        mat_ref[0], mat_ref[1] = split(mat)
 
     both = jnp.concatenate([core_ref[0, 0], core_ref[0, 1], core_ref[1, 0], core_ref[1, 1]], axis=1)
-    out = dot(mat_ref[...], both)
+    high, low = split(both)
+    out = dot(mat_ref[0], high) + dot(mat_ref[0], low) + dot(mat_ref[1], high)
     for part in range(2):
         for r in range(4):
             out_ref[pl.ds(part * 4 + r, 128, stride=8), :] = out[
@@ -47,27 +71,35 @@
             ]
 
 
-def core_chunks(core, second, third):
+def core_chunks(core, factors, third):
     return pl.pallas_call(
         core_kernel,
         grid=(4,),
         in_specs=[
             pl.BlockSpec((2, 2, 256, 64), lambda i: (0, i, 0, 0)),
-            pl.BlockSpec(second.shape, lambda i: (0, 0)),
+            pl.BlockSpec((128, LANES), lambda i: (0, 0)),
             pl.BlockSpec(third.shape, lambda i: (0, 0)),
         ],
         out_specs=pl.BlockSpec((1024, LANES), lambda i: (0, i)),
         out_shape=jax.ShapeDtypeStruct((1024, 512), jnp.float32),
-        scratch_shapes=[pltpu.VMEM((512, 256), jnp.float32)],
+        scratch_shapes=[pltpu.VMEM((2, 512, 256), jnp.bfloat16)],
+        compiler_params=pltpu.CompilerParams(vmem_limit_bytes=VMEM_SMALL),
         name="core_chunks",
-    )(core, second, third)
+    )(core, factors, third)
 
 
 def spectrum_kernel(spec_ref, factor_ref, out_ref):
-    factor = factor_ref[...]
+    high, low = split(factor_ref[...])
+    rows = jnp.concatenate(
+        [jnp.concatenate([high, high], axis=1), jnp.concatenate([low, low], axis=1)], axis=0
+    )
     for k in range(8):
-        halves = [dot(factor, spec_ref[0, b, pl.ds(k, 128, stride=8), :]) for b in range(2)]
-        turned = jnp.concatenate(halves, axis=0).T
+        both = jnp.concatenate(
+            [spec_ref[0, b, pl.ds(k, 128, stride=8), :] for b in range(2)], axis=1
+        )
+        out = dot(rows, jnp.concatenate(split(both), axis=0))
+        out = out[:64] + out[64:]
+        turned = jnp.concatenate([out[:, :LANES], out[:, LANES:]], axis=0).T
         for r in range(4):
             out_ref[pl.ds(k * 4 + r, 32, stride=32), :] = turned[r * 32 : (r + 1) * 32]
 
@@ -82,21 +114,28 @@
         ],
         out_specs=pl.BlockSpec((1024, LANES), lambda i: (0, i)),
         out_shape=jax.ShapeDtypeStruct((1024, 256), jnp.float32),
+        compiler_params=pltpu.CompilerParams(vmem_limit_bytes=VMEM_SMALL),
         name="spectrum_chunks",
     )(spec, factor)
 
 
-def mode_kernel(core_ref, spec_ref, first_ref, out_ref, w_ref, x_ref, v_ref):
-    of_s = (iota((128, 16), 0) >> 3 == iota((128, 16), 1)).astype(jnp.float32)
-    of_k = ((iota((32, 256), 1) >> 2) & 31 == iota((32, 256), 0)).astype(jnp.float32)
+def mode_kernel(core_ref, spec_ref, factors_ref, out_ref, w_ref, x_ref, v_ref):
+    of_s = iota((128, 16), 0) >> 3 == iota((128, 16), 1)
+    kx = (iota((128, 256), 1) >> 2) & 31
+    of_k = (kx >> 3) * 32 + (kx & 7) == iota((128, 256), 0)
     row, col = iota((128, 256), 0), iota((128, 256), 1)
     same = (((row >> 2) & 1) == (col >> 7)) & ((row & 3) == (col & 3))
-    expand = jnp.where(same, dot(dot(of_s, first_ref[...], (1, 1)), of_k), 0.0)
+    first = pick_lanes(factors_ref[...].T[:16], of_k)
+    expand = jnp.where(same, pick(of_s, first), 0.0)
+    high, low = split(expand)
+    expand_high = jnp.concatenate([high, high], axis=0)
+    expand_low = jnp.concatenate([low, low], axis=0)
 
     for src in range(8):
         for pair in range(4):
             block = core_ref[:, src, :, pair * LANES : (pair + 1) * LANES].reshape(128, LANES)
-            w = dot(block.T, expand)
+            turned = jnp.concatenate(split(block.T), axis=1)
+            w = dot(turned, expand_high) + dot(turned, expand_low)
             for half in range(2):
                 rows = w[half * 64 : (half + 1) * 64]
                 p = src * 8 + pair * 2 + half
@@ -139,7 +178,7 @@
             out_ref[:, src, :, part * LANES : (part + 1) * LANES] = both.T.reshape(4, 32, LANES)
 
 
-def mode_products(core, spec, first):
+def mode_products(core, spec, factors):
     return pl.pallas_call(
         mode_kernel,
         out_shape=jax.ShapeDtypeStruct((4, 8, 32, 256), jnp.float32),
@@ -148,17 +187,22 @@
             pltpu.VMEM((16, 3, 64, LANES), jnp.float32),
             pltpu.VMEM((16, 2, 64, LANES), jnp.float32),
         ],
+        compiler_params=pltpu.CompilerParams(vmem_limit_bytes=VMEM_LARGE),
         name="mode_products",
-    )(core, spec, first)
+    )(core, spec, factors)
 
 
 def output_kernel(value_ref, factor_ref, out_ref):
-    factor = factor_ref[...].T
+    high, low = split(factor_ref[...].T)
+    factor = jnp.concatenate([high, high, low, low], axis=1)
     for k in range(8):
         rows = [value_ref[pl.ds(k * 4 + r, 32, stride=32), :] for r in range(4)]
         turned = jnp.concatenate(rows, axis=0).T
+        turned = jnp.concatenate([turned[:64], turned[64:]], axis=1)
+        high, low = split(turned)
+        out = dot(factor, jnp.concatenate([high, low, high, low], axis=0))
         for b in range(2):
-            out_ref[0, b, pl.ds(k, 128, stride=8), :] = dot(factor, turned[b * 64 : (b + 1) * 64])
+            out_ref[0, b, pl.ds(k, 128, stride=8), :] = out[:, b * LANES : (b + 1) * LANES]
 
 
 def output_modes(values, factor):
@@ -171,6 +215,7 @@
         ],
         out_specs=pl.BlockSpec((1, 2, 1024, LANES), lambda i: (i, 0, 0, 0)),
         out_shape=jax.ShapeDtypeStruct((2, 2, 1024, LANES), jnp.float32),
+        compiler_params=pltpu.CompilerParams(vmem_limit_bytes=VMEM_SMALL),
         name="output_modes",
     )(values, factor)
 
@@ -182,14 +227,16 @@
 def per_device(
     spectrum, core_tensor, input_factor, output_factor, first_factor, second_factor, third_factor
 ):
-    second = lax.all_gather(second_factor, "my", axis=0, tiled=True)
-    first = lax.all_gather(first_factor, "mx", axis=0, tiled=True)
+    mine = jnp.concatenate(
+        [first_factor, second_factor, jnp.zeros((8, LANES - 32), jnp.float32)], axis=1
+    )
+    factors = swap(jnp.broadcast_to(mine, (16, 8, LANES)), ("mx", "my")).reshape(128, LANES)
     core = jnp.transpose(core_tensor, (0, 1, 3, 4, 5, 2)).reshape(2, 8, 256, 64)
-    core = core_chunks(core, second, third_factor)
+    core = core_chunks(core, factors, third_factor)
     core = swap(core.reshape(128, 8, 512), ("mx", "my", "col"))
     spec = spectrum_chunks(spectrum.reshape(2, 2, 1024, LANES), input_factor.T)
     spec = swap(spec.reshape(32, 32, 256), ("mx", "col"))
-    values = mode_products(core.reshape(16, 8, 8, 512), spec.reshape(4, 8, 32, 256), first)
+    values = mode_products(core.reshape(16, 8, 8, 512), spec.reshape(4, 8, 32, 256), factors)
     values = swap(values.reshape(32, 32, 256), ("mx", "col"))
     out = output_modes(values.reshape(1024, 256), output_factor.T)
     return out.reshape(spectrum.shape)

time: 121 us -> 110 us (0.909)
  Pallas kernels: 33.7 us -> 18 us
  starting transfers between devices: 20.7 us -> 14.6 us
  blocking collectives: 50.2 us -> 56.3 us
  local copies, waits for them, and re-layouts: 2.35 us -> 4.66 us
    all_to_all x1 -> x2, blocking collectives: 19.8 us -> 56.3 us  [swap(): return lax.all_to_all(chunks, axes, split_axis=0, concat_axis=0, tiled=True)]
    all_gather x2 -> x0, blocking collectives: 30.4 us -> none  [the longest x1 17.7 us: per_device(): first = lax.all_gather(first_factor, 'mx', axis=0, tiled=True)]
    all_to_all x2, starting transfers between devices: 20.7 us -> 14.6 us  [swap(): return lax.all_to_all(chunks, axes, split_axis=0, concat_axis=0, tiled=True)]
    pallas_call x1, Pallas kernels: 15.4 us -> 10.3 us  [mode_products(): pl.pallas_call(mode_kernel, out_shape=jax.ShapeDtypeStruct((4, 8, 32, 256...]
    pallas_call x1, Pallas kernels: 6.99 us -> 2.37 us  [output_modes(): pl.pallas_call(output_kernel, grid=(2,), in_specs=[pl.BlockSpec((1024, LA...]
    pallas_call x1, Pallas kernels: 6.8 us -> 3.13 us  [core_chunks(): pl.pallas_call(core_kernel, grid=(4,), in_specs=[pl.BlockSpec((2, 2, 256,...]
    pallas_call x1, Pallas kernels: 4.53 us -> 2.18 us  [spectrum_chunks(): pl.pallas_call(spectrum_kernel, grid=(2,), in_specs=[pl.BlockSpec((1, 2,...]
    unnamed x8 -> x10, local copies, waits for them, and re-layouts: 2.35 us -> 3.94 us
  transfers between devices with their start and end apart: 2 -> 2, of which waited for: 1 -> 2; matrix products, arithmetic and copies ran while one was open for 0% -> 0% of each run, Pallas kernels for 6% -> 5%
where the time goes in v2:
time: 110 us; the launch traced here: 108 us
  blocking collectives  56.3 us (51%)
  Pallas kernels  18 us (16%)
  starting transfers between devices  14.6 us (13%)
  waiting for transfers between devices  13.8 us (13%)
  local copies, waits for them, and re-layouts  4.66 us (4%)
    all_to_all x2, blocking collectives, swap(): return lax.all_to_all(chunks, axes, split_axis=0, concat_axis=0, tiled=True)  56.3 us
    all_to_all x2, starting transfers between devices, swap(): return lax.all_to_all(chunks, axes, split_axis=0, concat_axis=0, tiled=True)  14.6 us
    all_to_all x2, waiting for transfers between devices, swap(): return lax.all_to_all(chunks, axes, split_axis=0, concat_axis=0, tiled=True)  13.8 us
    pallas_call x1, Pallas kernels, mode_products(): pl.pallas_call(mode_kernel, out_shape=jax.ShapeDtypeStruct((4, 8, 32, 256...  10.3 us
    unnamed x10, local copies, waits for them, and re-layouts  3.94 us
    pallas_call x1, Pallas kernels, core_chunks(): pl.pallas_call(core_kernel, grid=(4,), in_specs=[pl.BlockSpec((2, 2, 256,...  3.13 us
    pallas_call x1, Pallas kernels, output_modes(): pl.pallas_call(output_kernel, grid=(2,), in_specs=[pl.BlockSpec((1024, LA...  2.37 us
  transfers between devices with their start and end apart: 2, of which 2 were waited for; matrix products, arithmetic and copies ran while one was open for 0% of the time, Pallas kernels for 5%

profile of v2, /device:TPU:1, one launch (start us, length us, event | category | flops | bytes accessed | tf_op | source)
XLA Modules:
  0.0 108.2 jit_solution(8764974912259365665)
XLA Ops:
  0.0 0.1 pad.2.clone
  0.1 0.8 maximum_maximum_fusion
  0.9 0.6 broadcast_in_dim.7
  1.5 9.4 %all-to-all-start = ((f32[16,8,128]{2,1,0:T(8,128)}), f32[16,8,128]{2,1,0:T(8,128)S(1)}, u32[]{:S(2)}, u32[]{:S(2)}) async-start(f32[16,8,128]{2,1,0:T(8,128)} %broadcast_in_dim.7), calls=%async_computation | async-start | bytes 131072 | tf_op jit(solution)/shard_map/all_to_all | solution.py:224
  10.9 0.0 copy-start
  11.0 1.6 %copy-done = f32[2,2,128,8,128]{4,3,2,1,0:T(8,128)S(1)} copy-done((f32[2,2,128,8,128]{4,3,2,1,0:T(8,128)S(1)}, f32[2,2,128,8,128]{4,3,2,1,0:T(8,128)}, u32[]{:S(2)}) %copy-start) | copy-done | bytes 2097176
  12.5 0.0 copy-start.2
  12.5 0.8 copy-done.2
  13.3 0.0 copy-start.4
  13.3 2.2 %spectrum_chunks.1 = f32[1024,256]{1,0:T(8,128)} custom-call(f32[2,2,1024,128]{3,2,1,0:T(8,128)S(1)} %bitcast.19, f32[64,128]{1,0:T(8,128)S(1)} %bitcast.23), custom_call_target="tpu_custom_call" | custom-call | tf_op jit(solution)/shard_map/spectrum_chunks/pallas_call | solution.py:108
  15.5 2.8 %all-to-all-done = f32[16,8,128]{2,1,0:T(8,128)S(1)} async-done(((f32[16,8,128]{2,1,0:T(8,128)}), f32[16,8,128]{2,1,0:T(8,128)S(1)}, u32[]{:S(2)}, u32[]{:S(2)}) %all-to-all-start) | async-done | bytes 65568 | tf_op jit(solution)/shard_map/all_to_all | solution.py:224
  18.3 5.2 %all-to-all-start.2 = ((f32[32,32,256]{2,1,0:T(8,128)}), f32[32,32,256]{2,1,0:T(8,128)S(1)}, u32[]{:S(2)}, u32[]{:S(2)}) async-start(f32[32,32,256]{2,1,0:T(8,128)} %bitcast.7), calls=%async_computation.2 | async-start | bytes 2097152 | tf_op jit(solution)/shard_map/all_to_all | solution.py:224
  23.5 0.0 copy-done.4
  23.5 0.0 copy-start.1
  23.5 1.6 %copy-done.1 = f32[2,8,64,1,16,16]{2,5,4,3,1,0:T(8,128)S(1)} copy-done((f32[2,8,64,1,16,16]{2,5,4,3,1,0:T(8,128)S(1)}, f32[2,8,64,1,16,16]{2,5,4,3,1,0:T(8,128)}, u32[]{:S(2)}) %copy-start.1) | copy-done | bytes 1048600
  25.1 3.1 %core_chunks.1 = f32[1024,512]{1,0:T(8,128)S(1)} custom-call(f32[2,8,256,64]{3,2,1,0:T(8,128)S(1)} %bitcast.20, f32[128,128]{1,0:T(8,128)S(1)} %bitcast.21, f32[16,16]{1,0:T(8,128)S(1)} %copy-done.4), custom_call_target="tpu_custom_call" | custom-call | tf_op jit(solution)/shard_map/core_chunks/pallas_call | solution.py:75
  28.2 11.0 %all-to-all-done.2 = f32[32,32,256]{2,1,0:T(8,128)S(1)} async-done(((f32[32,32,256]{2,1,0:T(8,128)}), f32[32,32,256]{2,1,0:T(8,128)S(1)}, u32[]{:S(2)}, u32[]{:S(2)}) %all-to-all-start.2) | async-done | bytes 1048608 | tf_op jit(solution)/shard_map/all_to_all | solution.py:224
  39.2 38.1 %all_to_all.20 = f32[128,8,512]{2,1,0:T(8,128)S(1)} all-to-all(f32[128,8,512]{2,1,0:T(8,128)S(1)} %bitcast.14), channel_id=1, replica_groups=mesh['mx'=4,'my'=4,'col'=8] {'mx','my','col'}, dimensions={0} | all-to-all | bytes 4194304 | tf_op jit(solution)/shard_map/all_to_all | solution.py:224
  77.3 10.3 %mode_products.1 = f32[4,8,32,256]{3,2,1,0:T(8,128)S(1)} custom-call(f32[16,8,8,512]{3,2,1,0:T(8,128)S(1)} %bitcast.15, f32[4,8,32,256]{3,2,1,0:T(8,128)S(1)} %bitcast.17, f32[128,128]{1,0:T(8,128)S(1)} %bitcast.22), custom_call_target="tpu_custom_call" | custom-call | tf_op jit(solution)/shard_map/mode_products/pallas_call | solution.py:182
  87.7 0.0 copy-start.3
  87.7 18.2 %all_to_all.21 = f32[32,32,256]{2,1,0:T(8,128)S(1)} all-to-all(f32[32,32,256]{2,1,0:T(8,128)S(1)} %bitcast.18), channel_id=1, replica_groups=mesh['mx'=4,'my'=4,'col'=8] {'mx','col'}, dimensions={0} | all-to-all | bytes 2097152 | tf_op jit(solution)/shard_map/all_to_all | solution.py:224
  105.9 0.0 copy-done.3
  105.9 2.4 %output_modes.1 = f32[2,2,1024,128]{3,2,1,0:T(8,128)} custom-call(f32[1024,256]{1,0:T(8,128)S(1)} %bitcast.16, f32[64,128]{1,0:T(8,128)S(1)} %bitcast.24), custom_call_target="tpu_custom_call" | custom-call | tf_op jit(solution)/shard_map/output_modes/pallas_call | solution.py:209
  (1 shorter events, 0.0 us)
Async XLA Ops:
  1.5 16.8 %all-to-all-start = ((f32[16,8,128]{2,1,0:T(8,128)}), f32[16,8,128]{2,1,0:T(8,128)S(1)}, u32[]{:S(2)}, u32[]{:S(2)}) async-start(f32[16,8,128]{2,1,0:T(8,128)} %broadcast_in_dim.7), calls=%async_computation | async-start | bytes 131072 | tf_op jit(solution)/shard_map/all_to_all | solution.py:224
  10.9 1.6 %copy-start = (f32[2,2,128,8,128]{4,3,2,1,0:T(8,128)S(1)}, f32[2,2,128,8,128]{4,3,2,1,0:T(8,128)}, u32[]{:S(2)}) copy-start(f32[2,2,128,8,128]{4,3,2,1,0:T(8,128)} %param.7) | copy-start | bytes 6291460
  12.5 0.8 copy-start.2
  13.3 10.2 %copy-start.4 = (f32[16,16]{1,0:T(8,128)S(1)}, f32[16,16]{1,0:T(8,128)}, u32[]{:S(2)}) copy-start(f32[16,16]{1,0:T(8,128)} %third_ref.1) | copy-start | bytes 3076
  18.3 20.9 %all-to-all-start.2 = ((f32[32,32,256]{2,1,0:T(8,128)}), f32[32,32,256]{2,1,0:T(8,128)S(1)}, u32[]{:S(2)}, u32[]{:S(2)}) async-start(f32[32,32,256]{2,1,0:T(8,128)} %bitcast.7), calls=%async_computation.2 | async-start | bytes 2097152 | tf_op jit(solution)/shard_map/all_to_all | solution.py:224
  23.5 1.6 %copy-start.1 = (f32[2,8,64,1,16,16]{2,5,4,3,1,0:T(8,128)S(1)}, f32[2,8,64,1,16,16]{2,5,4,3,1,0:T(8,128)}, u32[]{:S(2)}) copy-start(f32[2,8,64,1,16,16]{2,5,4,3,1,0:T(8,128)} %param.8) | copy-start | bytes 3145732
  87.7 18.2 %copy-start.3 = (f32[128,64]{0,1:T(8,128)S(1)}, f32[128,64]{0,1:T(8,128)}, u32[]{:S(2)}) copy-start(f32[128,64]{0,1:T(8,128)} %param.10) | copy-start | bytes 98308

commit v3 on v2

--- a/solution.py
+++ b/solution.py
@@ -1,5 +1,3 @@
-import functools
-
 import jax
 import jax.numpy as jnp
 from jax import lax
@@ -7,9 +5,11 @@
 from jax.experimental.pallas import tpu as pltpu
 from jax.sharding import PartitionSpec as P
 
+
 LANES = 128
 VMEM_SMALL = 16 * 2**20
 VMEM_LARGE = 32 * 2**20
+VMEM_ALONE = 61 * 2**20
 
 
 def dot(a, b):
@@ -43,7 +43,7 @@
     return (dot(high, one) + dot(mid, one)) + dot(low, one)
 
 
-def core_kernel(core_ref, factors_ref, third_ref, out_ref, mat_ref):
+def core_kernel(core_ref, second_ref, third_ref, out_ref, mat_ref):
     @pl.when(pl.program_id(0) == 0)
     def _():
         def place(width):
@@ -53,7 +53,7 @@
 
         of_t = iota((16, 256), 1) >> 4 == iota((16, 256), 0)
         of_u = iota((16, 256), 1) & 15 == iota((16, 256), 0)
-        second = pick_lanes(factors_ref[:32, 16:32], of_t)
+        second = pick_lanes(second_ref[...], of_t)
         third = pick_lanes(third_ref[...], of_u)
         col, ky, _ = place(32)
         by_y = pick(col == ky, second)
@@ -71,61 +71,79 @@
             ]
 
 
-def core_chunks(core, factors, third):
+def core_chunks(core, second, third):
     return pl.pallas_call(
         core_kernel,
         grid=(4,),
         in_specs=[
             pl.BlockSpec((2, 2, 256, 64), lambda i: (0, i, 0, 0)),
-            pl.BlockSpec((128, LANES), lambda i: (0, 0)),
+            pl.BlockSpec(second.shape, lambda i: (0, 0)),
             pl.BlockSpec(third.shape, lambda i: (0, 0)),
         ],
         out_specs=pl.BlockSpec((1024, LANES), lambda i: (0, i)),
         out_shape=jax.ShapeDtypeStruct((1024, 512), jnp.float32),
         scratch_shapes=[pltpu.VMEM((2, 512, 256), jnp.bfloat16)],
-        compiler_params=pltpu.CompilerParams(vmem_limit_bytes=VMEM_SMALL),
+        compiler_params=pltpu.CompilerParams(vmem_limit_bytes=VMEM_ALONE),
         name="core_chunks",
-    )(core, factors, third)
-
-
-def spectrum_kernel(spec_ref, factor_ref, out_ref):
+    )(core, second, third)
+
+
+def spectrum_kernel(spec_hbm, factor_ref, first_ref, out_ref, spec_ref, sems):
+    copies = [
+        pltpu.make_async_copy(spec_hbm.at[part, b], spec_ref.at[part, b], sems.at[part, b])
+        for part in range(2)
+        for b in range(2)
+    ]
+    for copy in copies:
+        copy.start()
     high, low = split(factor_ref[...])
     rows = jnp.concatenate(
         [jnp.concatenate([high, high], axis=1), jnp.concatenate([low, low], axis=1)], axis=0
     )
+    for part in range(2):
+        copies[2 * part].wait()
+        copies[2 * part + 1].wait()
+        for k in range(8):
+            both = jnp.concatenate(
+                [spec_ref[part, b, pl.ds(k, 128, stride=8), :] for b in range(2)], axis=1
+            )
+            out = dot(rows, jnp.concatenate(split(both), axis=0))
+            out = out[:64] + out[64:]
+            turned = jnp.concatenate([out[:, :LANES], out[:, LANES:]], axis=0).T
+            for r in range(4):
+                row = part * 32 + k * 4 + r
+                out_ref[pl.ds(row, 32, stride=72), :] = turned[r * 32 : (r + 1) * 32]
+    first = jnp.concatenate([first_ref[...], jnp.zeros((8, LANES - 16), jnp.float32)], axis=1)
     for k in range(8):
-        both = jnp.concatenate(
-            [spec_ref[0, b, pl.ds(k, 128, stride=8), :] for b in range(2)], axis=1
-        )
-        out = dot(rows, jnp.concatenate(split(both), axis=0))
-        out = out[:64] + out[64:]
-        turned = jnp.concatenate([out[:, :LANES], out[:, LANES:]], axis=0).T
-        for r in range(4):
-            out_ref[pl.ds(k * 4 + r, 32, stride=32), :] = turned[r * 32 : (r + 1) * 32]
-
-
-def spectrum_chunks(spec, factor):
+        out_ref[pl.ds(64 + k, 32, stride=72), :] = jnp.broadcast_to(first[k : k + 1], (32, LANES))
+
+
+def spectrum_chunks(spec, factor, first):
     return pl.pallas_call(
         spectrum_kernel,
-        grid=(2,),
         in_specs=[
-            pl.BlockSpec((1, 2, 1024, LANES), lambda i: (i, 0, 0, 0)),
-            pl.BlockSpec((64, 128), lambda i: (0, 0)),
-        ],
-        out_specs=pl.BlockSpec((1024, LANES), lambda i: (0, i)),
-        out_shape=jax.ShapeDtypeStruct((1024, 256), jnp.float32),
-        compiler_params=pltpu.CompilerParams(vmem_limit_bytes=VMEM_SMALL),
+            pl.BlockSpec(memory_space=pltpu.MemorySpace.HBM),
+            pl.BlockSpec(memory_space=pltpu.VMEM),
+            pl.BlockSpec(memory_space=pltpu.VMEM),
+        ],
+        scratch_shapes=[
+            pltpu.VMEM((2, 2, 1024, LANES), jnp.float32),
+            pltpu.SemaphoreType.DMA((2, 2)),
+        ],
+        out_shape=jax.ShapeDtypeStruct((32 * 72, LANES), jnp.float32),
+        compiler_params=pltpu.CompilerParams(vmem_limit_bytes=VMEM_ALONE),
         name="spectrum_chunks",
-    )(spec, factor)
-
-
-def mode_kernel(core_ref, spec_ref, factors_ref, out_ref, w_ref, x_ref, v_ref):
+    )(spec, factor, first)
+
+
+def mode_kernel(core_ref, spec_ref, out_ref, w_ref, x_ref, v_ref):
     of_s = iota((128, 16), 0) >> 3 == iota((128, 16), 1)
-    kx = (iota((128, 256), 1) >> 2) & 31
-    of_k = (kx >> 3) * 32 + (kx & 7) == iota((128, 256), 0)
+    of_k = (iota((LANES, 256), 1) >> 2) & 31 == iota((LANES, 256), 0)
     row, col = iota((128, 256), 0), iota((128, 256), 1)
     same = (((row >> 2) & 1) == (col >> 7)) & ((row & 3) == (col & 3))
-    first = pick_lanes(factors_ref[...].T[:16], of_k)
+    first = [spec_ref[a, 0, 64:72, :] for a in range(4)]
+    first = jnp.concatenate(first + [jnp.zeros((96, LANES), jnp.float32)], axis=0)
+    first = pick_lanes(first.T[:16], of_k)
     expand = jnp.where(same, pick(of_s, first), 0.0)
     high, low = split(expand)
     expand_high = jnp.concatenate([high, high], axis=0)
@@ -145,7 +163,7 @@
 
     for src in range(8):
         parts = [
-            spec_ref[:, src, :, part * LANES : (part + 1) * LANES].reshape(128, LANES).T
+            spec_ref[:, src, part * 32 : (part + 1) * 32, :].reshape(128, LANES).T
             for part in range(2)
         ]
         parts.append(parts[0] + parts[1])
@@ -178,7 +196,7 @@
             out_ref[:, src, :, part * LANES : (part + 1) * LANES] = both.T.reshape(4, 32, LANES)
 
 
-def mode_products(core, spec, factors):
+def mode_products(core, spec):
     return pl.pallas_call(
         mode_kernel,
         out_shape=jax.ShapeDtypeStruct((4, 8, 32, 256), jnp.float32),
@@ -189,7 +207,7 @@
         ],
         compiler_params=pltpu.CompilerParams(vmem_limit_bytes=VMEM_LARGE),
         name="mode_products",
-    )(core, spec, factors)
+    )(core, spec)
 
 
 def output_kernel(value_ref, factor_ref, out_ref):
@@ -227,16 +245,13 @@
 def per_device(
     spectrum, core_tensor, input_factor, output_factor, first_factor, second_factor, third_factor
 ):
-    mine = jnp.concatenate(
-        [first_factor, second_factor, jnp.zeros((8, LANES - 32), jnp.float32)], axis=1
-    )
-    factors = swap(jnp.broadcast_to(mine, (16, 8, LANES)), ("mx", "my")).reshape(128, LANES)
+    spec = spectrum_chunks(spectrum.reshape(2, 2, 1024, LANES), input_factor.T, first_factor)
+    spec = swap(spec.reshape(32, 72, LANES), ("mx", "col"))
+    second = lax.all_gather(second_factor, "my", axis=0, tiled=True)
     core = jnp.transpose(core_tensor, (0, 1, 3, 4, 5, 2)).reshape(2, 8, 256, 64)
-    core = core_chunks(core, factors, third_factor)
+    core = core_chunks(core, second, third_factor)
     core = swap(core.reshape(128, 8, 512), ("mx", "my", "col"))
-    spec = spectrum_chunks(spectrum.reshape(2, 2, 1024, LANES), input_factor.T)
-    spec = swap(spec.reshape(32, 32, 256), ("mx", "col"))
-    values = mode_products(core.reshape(16, 8, 8, 512), spec.reshape(4, 8, 32, 256), factors)
+    values = mode_products(core.reshape(16, 8, 8, 512), spec.reshape(4, 8, 72, LANES))
     values = swap(values.reshape(32, 32, 256), ("mx", "col"))
     out = output_modes(values.reshape(1024, 256), output_factor.T)
     return out.reshape(spectrum.shape)

time: 110 us -> 108 us (0.982)
  blocking collectives: 56.3 us -> 74.4 us
  waiting for transfers between devices: 13.8 us -> 0.01 us
  starting transfers between devices: 14.6 us -> 9.72 us
  local copies, waits for them, and re-layouts: 4.66 us -> 0.01 us
  Pallas kernels: 18 us -> 22.1 us
    all_to_all x2 -> x1, waiting for transfers between devices: 13.8 us -> 0.01 us  [swap(): return lax.all_to_all(chunks, axes, split_axis=0, concat_axis=0, tiled=True)]
    all_gather x0 -> x1, blocking collectives: none -> 13.5 us  [per_device(): second = lax.all_gather(second_factor, 'my', axis=0, tiled=True)]
    all_to_all x2 -> x1, starting transfers between devices: 14.6 us -> 9.72 us  [swap(): return lax.all_to_all(chunks, axes, split_axis=0, concat_axis=0, tiled=True)]
    all_to_all x2, blocking collectives: 56.3 us -> 60.9 us  [swap(): return lax.all_to_all(chunks, axes, split_axis=0, concat_axis=0, tiled=True)]
    unnamed x10 -> x4, local copies, waits for them, and re-layouts: 3.94 us -> 0.01 us
    pallas_call x1, Pallas kernels: 3.13 us -> 5.4 us  [core_chunks(): pl.pallas_call(core_kernel, grid=(4,), in_specs=[pl.BlockSpec((2, 2, 256,...]
    pallas_call x1, Pallas kernels: 2.18 us -> 3.98 us  [spectrum_chunks(): pl.pallas_call(spectrum_kernel, in_specs=[pl.BlockSpec(memory_space=pltpu...]
  transfers between devices with their start and end apart: 2 -> 1, of which waited for: 2 -> 0; matrix products, arithmetic and copies ran while one was open for 0% -> 0% of each run, Pallas kernels for 5% -> 5%
where the time goes in v3:
time: 108 us; the launch traced here: 106 us
  blocking collectives  74.4 us (69%)
  Pallas kernels  22.1 us (20%)
  starting transfers between devices  9.72 us (9%)
    all_to_all x2, blocking collectives, swap(): return lax.all_to_all(chunks, axes, split_axis=0, concat_axis=0, tiled=True)  60.9 us
    all_gather x1, blocking collectives, per_device(): second = lax.all_gather(second_factor, 'my', axis=0, tiled=True)  13.5 us
    pallas_call x1, Pallas kernels, mode_products(): pl.pallas_call(mode_kernel, out_shape=jax.ShapeDtypeStruct((4, 8, 32, 256...  10.3 us
    all_to_all x1, starting transfers between devices, swap(): return lax.all_to_all(chunks, axes, split_axis=0, concat_axis=0, tiled=True)  9.72 us
    pallas_call x1, Pallas kernels, core_chunks(): pl.pallas_call(core_kernel, grid=(4,), in_specs=[pl.BlockSpec((2, 2, 256,...  5.4 us
    pallas_call x1, Pallas kernels, spectrum_chunks(): pl.pallas_call(spectrum_kernel, in_specs=[pl.BlockSpec(memory_space=pltpu...  3.98 us
    pallas_call x1, Pallas kernels, output_modes(): pl.pallas_call(output_kernel, grid=(2,), in_specs=[pl.BlockSpec((1024, LA...  2.37 us
  transfers between devices with their start and end apart: 1, of which 0 were waited for; matrix products, arithmetic and copies ran while one was open for 0% of the time, Pallas kernels for 5%

profile of v3, /device:TPU:1, one launch (start us, length us, event | category | flops | bytes accessed | tf_op | source)
XLA Modules:
  0.0 106.2 jit_solution(9952675450763318846)
XLA Ops:
  0.0 0.0 copy-start.1
  0.0 4.0 %spectrum_chunks.1 = f32[2304,128]{1,0:T(8,128)} custom-call(f32[2,2,1024,128]{3,2,1,0:T(8,128)} %bitcast.20, f32[64,128]{1,0:T(8,128)} %bitcast.22, f32[8,16]{1,0:T(8,128)} %first_ref.1), custom_call_target="tpu_custom_call" | custom-call | tf_op jit(solution)/shard_map/spectrum_chunks/pallas_call | solution.py:122
  4.0 9.7 %all-to-all-start.1 = ((f32[32,72,128]{2,1,0:T(8,128)}), f32[32,72,128]{2,1,0:T(8,128)S(1)}, u32[]{:S(2)}, u32[]{:S(2)}) async-start(f32[32,72,128]{2,1,0:T(8,128)} %bitcast.19), calls=%async_computation.1 | async-start | bytes 2359296 | tf_op jit(solution)/shard_map/all_to_all | solution.py:242
  13.7 0.0 copy-done.1
  13.7 13.5 %all_gather.3.second_ref = f32[32,16]{1,0:T(8,128)} all-gather(f32[8,16]{1,0:T(8,128)S(1)} %copy-done.1), channel_id=1, replica_groups=mesh['mx'=4,'my'=4,'col'=8] {'my'}, dimensions={0}, use_global_device_ids=true | all-gather | bytes 2560 | tf_op jit(solution)/shard_map/all_gather | solution.py:250
  27.2 5.4 %core_chunks.1 = f32[1024,512]{1,0:T(8,128)} custom-call(f32[2,8,256,64]{3,2,1,0:T(8,128)} %bitcast.21, f32[32,16]{1,0:T(8,128)} %all_gather.3.second_ref, f32[16,16]{1,0:T(8,128)} %third_ref.1), custom_call_target="tpu_custom_call" | custom-call | tf_op jit(solution)/shard_map/core_chunks/pallas_call | solution.py:75
  32.6 0.0 all-to-all-done.1
  32.6 42.7 %all_to_all.15 = f32[128,8,512]{2,1,0:T(8,128)S(1)} all-to-all(f32[128,8,512]{2,1,0:T(8,128)} %bitcast.18), channel_id=1, replica_groups=mesh['mx'=4,'my'=4,'col'=8] {'mx','my','col'}, dimensions={0} | all-to-all | bytes 4194304 | tf_op jit(solution)/shard_map/all_to_all | solution.py:242
  75.3 10.3 %mode_products.1 = f32[4,8,32,256]{3,2,1,0:T(8,128)S(1)} custom-call(f32[16,8,8,512]{3,2,1,0:T(8,128)S(1)} %bitcast.13, f32[4,8,72,128]{3,2,1,0:T(8,128)S(1)} %bitcast.14), custom_call_target="tpu_custom_call" | custom-call | tf_op jit(solution)/shard_map/mode_products/pallas_call | solution.py:200
  85.6 0.0 copy-start
  85.7 18.2 %all_to_all.16 = f32[32,32,256]{2,1,0:T(8,128)S(1)} all-to-all(f32[32,32,256]{2,1,0:T(8,128)S(1)} %bitcast.16), channel_id=1, replica_groups=mesh['mx'=4,'my'=4,'col'=8] {'mx','col'}, dimensions={0} | all-to-all | bytes 2097152 | tf_op jit(solution)/shard_map/all_to_all | solution.py:242
  103.8 0.0 copy-done
  103.8 2.4 %output_modes.1 = f32[2,2,1024,128]{3,2,1,0:T(8,128)} custom-call(f32[1024,256]{1,0:T(8,128)S(1)} %bitcast.15, f32[64,128]{1,0:T(8,128)S(1)} %bitcast.17), custom_call_target="tpu_custom_call" | custom-call | tf_op jit(solution)/shard_map/output_modes/pallas_call | solution.py:227
Async XLA Ops:
  0.0 13.7 %copy-start.1 = (f32[8,16]{1,0:T(8,128)S(1)}, f32[8,16]{1,0:T(8,128)}, u32[]{:S(2)}) copy-start(f32[8,16]{1,0:T(8,128)} %param.12) | copy-start | bytes 1540
  4.0 28.6 %all-to-all-start.1 = ((f32[32,72,128]{2,1,0:T(8,128)}), f32[32,72,128]{2,1,0:T(8,128)S(1)}, u32[]{:S(2)}, u32[]{:S(2)}) async-start(f32[32,72,128]{2,1,0:T(8,128)} %bitcast.19), calls=%async_computation.1 | async-start | bytes 2359296 | tf_op jit(solution)/shard_map/all_to_all | solution.py:242
  85.6 18.2 %copy-start = (f32[128,64]{0,1:T(8,128)S(1)}, f32[128,64]{0,1:T(8,128)}, u32[]{:S(2)}) copy-start(f32[128,64]{0,1:T(8,128)} %param.10) | copy-start | bytes 98308

commit v4 on v3

--- a/solution.py
+++ b/solution.py
@@ -88,21 +88,12 @@
     )(core, second, third)
 
 
-def spectrum_kernel(spec_hbm, factor_ref, first_ref, out_ref, spec_ref, sems):
-    copies = [
-        pltpu.make_async_copy(spec_hbm.at[part, b], spec_ref.at[part, b], sems.at[part, b])
-        for part in range(2)
-        for b in range(2)
-    ]
-    for copy in copies:
-        copy.start()
+def spectrum_kernel(spec_ref, factor_ref, first_ref, out_ref):
     high, low = split(factor_ref[...])
     rows = jnp.concatenate(
         [jnp.concatenate([high, high], axis=1), jnp.concatenate([low, low], axis=1)], axis=0
     )
     for part in range(2):
-        copies[2 * part].wait()
-        copies[2 * part + 1].wait()
         for k in range(8):
             both = jnp.concatenate(
                 [spec_ref[part, b, pl.ds(k, 128, stride=8), :] for b in range(2)], axis=1
@@ -121,17 +112,8 @@
 def spectrum_chunks(spec, factor, first):
     return pl.pallas_call(
         spectrum_kernel,
-        in_specs=[
-            pl.BlockSpec(memory_space=pltpu.MemorySpace.HBM),
-            pl.BlockSpec(memory_space=pltpu.VMEM),
-            pl.BlockSpec(memory_space=pltpu.VMEM),
-        ],
-        scratch_shapes=[
-            pltpu.VMEM((2, 2, 1024, LANES), jnp.float32),
-            pltpu.SemaphoreType.DMA((2, 2)),
-        ],
         out_shape=jax.ShapeDtypeStruct((32 * 72, LANES), jnp.float32),
-        compiler_params=pltpu.CompilerParams(vmem_limit_bytes=VMEM_ALONE),
+        compiler_params=pltpu.CompilerParams(vmem_limit_bytes=VMEM_SMALL),
         name="spectrum_chunks",
     )(spec, factor, first)
 
@@ -245,12 +227,12 @@
 def per_device(
     spectrum, core_tensor, input_factor, output_factor, first_factor, second_factor, third_factor
 ):
-    spec = spectrum_chunks(spectrum.reshape(2, 2, 1024, LANES), input_factor.T, first_factor)
-    spec = swap(spec.reshape(32, 72, LANES), ("mx", "col"))
     second = lax.all_gather(second_factor, "my", axis=0, tiled=True)
     core = jnp.transpose(core_tensor, (0, 1, 3, 4, 5, 2)).reshape(2, 8, 256, 64)
     core = core_chunks(core, second, third_factor)
     core = swap(core.reshape(128, 8, 512), ("mx", "my", "col"))
+    spec = spectrum_chunks(spectrum.reshape(2, 2, 1024, LANES), input_factor.T, first_factor)
+    spec = swap(spec.reshape(32, 72, LANES), ("mx", "col"))
     values = mode_products(core.reshape(16, 8, 8, 512), spec.reshape(4, 8, 72, LANES))
     values = swap(values.reshape(32, 32, 256), ("mx", "col"))
     out = output_modes(values.reshape(1024, 256), output_factor.T)

time: 108 us -> 108 us (level)
  local copies, waits for them, and re-layouts: 0.01 us -> 3.04 us
  Pallas kernels: 22.1 us -> 19.9 us
    unnamed x4 -> x10, local copies, waits for them, and re-layouts: 0.01 us -> 3.04 us
    pallas_call x1, Pallas kernels: 3.98 us -> 1.75 us  [spectrum_chunks(): pl.pallas_call(spectrum_kernel, out_shape=jax.ShapeDtypeStruct((32 * 72,...]
where the time goes in v4:
time: 108 us; the launch traced here: 107 us
  blocking collectives  74.2 us (69%)
  Pallas kernels  19.9 us (18%)
  starting transfers between devices  9.71 us (9%)
  local copies, waits for them, and re-layouts  3.04 us (3%)
    all_to_all x2, blocking collectives, swap(): return lax.all_to_all(chunks, axes, split_axis=0, concat_axis=0, tiled=True)  60.7 us
    all_gather x1, blocking collectives, per_device(): second = lax.all_gather(second_factor, 'my', axis=0, tiled=True)  13.5 us
    pallas_call x1, Pallas kernels, mode_products(): pl.pallas_call(mode_kernel, out_shape=jax.ShapeDtypeStruct((4, 8, 32, 256...  10.3 us
    all_to_all x1, starting transfers between devices, swap(): return lax.all_to_all(chunks, axes, split_axis=0, concat_axis=0, tiled=True)  9.71 us
    pallas_call x1, Pallas kernels, core_chunks(): pl.pallas_call(core_kernel, grid=(4,), in_specs=[pl.BlockSpec((2, 2, 256,...  5.4 us
    unnamed x10, local copies, waits for them, and re-layouts  3.04 us
    pallas_call x1, Pallas kernels, output_modes(): pl.pallas_call(output_kernel, grid=(2,), in_specs=[pl.BlockSpec((1024, LA...  2.38 us
  transfers between devices with their start and end apart: 1, of which 0 were waited for; matrix products, arithmetic and copies ran while one was open for 0% of the time, Pallas kernels for 5%

profile of v4, /device:TPU:1, one launch (start us, length us, event | category | flops | bytes accessed | tf_op | source)
XLA Modules:
  0.0 106.9 jit_solution(3184669979038815523)
XLA Ops:
  0.0 0.0 copy-start
  0.0 1.6 %copy-done = f32[2,2,128,8,128]{4,3,2,1,0:T(8,128)S(1)} copy-done((f32[2,2,128,8,128]{4,3,2,1,0:T(8,128)S(1)}, f32[2,2,128,8,128]{4,3,2,1,0:T(8,128)}, u32[]{:S(2)}) %copy-start) | copy-done | bytes 2097176
  1.6 0.0 copy-start.1
  1.6 0.8 copy-done.1
  2.4 0.0 copy-start.3
  2.4 0.7 copy-done.3
  3.0 0.0 copy-start.4
  3.0 1.7 %spectrum_chunks.1 = f32[2304,128]{1,0:T(8,128)} custom-call(f32[2,2,1024,128]{3,2,1,0:T(8,128)S(1)} %bitcast.17, f32[64,128]{1,0:T(8,128)S(1)} %bitcast.18, f32[8,16]{1,0:T(8,128)S(1)} %copy-done.3), custom_call_target="tpu_custom_call" | custom-call | tf_op jit(solution)/shard_map/spectrum_chunks/pallas_call | solution.py:113
  4.8 9.7 %all-to-all-start.1 = ((f32[32,72,128]{2,1,0:T(8,128)}), f32[32,72,128]{2,1,0:T(8,128)S(1)}, u32[]{:S(2)}, u32[]{:S(2)}) async-start(f32[32,72,128]{2,1,0:T(8,128)} %bitcast.6), calls=%async_computation.1 | async-start | bytes 2359296 | tf_op jit(solution)/shard_map/all_to_all | solution.py:224
  14.5 0.0 copy-done.4
  14.5 13.5 %all_gather.3.second_ref = f32[32,16]{1,0:T(8,128)} all-gather(f32[8,16]{1,0:T(8,128)S(1)} %copy-done.4), channel_id=1, replica_groups=mesh['mx'=4,'my'=4,'col'=8] {'my'}, dimensions={0}, use_global_device_ids=true | all-gather | bytes 2560 | tf_op jit(solution)/shard_map/all_gather | solution.py:230
  28.0 5.4 %core_chunks.1 = f32[1024,512]{1,0:T(8,128)} custom-call(f32[2,8,256,64]{3,2,1,0:T(8,128)} %bitcast.21, f32[32,16]{1,0:T(8,128)} %all_gather.3.second_ref, f32[16,16]{1,0:T(8,128)} %third_ref.1), custom_call_target="tpu_custom_call" | custom-call | tf_op jit(solution)/shard_map/core_chunks/pallas_call | solution.py:75
  33.4 0.0 all-to-all-done.1
  33.4 42.5 %all_to_all.15 = f32[128,8,512]{2,1,0:T(8,128)S(1)} all-to-all(f32[128,8,512]{2,1,0:T(8,128)} %bitcast.20), channel_id=1, replica_groups=mesh['mx'=4,'my'=4,'col'=8] {'mx','my','col'}, dimensions={0} | all-to-all | bytes 4194304 | tf_op jit(solution)/shard_map/all_to_all | solution.py:224
  75.9 10.3 %mode_products.1 = f32[4,8,32,256]{3,2,1,0:T(8,128)S(1)} custom-call(f32[16,8,8,512]{3,2,1,0:T(8,128)S(1)} %bitcast.13, f32[4,8,72,128]{3,2,1,0:T(8,128)S(1)} %bitcast.14), custom_call_target="tpu_custom_call" | custom-call | tf_op jit(solution)/shard_map/mode_products/pallas_call | solution.py:182
  86.3 0.0 copy-start.2
  86.3 18.2 %all_to_all.16 = f32[32,32,256]{2,1,0:T(8,128)S(1)} all-to-all(f32[32,32,256]{2,1,0:T(8,128)S(1)} %bitcast.16), channel_id=1, replica_groups=mesh['mx'=4,'my'=4,'col'=8] {'mx','col'}, dimensions={0} | all-to-all | bytes 2097152 | tf_op jit(solution)/shard_map/all_to_all | solution.py:224
  104.5 0.0 copy-done.2
  104.5 2.4 %output_modes.1 = f32[2,2,1024,128]{3,2,1,0:T(8,128)} custom-call(f32[1024,256]{1,0:T(8,128)S(1)} %bitcast.15, f32[64,128]{1,0:T(8,128)S(1)} %bitcast.19), custom_call_target="tpu_custom_call" | custom-call | tf_op jit(solution)/shard_map/output_modes/pallas_call | solution.py:209
Async XLA Ops:
  0.0 1.6 %copy-start = (f32[2,2,128,8,128]{4,3,2,1,0:T(8,128)S(1)}, f32[2,2,128,8,128]{4,3,2,1,0:T(8,128)}, u32[]{:S(2)}) copy-start(f32[2,2,128,8,128]{4,3,2,1,0:T(8,128)} %param.7) | copy-start | bytes 6291460
  1.6 0.8 copy-start.1
  2.4 0.7 copy-start.3
  3.0 11.5 %copy-start.4 = (f32[8,16]{1,0:T(8,128)S(1)}, f32[8,16]{1,0:T(8,128)}, u32[]{:S(2)}) copy-start(f32[8,16]{1,0:T(8,128)} %param.12) | copy-start | bytes 1540
  4.8 28.6 %all-to-all-start.1 = ((f32[32,72,128]{2,1,0:T(8,128)}), f32[32,72,128]{2,1,0:T(8,128)S(1)}, u32[]{:S(2)}, u32[]{:S(2)}) async-start(f32[32,72,128]{2,1,0:T(8,128)} %bitcast.6), calls=%async_computation.1 | async-start | bytes 2359296 | tf_op jit(solution)/shard_map/all_to_all | solution.py:224
  86.3 18.2 %copy-start.2 = (f32[128,64]{0,1:T(8,128)S(1)}, f32[128,64]{0,1:T(8,128)}, u32[]{:S(2)}) copy-start(f32[128,64]{0,1:T(8,128)} %param.10) | copy-start | bytes 98308

commit v5 on v0

v5 whole, which is shorter than its diff:
```python
import jax
import jax.numpy as jnp
from jax import lax
from jax.experimental import pallas as pl
from jax.experimental.pallas import tpu as pltpu
from jax.sharding import PartitionSpec as P

LANES = 128
CHUNK = 48
VMEM_SMALL = 16 * 2**20
VMEM_LARGE = 32 * 2**20


def dot(a, b):
    return jnp.dot(a, b, preferred_element_type=jnp.float32)


def split(x):
    high = x.astype(jnp.bfloat16)
    return high, (x - high.astype(jnp.float32)).astype(jnp.bfloat16)


def split3(x):
    high = x.astype(jnp.bfloat16)
    return (high, *split(x - high.astype(jnp.float32)))


def iota(shape, dim):
    return lax.broadcasted_iota(jnp.int32, shape, dim)


def pick(chosen, table):
    one = chosen.astype(jnp.bfloat16)
    high, mid, low = split3(table)
    return (dot(one, high) + dot(one, mid)) + dot(one, low)


def pick_lanes(table, chosen):
    one = chosen.astype(jnp.bfloat16)
    high, mid, low = split3(table)
    return (dot(high, one) + dot(mid, one)) + dot(low, one)


def send_kernel(spec_ref, core_ref, in_ref, factors_ref, third_ref, out_ref):
    high, low = split(in_ref[...])
    rows = jnp.concatenate(
        [jnp.concatenate([high, high], axis=1), jnp.concatenate([low, low], axis=1)], axis=0
    )
    for b in range(2):
        for k in range(8):
            both = jnp.concatenate(
                [spec_ref[part, b, pl.ds(k, 128, stride=8), :] for part in range(2)], axis=1
            )
            out = dot(rows, jnp.concatenate(split(both), axis=0))
            out = out[:64] + out[64:]
            turned = jnp.concatenate([out[:, :LANES], out[:, LANES:]], axis=0).T
            out_ref[pl.ds(2 * k + b, 128, stride=CHUNK), :] = turned

    of_t = iota((16, 256), 1) >> 4 == iota((16, 256), 0)
    of_u = iota((16, 256), 1) & 15 == iota((16, 256), 0)
    second = pick_lanes(factors_ref[:32, 16:32], of_t)
    third = pick_lanes(third_ref[...], of_u)
    by_y = pick(iota((512, 32), 0) >> 4 == iota((512, 32), 1), second)
    by_z = pick(iota((512, 16), 0) & 15 == iota((512, 16), 1), third)
    mat_high, mat_low = split(by_y * by_z)
    for pair in range(4):
        both = jnp.concatenate(
            [core_ref[part, 2 * pair + half] for half in range(2) for part in range(2)], axis=1
        )
        high, low = split(both)
        out = dot(mat_high, high) + dot(mat_high, low) + dot(mat_low, high)
        for half in range(2):
            for r in range(4):
                row = 16 + (2 * pair + half) * 4 + r
                out_ref[pl.ds(row, 128, stride=CHUNK), :] = out[
                    r * 128 : (r + 1) * 128, half * LANES : (half + 1) * LANES
                ]


def send_chunks(spec, core, factor, factors, third):
    return pl.pallas_call(
        send_kernel,
        out_shape=jax.ShapeDtypeStruct((128 * CHUNK, LANES), jnp.float32),
        compiler_params=pltpu.CompilerParams(vmem_limit_bytes=VMEM_SMALL),
        name="send_chunks",
    )(spec, core, factor, factors, third)


def mode_kernel(got_ref, factors_ref, out_ref, w_ref):
    of_s = iota((16, 128), 1) >> 3 == iota((16, 128), 0)
    row, col = iota((256, 128), 0), iota((256, 128), 1)
    of_k = ((row >> 5) & 3) * 32 + (row & 7) == col
    same = ((row >> 7) == ((col >> 2) & 1)) & (((row >> 3) & 3) == (col & 3))
    first = pick_lanes(factors_ref[:, :16], of_s)
    high, low = split(jnp.where(same, pick(of_k, first), 0.0))
    expand = jnp.concatenate(
        [jnp.concatenate([high, high], axis=1), jnp.concatenate([low, low], axis=1)], axis=0
    )
    for src in range(8):
        for two in range(2):
            blocks = [
                got_ref[:, src, 16 + 8 * pair : 24 + 8 * pair, :].reshape(128, LANES)
                for pair in (2 * two, 2 * two + 1)
            ]
            out = dot(expand, jnp.concatenate(split(jnp.concatenate(blocks, axis=1)), axis=0))
            out = out[:256] + out[256:]
            for pair in range(2):
                for half in range(2):
                    p = src * 8 + (2 * two + pair) * 2 + half
                    w_ref[pl.ds(p, 128, stride=64), :] = out[
                        half * 128 : (half + 1) * 128, pair * LANES : (pair + 1) * LANES
                    ]

    got = got_ref.reshape(128 * CHUNK, LANES)
    left = iota((16, LANES), 1) < 64

    @pl.loop(0, 16)
    def _(g):
        for k in range(8):
            x = jnp.concatenate(
                [got[pl.ds(g * 8 * CHUNK + 2 * k + b, 8, stride=CHUNK), :] for b in range(2)],
                axis=0,
            )
            swapped = pltpu.roll(x, 64, 1)
            real, imag = jnp.where(left, x, swapped), jnp.where(left, swapped, x)
            rows = jnp.concatenate([*split(real), *split(imag)], axis=0)
            w = w_ref[pl.ds(pl.multiple_of((g * 8 + k) * 64, 64), 64), :]
            out = dot(rows, jnp.concatenate(split(w), axis=0))
            by_real, by_imag = out[:16] + out[16:32], out[32:48] + out[48:]
            swapped = pltpu.roll(by_imag, 64, 1)
            value = by_real + jnp.where(left, -swapped, swapped)
            for b in range(2):
                out_ref[pl.ds(g * 128 + 2 * k + b, 8, stride=16), :] = value[b * 8 : (b + 1) * 8]


def mode_products(got, factors):
    return pl.pallas_call(
        mode_kernel,
        out_shape=jax.ShapeDtypeStruct((128 * 16, LANES), jnp.float32),
        scratch_shapes=[pltpu.VMEM((128 * 64, LANES), jnp.float32)],
        compiler_params=pltpu.CompilerParams(vmem_limit_bytes=VMEM_LARGE),
        name="mode_products",
    )(got, factors)


def output_kernel(value_ref, factor_ref, out_ref):
    high, low = split(factor_ref[...].T)
    factor = jnp.concatenate([high, high, low, low], axis=1)
    step = pl.program_id(0)
    for k in range(8):
        turned = value_ref[pl.ds(2 * k + step, 128, stride=16), :].T
        high, low = split(jnp.concatenate([turned[:64], turned[64:]], axis=1))
        out = dot(factor, jnp.concatenate([high, low, high, low], axis=0))
        for part in range(2):
            out_ref[part, 0, pl.ds(k, 128, stride=8), :] = out[:, part * LANES : (part + 1) * LANES]


def output_modes(values, factor):
    return pl.pallas_call(
        output_kernel,
        grid=(2,),
        in_specs=[
            pl.BlockSpec((2048, LANES), lambda i: (0, 0)),
            pl.BlockSpec((64, 128), lambda i: (0, 0)),
        ],
        out_specs=pl.BlockSpec((2, 1, 1024, LANES), lambda i: (0, i, 0, 0)),
        out_shape=jax.ShapeDtypeStruct((2, 2, 1024, LANES), jnp.float32),
        compiler_params=pltpu.CompilerParams(vmem_limit_bytes=VMEM_SMALL),
        name="output_modes",
    )(values, factor)


def swap(chunks, axes):
    return lax.all_to_all(chunks, axes, split_axis=0, concat_axis=0, tiled=True)


def per_device(
    spectrum, core_tensor, input_factor, output_factor, first_factor, second_factor, third_factor
):
    mine = jnp.concatenate(
        [first_factor, second_factor, jnp.zeros((8, LANES - 32), jnp.float32)], axis=1
    )
    factors = swap(jnp.broadcast_to(mine, (16, 8, LANES)), ("mx", "my")).reshape(128, LANES)
    everyone = ("mx", "my", "col")
    core = jnp.transpose(core_tensor, (0, 1, 3, 4, 5, 2)).reshape(2, 8, 256, 64)
    chunks = send_chunks(
        spectrum.reshape(2, 2, 1024, LANES), core, input_factor.T, factors, third_factor
    )
    got = swap(chunks.reshape(128, CHUNK, LANES), everyone)
    values = mode_products(got.reshape(16, 8, CHUNK, LANES), factors)
    values = swap(values.reshape(128, 16, LANES), everyone)
    out = output_modes(values.reshape(2048, LANES), output_factor.T)
    return out.reshape(spectrum.shape)


def solution(mesh):
    placed = (
        P(None, "col", None, "mx", "my"),
        P(None, "col", None, ("mx", "my"), None, None),
        P(),
        P(),
        P("mx", None),
        P("my", None),
        P(),
    )
    return jax.shard_map(
        per_device,
        mesh=mesh,
        in_specs=placed,
        out_specs=P(None, "col", None, "mx", "my"),
        check_vma=False,
    )
```

time: 383 us -> 106 us (0.28); the launches traced: 377 us -> 106 us
  waiting for transfers between devices: 180 us -> 0 us
  matrix products: 114 us -> 0 us
  blocking collectives: 20.6 us -> 86.6 us
  local copies, waits for them, and re-layouts: 42.2 us -> 4.73 us
  Pallas kernels: 0 us -> 13.8 us
  between operations: 13.8 us -> 0.03 us
  other arithmetic: 6.1 us -> 0.78 us
    dot_general x9 -> x0, matrix products: 114 us -> none  [the longest x1 25.8 us: per_device(): jnp.einsum('cpqsm,ks->cpqkm', core_gathered, first_factor, precision=prec...]
    all_gather x1 -> x0, waiting for transfers between devices: 90.1 us -> none  [per_device(): core_gathered = lax.all_gather(core_third, ('mx', 'my'), axis=3, tiled=True)]
    reduce_scatter x1 -> x0, waiting for transfers between devices: 89.9 us -> none  [per_device(): lax.psum_scatter(mode_values, 'col', scatter_dimension=1, tiled=True)]
    all_to_all x1 -> x3, blocking collectives: 20.6 us -> 86.6 us  [swap(): return lax.all_to_all(chunks, axes, split_axis=0, concat_axis=0, tiled=True)]
    transpose x3 -> x0, local copies, waits for them, and re-layouts: 15.7 us -> none  [the longest x1 12.2 us: per_device(): jnp.einsum('cpqsm,ks->cpqkm', core_gathered, first_factor, precision=prec...]
    pallas_call x0 -> x3, Pallas kernels: none -> 13.8 us  [the longest x1 9.04 us: mode_products(): pl.pallas_call(mode_kernel, out_shape=jax.ShapeDtypeStruct((128 * 16, LAN...]
    another operation x1 -> x0, local copies, waits for them, and re-layouts: 11 us -> none  [per_device(): mode_values = jnp.stack([real_part, imag_part])]
    squeeze x2 -> x0, local copies, waits for them, and re-layouts: 6.25 us -> none  [the longest x1 3.15 us: per_device(): rank_spectrum[0]]
  transfers between devices with their start and end apart: 2 -> 0, of which waited for: 2 -> 0; matrix products, arithmetic and copies ran while one was open for 3% -> 0% of each run, Pallas kernels for 0% -> 0%
where the time goes in v5:
time: 106 us
  blocking collectives  86.6 us (82%)
  Pallas kernels  13.8 us (13%)
  local copies, waits for them, and re-layouts  4.73 us (4%)
    all_to_all x3, blocking collectives, swap(): return lax.all_to_all(chunks, axes, split_axis=0, concat_axis=0, tiled=True)  86.6 us
    pallas_call x1, Pallas kernels, mode_products(): pl.pallas_call(mode_kernel, out_shape=jax.ShapeDtypeStruct((128 * 16, LAN...  9.04 us
    unnamed x10, local copies, waits for them, and re-layouts  4.64 us
    pallas_call x1, Pallas kernels, send_chunks(): pl.pallas_call(send_kernel, out_shape=jax.ShapeDtypeStruct((128 * CHUNK,...  2.57 us
    pallas_call x1, Pallas kernels, output_modes(): pl.pallas_call(output_kernel, grid=(2,), in_specs=[pl.BlockSpec((2048, LA...  2.2 us

profile of v5, /device:TPU:1, one launch (start us, length us, event | category | flops | bytes accessed | tf_op | source)
XLA Modules:
  0.0 106.0 jit_solution(7157861488086063351)
XLA Ops:
  0.0 0.1 pad.2.clone
  0.1 0.8 maximum_maximum_fusion
  0.9 16.6 %all_to_all.15 = f32[16,8,128]{2,1,0:T(8,128)S(1)} all-to-all(f32[16,8,128]{2,1,0:T(8,128)S(1)} %broadcast_in_dim.7), channel_id=1, replica_groups=mesh['mx'=4,'my'=4,'col'=8] {'mx','my'}, dimensions={0} | all-to-all | bytes 131072 | tf_op jit(solution)/shard_map/all_to_all | solution.py:174
  17.4 0.0 copy-start
  17.4 1.6 %copy-done = f32[2,2,128,8,128]{4,3,2,1,0:T(8,128)S(1)} copy-done((f32[2,2,128,8,128]{4,3,2,1,0:T(8,128)S(1)}, f32[2,2,128,8,128]{4,3,2,1,0:T(8,128)}, u32[]{:S(2)}) %copy-start) | copy-done | bytes 2097176
  19.0 0.0 copy-start.1
  19.0 1.6 %copy-done.1 = f32[2,8,64,1,16,16]{2,5,4,3,1,0:T(8,128)S(1)} copy-done((f32[2,8,64,1,16,16]{2,5,4,3,1,0:T(8,128)S(1)}, f32[2,8,64,1,16,16]{2,5,4,3,1,0:T(8,128)}, u32[]{:S(2)}) %copy-start.1) | copy-done | bytes 1048600
  20.6 0.0 copy-start.2
  20.6 0.8 copy-done.2
  21.4 0.0 copy-start.4
  21.4 0.7 copy-done.4
  22.1 2.6 %send_chunks.1 = f32[6144,128]{1,0:T(8,128)S(1)} custom-call(f32[2,2,1024,128]{3,2,1,0:T(8,128)S(1)} %bitcast.16, f32[2,8,256,64]{3,2,1,0:T(8,128)S(1)} %bitcast.17, f32[64,128]{1,0:T(8,128)S(1)} %bitcast.20, f32[128,128]{1,0:T(8,128)S(1)} %bitcast.18, f32[16,16]{1,0:T(8,128)S(1)} %copy-done.4), custom_call_target="tpu_custom_call" | custom-call | tf_op jit(solution)/shard_map/send_chunks/pallas_call | solution.py:81
  24.6 46.3 %all_to_all.16 = f32[128,48,128]{2,1,0:T(8,128)S(1)} all-to-all(f32[128,48,128]{2,1,0:T(8,128)S(1)} %bitcast.13), channel_id=1, replica_groups=mesh['mx'=4,'my'=4,'col'=8] {'mx','my','col'}, dimensions={0} | all-to-all | bytes 6291456 | tf_op jit(solution)/shard_map/all_to_all | solution.py:174
  71.0 9.0 %mode_products.1 = f32[2048,128]{1,0:T(8,128)S(1)} custom-call(f32[16,8,48,128]{3,2,1,0:T(8,128)S(1)} %bitcast.12, f32[128,128]{1,0:T(8,128)S(1)} %bitcast.19), custom_call_target="tpu_custom_call" | custom-call | tf_op jit(solution)/shard_map/mode_products/pallas_call | solution.py:137
  80.0 0.0 copy-start.3
  80.0 23.8 %all_to_all.17 = f32[128,16,128]{2,1,0:T(8,128)S(1)} all-to-all(f32[128,16,128]{2,1,0:T(8,128)S(1)} %bitcast.15), channel_id=1, replica_groups=mesh['mx'=4,'my'=4,'col'=8] {'mx','my','col'}, dimensions={0} | all-to-all | bytes 2097152 | tf_op jit(solution)/shard_map/all_to_all | solution.py:174
  103.8 0.0 copy-done.3
  103.8 2.2 %output_modes.1 = f32[2,2,1024,128]{3,2,1,0:T(8,128)} custom-call(f32[2048,128]{1,0:T(8,128)S(1)} %bitcast.14, f32[64,128]{1,0:T(8,128)S(1)} %bitcast.21), custom_call_target="tpu_custom_call" | custom-call | tf_op jit(solution)/shard_map/output_modes/pallas_call | solution.py:159
  (2 shorter events, 0.0 us)
Async XLA Ops:
  17.4 1.6 %copy-start = (f32[2,2,128,8,128]{4,3,2,1,0:T(8,128)S(1)}, f32[2,2,128,8,128]{4,3,2,1,0:T(8,128)}, u32[]{:S(2)}) copy-start(f32[2,2,128,8,128]{4,3,2,1,0:T(8,128)} %param.7) | copy-start | bytes 6291460
  19.0 1.6 %copy-start.1 = (f32[2,8,64,1,16,16]{2,5,4,3,1,0:T(8,128)S(1)}, f32[2,8,64,1,16,16]{2,5,4,3,1,0:T(8,128)}, u32[]{:S(2)}) copy-start(f32[2,8,64,1,16,16]{2,5,4,3,1,0:T(8,128)} %param.8) | copy-start | bytes 3145732
  20.6 0.8 copy-start.2
  21.4 0.7 copy-start.4
  80.0 23.8 %copy-start.3 = (f32[128,64]{0,1:T(8,128)S(1)}, f32[128,64]{0,1:T(8,128)}, u32[]{:S(2)}) copy-start(f32[128,64]{0,1:T(8,128)} %param.10) | copy-start | bytes 98308

commit v6 on v5

--- a/solution.py
+++ b/solution.py
@@ -6,8 +6,10 @@
 from jax.sharding import PartitionSpec as P
 
 LANES = 128
-CHUNK = 48
+CHUNK = 49
+WIDE = 72
 VMEM_SMALL = 16 * 2**20
+VMEM_ALONE = 56 * 2**20
 VMEM_LARGE = 32 * 2**20
 
 
@@ -41,12 +43,33 @@
     return (dot(high, one) + dot(mid, one)) + dot(low, one)
 
 
-def send_kernel(spec_ref, core_ref, in_ref, factors_ref, third_ref, out_ref):
+def send_kernel(
+    spec_hbm, core_hbm, in_ref, first_ref, second_ref, third_ref, out_ref, spec_ref, core_ref, sems
+):
+    def spec_copy(b):
+        return pltpu.make_async_copy(spec_hbm.at[:, b], spec_ref.at[:, b], sems.at[b])
+
+    def core_copy(pair):
+        some = pl.ds(2 * pair, 2)
+        return pltpu.make_async_copy(core_hbm.at[:, some], core_ref.at[:, some], sems.at[2 + pair])
+
+    for b in range(2):
+        spec_copy(b).start()
+    for pair in range(4):
+        core_copy(pair).start()
+
+    of_s = iota((16, 128), 1) & 15 == iota((16, 128), 0)
+    mine = pick_lanes(first_ref[...], of_s)
+    mine = jnp.where(iota((8, 128), 1) >> 4 == iota((8, 128), 0), mine, 0.0)
+    mine = jnp.sum(mine, axis=0, keepdims=True)
+    out_ref[pl.ds(48, 128, stride=CHUNK), :] = jnp.broadcast_to(mine, (128, LANES))
+
     high, low = split(in_ref[...])
     rows = jnp.concatenate(
         [jnp.concatenate([high, high], axis=1), jnp.concatenate([low, low], axis=1)], axis=0
     )
     for b in range(2):
+        spec_copy(b).wait()
         for k in range(8):
             both = jnp.concatenate(
                 [spec_ref[part, b, pl.ds(k, 128, stride=8), :] for part in range(2)], axis=1
@@ -58,12 +81,15 @@
 
     of_t = iota((16, 256), 1) >> 4 == iota((16, 256), 0)
     of_u = iota((16, 256), 1) & 15 == iota((16, 256), 0)
-    second = pick_lanes(factors_ref[:32, 16:32], of_t)
+    second = pick_lanes(second_ref[...], of_t)
     third = pick_lanes(third_ref[...], of_u)
     by_y = pick(iota((512, 32), 0) >> 4 == iota((512, 32), 1), second)
     by_z = pick(iota((512, 16), 0) & 15 == iota((512, 16), 1), third)
     mat_high, mat_low = split(by_y * by_z)
     for pair in range(4):
+        if pair % 2 == 0:
+            core_copy(pair).wait()
+            core_copy(pair + 1).wait()
         both = jnp.concatenate(
             [core_ref[part, 2 * pair + half] for half in range(2) for part in range(2)], axis=1
         )
@@ -77,29 +103,45 @@
                 ]
 
 
-def send_chunks(spec, core, factor, factors, third):
+def send_chunks(spec, core, *factors):
+    whole = pl.BlockSpec(memory_space=pltpu.VMEM)
     return pl.pallas_call(
         send_kernel,
+        in_specs=[pl.BlockSpec(memory_space=pl.ANY)] * 2 + [whole] * 4,
         out_shape=jax.ShapeDtypeStruct((128 * CHUNK, LANES), jnp.float32),
-        compiler_params=pltpu.CompilerParams(vmem_limit_bytes=VMEM_SMALL),
+        scratch_shapes=[
+            pltpu.VMEM(spec.shape, jnp.float32),
+            pltpu.VMEM(core.shape, jnp.float32),
+            pltpu.SemaphoreType.DMA((6,)),
+        ],
+        compiler_params=pltpu.CompilerParams(vmem_limit_bytes=VMEM_ALONE),
         name="send_chunks",
-    )(spec, core, factor, factors, third)
-
-
-def mode_kernel(got_ref, factors_ref, out_ref, w_ref):
-    of_s = iota((16, 128), 1) >> 3 == iota((16, 128), 0)
+    )(spec, core, *factors)
+
+
+def mode_kernel(got, out_ref, w_ref):
     row, col = iota((256, 128), 0), iota((256, 128), 1)
-    of_k = ((row >> 5) & 3) * 32 + (row & 7) == col
+    first = jnp.concatenate([got[pl.ds(a * 32 * CHUNK + 48, 1), :] for a in range(4)] * 2, axis=0)
+    first = pick((iota((256, 8), 0) >> 5) & 3 == iota((256, 8), 1), first)
+    first = jnp.where(col >> 4 == row & 7, first, 0.0)
+    first = pick_lanes(first, iota((128, 128), 0) & 15 == iota((128, 128), 1) >> 3)
     same = ((row >> 7) == ((col >> 2) & 1)) & (((row >> 3) & 3) == (col & 3))
-    first = pick_lanes(factors_ref[:, :16], of_s)
-    high, low = split(jnp.where(same, pick(of_k, first), 0.0))
+    high, low = split(jnp.where(same, first, 0.0))
     expand = jnp.concatenate(
         [jnp.concatenate([high, high], axis=1), jnp.concatenate([low, low], axis=1)], axis=0
     )
-    for src in range(8):
+
+    @pl.loop(0, 8)
+    def _(src):
         for two in range(2):
             blocks = [
-                got_ref[:, src, 16 + 8 * pair : 24 + 8 * pair, :].reshape(128, LANES)
+                jnp.concatenate(
+                    [
+                        got[pl.ds((s * 8 + src) * CHUNK + 16 + 8 * pair, 8), :]
+                        for s in range(16)
+                    ],
+                    axis=0,
+                )
                 for pair in (2 * two, 2 * two + 1)
             ]
             out = dot(expand, jnp.concatenate(split(jnp.concatenate(blocks, axis=1)), axis=0))
@@ -107,11 +149,10 @@
             for pair in range(2):
                 for half in range(2):
                     p = src * 8 + (2 * two + pair) * 2 + half
-                    w_ref[pl.ds(p, 128, stride=64), :] = out[
+                    w_ref[pl.ds(p, 128, stride=WIDE), :] = out[
                         half * 128 : (half + 1) * 128, pair * LANES : (pair + 1) * LANES
                     ]
 
-    got = got_ref.reshape(128 * CHUNK, LANES)
     left = iota((16, LANES), 1) < 64
 
     @pl.loop(0, 16)
@@ -124,7 +165,7 @@
             swapped = pltpu.roll(x, 64, 1)
             real, imag = jnp.where(left, x, swapped), jnp.where(left, swapped, x)
             rows = jnp.concatenate([*split(real), *split(imag)], axis=0)
-            w = w_ref[pl.ds(pl.multiple_of((g * 8 + k) * 64, 64), 64), :]
+            w = w_ref[pl.ds(pl.multiple_of((g * 8 + k) * WIDE, 8), 64), :]
             out = dot(rows, jnp.concatenate(split(w), axis=0))
             by_real, by_imag = out[:16] + out[16:32], out[32:48] + out[48:]
             swapped = pltpu.roll(by_imag, 64, 1)
@@ -133,14 +174,14 @@
                 out_ref[pl.ds(g * 128 + 2 * k + b, 8, stride=16), :] = value[b * 8 : (b + 1) * 8]
 
 
-def mode_products(got, factors):
+def mode_products(got):
     return pl.pallas_call(
         mode_kernel,
         out_shape=jax.ShapeDtypeStruct((128 * 16, LANES), jnp.float32),
-        scratch_shapes=[pltpu.VMEM((128 * 64, LANES), jnp.float32)],
+        scratch_shapes=[pltpu.VMEM((128 * WIDE, LANES), jnp.float32)],
         compiler_params=pltpu.CompilerParams(vmem_limit_bytes=VMEM_LARGE),
         name="mode_products",
-    )(got, factors)
+    )(got)
 
 
 def output_kernel(value_ref, factor_ref, out_ref):
@@ -177,17 +218,13 @@
 def per_device(
     spectrum, core_tensor, input_factor, output_factor, first_factor, second_factor, third_factor
 ):
-    mine = jnp.concatenate(
-        [first_factor, second_factor, jnp.zeros((8, LANES - 32), jnp.float32)], axis=1
-    )
-    factors = swap(jnp.broadcast_to(mine, (16, 8, LANES)), ("mx", "my")).reshape(128, LANES)
     everyone = ("mx", "my", "col")
+    second = lax.all_gather(second_factor, "my", axis=0, tiled=True)
     core = jnp.transpose(core_tensor, (0, 1, 3, 4, 5, 2)).reshape(2, 8, 256, 64)
-    chunks = send_chunks(
-        spectrum.reshape(2, 2, 1024, LANES), core, input_factor.T, factors, third_factor
-    )
-    got = swap(chunks.reshape(128, CHUNK, LANES), everyone)
-    values = mode_products(got.reshape(16, 8, CHUNK, LANES), factors)
+    spec = spectrum.reshape(2, 2, 1024, LANES)
+    chunks = send_chunks(spec, core, input_factor.T, first_factor, second, third_factor)
+    got = swap(chunks.reshape(128, 1, CHUNK * LANES), everyone)
+    values = mode_products(got.reshape(128 * CHUNK, LANES))
     values = swap(values.reshape(128, 16, LANES), everyone)
     out = output_modes(values.reshape(2048, LANES), output_factor.T)
     return out.reshape(spectrum.shape)

time: 106 us -> 102 us (0.962)
  local copies, waits for them, and re-layouts: 4.73 us -> 0.01 us
  Pallas kernels: 13.8 us -> 17.2 us
  blocking collectives: 86.6 us -> 84.8 us
    all_to_all x3 -> x2, blocking collectives: 86.6 us -> 75.2 us  [swap(): return lax.all_to_all(chunks, axes, split_axis=0, concat_axis=0, tiled=True)]
    all_gather x0 -> x1, blocking collectives: none -> 9.59 us  [per_device(): second = lax.all_gather(second_factor, 'my', axis=0, tiled=True)]
    unnamed x10 -> x2, local copies, waits for them, and re-layouts: 4.64 us -> 0.01 us
    pallas_call x1, Pallas kernels: 2.57 us -> 6.68 us  [send_chunks(): pl.pallas_call(send_kernel, in_specs=[pl.BlockSpec(memory_space=pl.ANY)]...]
where the time goes in v6:
time: 102 us
  blocking collectives  84.8 us (83%)
  Pallas kernels  17.2 us (17%)
    all_to_all x2, blocking collectives, swap(): return lax.all_to_all(chunks, axes, split_axis=0, concat_axis=0, tiled=True)  75.2 us
    all_gather x1, blocking collectives, per_device(): second = lax.all_gather(second_factor, 'my', axis=0, tiled=True)  9.59 us
    pallas_call x1, Pallas kernels, mode_products(): pl.pallas_call(mode_kernel, out_shape=jax.ShapeDtypeStruct((128 * 16, LAN...  8.33 us
    pallas_call x1, Pallas kernels, send_chunks(): pl.pallas_call(send_kernel, in_specs=[pl.BlockSpec(memory_space=pl.ANY)]...  6.68 us
    pallas_call x1, Pallas kernels, output_modes(): pl.pallas_call(output_kernel, grid=(2,), in_specs=[pl.BlockSpec((2048, LA...  2.2 us

profile of v6, /device:TPU:1, one launch (start us, length us, event | category | flops | bytes accessed | tf_op | source)
XLA Modules:
  0.0 102.0 jit_solution(13983880340872408458)
XLA Ops:
  0.0 9.6 %all_gather.3.second_ref = f32[32,16]{1,0:T(8,128)} all-gather(f32[8,16]{1,0:T(8,128)} %param.12), channel_id=1, replica_groups=mesh['mx'=4,'my'=4,'col'=8] {'my'}, dimensions={0}, use_global_device_ids=true | all-gather | bytes 2560 | tf_op jit(solution)/shard_map/all_gather | solution.py:222
  9.6 6.7 %send_chunks.1 = f32[6272,128]{1,0:T(8,128)} custom-call(f32[2,2,1024,128]{3,2,1,0:T(8,128)} %bitcast.16, f32[2,8,256,64]{3,2,1,0:T(8,128)} %bitcast.17, f32[64,128]{1,0:T(8,128)} %bitcast.18, f32[8,16]{1,0:T(8,128)} %first_ref.1, f32[32,16]{1,0:T(8,128)} %all_gather.3.second_ref, f32[16,16]{1,0:T(8,128)} %third_ref.1), custom_call_target="tpu_custom_call" | custom-call | tf_op jit(solution)/shard_map/send_chunks/pallas_call | solution.py:108
  16.3 51.4 %all_to_all.10 = f32[128,1,6272]{2,1,0:T(1,128)S(1)} all-to-all(f32[128,1,6272]{2,1,0:T(1,128)} %bitcast.15), channel_id=1, replica_groups=mesh['mx'=4,'my'=4,'col'=8] {'mx','my','col'}, dimensions={0} | all-to-all | bytes 6422528 | tf_op jit(solution)/shard_map/all_to_all | solution.py:215
  67.7 8.3 %mode_products.1 = f32[2048,128]{1,0:T(8,128)S(1)} custom-call(f32[6272,128]{1,0:T(8,128)S(1)} %bitcast.11), custom_call_target="tpu_custom_call" | custom-call | tf_op jit(solution)/shard_map/mode_products/pallas_call | solution.py:178
  76.0 0.0 copy-start
  76.0 23.8 %all_to_all.11 = f32[128,16,128]{2,1,0:T(8,128)S(1)} all-to-all(f32[128,16,128]{2,1,0:T(8,128)S(1)} %bitcast.13), channel_id=1, replica_groups=mesh['mx'=4,'my'=4,'col'=8] {'mx','my','col'}, dimensions={0} | all-to-all | bytes 2097152 | tf_op jit(solution)/shard_map/all_to_all | solution.py:215
  99.8 0.0 copy-done
  99.8 2.2 %output_modes.1 = f32[2,2,1024,128]{3,2,1,0:T(8,128)} custom-call(f32[2048,128]{1,0:T(8,128)S(1)} %bitcast.12, f32[64,128]{1,0:T(8,128)S(1)} %bitcast.14), custom_call_target="tpu_custom_call" | custom-call | tf_op jit(solution)/shard_map/output_modes/pallas_call | solution.py:200
Async XLA Ops:
  76.0 23.8 %copy-start = (f32[128,64]{0,1:T(8,128)S(1)}, f32[128,64]{0,1:T(8,128)}, u32[]{:S(2)}) copy-start(f32[128,64]{0,1:T(8,128)} %param.10) | copy-start | bytes 98308

commit v7 on v6

--- a/solution.py
+++ b/solution.py
@@ -64,12 +64,21 @@
     mine = jnp.sum(mine, axis=0, keepdims=True)
     out_ref[pl.ds(48, 128, stride=CHUNK), :] = jnp.broadcast_to(mine, (128, LANES))
 
+    of_t = iota((16, 256), 1) >> 4 == iota((16, 256), 0)
+    of_u = iota((16, 256), 1) & 15 == iota((16, 256), 0)
+    second = pick_lanes(second_ref[...], of_t)
+    third = pick_lanes(third_ref[...], of_u)
+    by_y = pick(iota((512, 32), 0) >> 4 == iota((512, 32), 1), second)
+    by_z = pick(iota((512, 16), 0) & 15 == iota((512, 16), 1), third)
+    mat_high, mat_low = split(by_y * by_z)
+
     high, low = split(in_ref[...])
     rows = jnp.concatenate(
         [jnp.concatenate([high, high], axis=1), jnp.concatenate([low, low], axis=1)], axis=0
     )
     for b in range(2):
         spec_copy(b).wait()
+    for b in range(2):
         for k in range(8):
             both = jnp.concatenate(
                 [spec_ref[part, b, pl.ds(k, 128, stride=8), :] for part in range(2)], axis=1
@@ -79,17 +88,9 @@
             turned = jnp.concatenate([out[:, :LANES], out[:, LANES:]], axis=0).T
             out_ref[pl.ds(2 * k + b, 128, stride=CHUNK), :] = turned
 
-    of_t = iota((16, 256), 1) >> 4 == iota((16, 256), 0)
-    of_u = iota((16, 256), 1) & 15 == iota((16, 256), 0)
-    second = pick_lanes(second_ref[...], of_t)
-    third = pick_lanes(third_ref[...], of_u)
-    by_y = pick(iota((512, 32), 0) >> 4 == iota((512, 32), 1), second)
-    by_z = pick(iota((512, 16), 0) & 15 == iota((512, 16), 1), third)
-    mat_high, mat_low = split(by_y * by_z)
     for pair in range(4):
-        if pair % 2 == 0:
-            core_copy(pair).wait()
-            core_copy(pair + 1).wait()
+        core_copy(pair).wait()
+    for pair in range(4):
         both = jnp.concatenate(
             [core_ref[part, 2 * pair + half] for half in range(2) for part in range(2)], axis=1
         )
@@ -108,7 +109,7 @@
     return pl.pallas_call(
         send_kernel,
         in_specs=[pl.BlockSpec(memory_space=pl.ANY)] * 2 + [whole] * 4,
-        out_shape=jax.ShapeDtypeStruct((128 * CHUNK, LANES), jnp.float32),
+        out_shape=pltpu.VMEM((128 * CHUNK, LANES), jnp.float32),
         scratch_shapes=[
             pltpu.VMEM(spec.shape, jnp.float32),
             pltpu.VMEM(core.shape, jnp.float32),
@@ -131,8 +132,7 @@
         [jnp.concatenate([high, high], axis=1), jnp.concatenate([low, low], axis=1)], axis=0
     )
 
-    @pl.loop(0, 8)
-    def _(src):
+    for src in range(8):
         for two in range(2):
             blocks = [
                 jnp.concatenate(
@@ -155,8 +155,7 @@
 
     left = iota((16, LANES), 1) < 64
 
-    @pl.loop(0, 16)
-    def _(g):
+    for g in range(16):
         for k in range(8):
             x = jnp.concatenate(
                 [got[pl.ds(g * 8 * CHUNK + 2 * k + b, 8, stride=CHUNK), :] for b in range(2)],
@@ -165,7 +164,7 @@
             swapped = pltpu.roll(x, 64, 1)
             real, imag = jnp.where(left, x, swapped), jnp.where(left, swapped, x)
             rows = jnp.concatenate([*split(real), *split(imag)], axis=0)
-            w = w_ref[pl.ds(pl.multiple_of((g * 8 + k) * WIDE, 8), 64), :]
+            w = w_ref[pl.ds((g * 8 + k) * WIDE, 64), :]
             out = dot(rows, jnp.concatenate(split(w), axis=0))
             by_real, by_imag = out[:16] + out[16:32], out[32:48] + out[48:]
             swapped = pltpu.roll(by_imag, 64, 1)

time: 102 us -> 94.4 us (0.925)
  Pallas kernels: 17.2 us -> 9.51 us
    pallas_call x1, Pallas kernels: 8.33 us -> 3.06 us  [mode_products(): pl.pallas_call(mode_kernel, out_shape=jax.ShapeDtypeStruct((128 * 16, LAN...]
    pallas_call x1, Pallas kernels: 6.68 us -> 4.25 us  [send_chunks(): pl.pallas_call(send_kernel, in_specs=[pl.BlockSpec(memory_space=pl.ANY)]...]
where the time goes in v7:
time: 94.4 us; the launch traced here: 94.1 us
  blocking collectives  84.6 us (90%)
  Pallas kernels  9.51 us (10%)
    all_to_all x2, blocking collectives, swap(): return lax.all_to_all(chunks, axes, split_axis=0, concat_axis=0, tiled=True)  75 us
    all_gather x1, blocking collectives, per_device(): second = lax.all_gather(second_factor, 'my', axis=0, tiled=True)  9.59 us
    pallas_call x1, Pallas kernels, send_chunks(): pl.pallas_call(send_kernel, in_specs=[pl.BlockSpec(memory_space=pl.ANY)]...  4.25 us
    pallas_call x1, Pallas kernels, mode_products(): pl.pallas_call(mode_kernel, out_shape=jax.ShapeDtypeStruct((128 * 16, LAN...  3.06 us
    pallas_call x1, Pallas kernels, output_modes(): pl.pallas_call(output_kernel, grid=(2,), in_specs=[pl.BlockSpec((2048, LA...  2.2 us

profile of v7, /device:TPU:1, one launch (start us, length us, event | category | flops | bytes accessed | tf_op | source)
XLA Modules:
  0.0 94.1 jit_solution(17608152797153894268)
XLA Ops:
  0.0 9.6 %all_gather.3.second_ref = f32[32,16]{1,0:T(8,128)} all-gather(f32[8,16]{1,0:T(8,128)} %param.12), channel_id=1, replica_groups=mesh['mx'=4,'my'=4,'col'=8] {'my'}, dimensions={0}, use_global_device_ids=true | all-gather | bytes 2560 | tf_op jit(solution)/shard_map/all_gather | solution.py:221
  9.6 4.3 %send_chunks.1 = f32[6272,128]{1,0:T(8,128)S(1)} custom-call(f32[2,2,1024,128]{3,2,1,0:T(8,128)} %bitcast.16, f32[2,8,256,64]{3,2,1,0:T(8,128)} %bitcast.17, f32[64,128]{1,0:T(8,128)} %bitcast.18, f32[8,16]{1,0:T(8,128)} %first_ref.1, f32[32,16]{1,0:T(8,128)} %all_gather.3.second_ref, f32[16,16]{1,0:T(8,128)} %third_ref.1), custom_call_target="tpu_custom_call" | custom-call | tf_op jit(solution)/shard_map/send_chunks/pallas_call | solution.py:109
  13.9 51.2 %all_to_all.10 = f32[128,1,6272]{2,1,0:T(1,128)S(1)} all-to-all(f32[128,1,6272]{2,1,0:T(1,128)S(1)} %bitcast.12), channel_id=1, replica_groups=mesh['mx'=4,'my'=4,'col'=8] {'mx','my','col'}, dimensions={0} | all-to-all | bytes 6422528 | tf_op jit(solution)/shard_map/all_to_all | solution.py:214
  65.0 3.1 %mode_products.1 = f32[2048,128]{1,0:T(8,128)S(1)} custom-call(f32[6272,128]{1,0:T(8,128)S(1)} %bitcast.11), custom_call_target="tpu_custom_call" | custom-call | tf_op jit(solution)/shard_map/mode_products/pallas_call | solution.py:177
  68.1 0.0 copy-start
  68.1 23.8 %all_to_all.11 = f32[128,16,128]{2,1,0:T(8,128)S(1)} all-to-all(f32[128,16,128]{2,1,0:T(8,128)S(1)} %bitcast.14), channel_id=1, replica_groups=mesh['mx'=4,'my'=4,'col'=8] {'mx','my','col'}, dimensions={0} | all-to-all | bytes 2097152 | tf_op jit(solution)/shard_map/all_to_all | solution.py:214
  91.9 0.0 copy-done
  91.9 2.2 %output_modes.1 = f32[2,2,1024,128]{3,2,1,0:T(8,128)} custom-call(f32[2048,128]{1,0:T(8,128)S(1)} %bitcast.13, f32[64,128]{1,0:T(8,128)S(1)} %bitcast.15), custom_call_target="tpu_custom_call" | custom-call | tf_op jit(solution)/shard_map/output_modes/pallas_call | solution.py:199
Async XLA Ops:
  68.1 23.8 %copy-start = (f32[128,64]{0,1:T(8,128)S(1)}, f32[128,64]{0,1:T(8,128)}, u32[]{:S(2)}) copy-start(f32[128,64]{0,1:T(8,128)} %param.10) | copy-start | bytes 98308

commit v8 on v7

--- a/solution.py
+++ b/solution.py
@@ -5,6 +5,7 @@
 from jax.experimental.pallas import tpu as pltpu
 from jax.sharding import PartitionSpec as P
 
+
 LANES = 128
 CHUNK = 49
 WIDE = 72
@@ -43,41 +44,32 @@
     return (dot(high, one) + dot(mid, one)) + dot(low, one)
 
 
-def send_kernel(
-    spec_hbm, core_hbm, in_ref, first_ref, second_ref, third_ref, out_ref, spec_ref, core_ref, sems
+def spectrum_kernel(
+    spec_hbm, core_hbm, in_hbm, first_hbm, out_ref, half_ref, spec_ref, core_ref, in_ref, first_ref, sems
 ):
-    def spec_copy(b):
-        return pltpu.make_async_copy(spec_hbm.at[:, b], spec_ref.at[:, b], sems.at[b])
-
-    def core_copy(pair):
-        some = pl.ds(2 * pair, 2)
-        return pltpu.make_async_copy(core_hbm.at[:, some], core_ref.at[:, some], sems.at[2 + pair])
-
-    for b in range(2):
-        spec_copy(b).start()
-    for pair in range(4):
-        core_copy(pair).start()
-
+    def copy(source, target, n):
+        made = pltpu.make_async_copy(source, target, sems.at[n])
+        made.start()
+        return made
+
+    small = [copy(first_hbm, first_ref, 0), copy(in_hbm, in_ref, 1)]
+    parts = [copy(spec_hbm.at[:, b], spec_ref.at[:, b], 2 + b) for b in range(2)]
+    parts.append(copy(core_hbm, core_ref, 4))
+
+    for made in small:
+        made.wait()
     of_s = iota((16, 128), 1) & 15 == iota((16, 128), 0)
     mine = pick_lanes(first_ref[...], of_s)
     mine = jnp.where(iota((8, 128), 1) >> 4 == iota((8, 128), 0), mine, 0.0)
     mine = jnp.sum(mine, axis=0, keepdims=True)
     out_ref[pl.ds(48, 128, stride=CHUNK), :] = jnp.broadcast_to(mine, (128, LANES))
 
-    of_t = iota((16, 256), 1) >> 4 == iota((16, 256), 0)
-    of_u = iota((16, 256), 1) & 15 == iota((16, 256), 0)
-    second = pick_lanes(second_ref[...], of_t)
-    third = pick_lanes(third_ref[...], of_u)
-    by_y = pick(iota((512, 32), 0) >> 4 == iota((512, 32), 1), second)
-    by_z = pick(iota((512, 16), 0) & 15 == iota((512, 16), 1), third)
-    mat_high, mat_low = split(by_y * by_z)
-
     high, low = split(in_ref[...])
     rows = jnp.concatenate(
         [jnp.concatenate([high, high], axis=1), jnp.concatenate([low, low], axis=1)], axis=0
     )
-    for b in range(2):
-        spec_copy(b).wait()
+    for made in parts:
+        made.wait()
     for b in range(2):
         for k in range(8):
             both = jnp.concatenate(
@@ -87,14 +79,45 @@
             out = out[:64] + out[64:]
             turned = jnp.concatenate([out[:, :LANES], out[:, LANES:]], axis=0).T
             out_ref[pl.ds(2 * k + b, 128, stride=CHUNK), :] = turned
-
-    for pair in range(4):
-        core_copy(pair).wait()
     for pair in range(4):
         both = jnp.concatenate(
             [core_ref[part, 2 * pair + half] for half in range(2) for part in range(2)], axis=1
         )
-        high, low = split(both)
+        half_ref[pair, 0], half_ref[pair, 1] = split(both)
+
+
+def spectrum_chunks(spec, core, factor, first):
+    return pl.pallas_call(
+        spectrum_kernel,
+        in_specs=[pl.BlockSpec(memory_space=pl.ANY)] * 4,
+        out_shape=(
+            pltpu.VMEM((128 * CHUNK, LANES), jnp.float32),
+            pltpu.VMEM((4, 2, 256, 256), jnp.bfloat16),
+        ),
+        scratch_shapes=[
+            pltpu.VMEM(spec.shape, jnp.float32),
+            pltpu.VMEM(core.shape, jnp.float32),
+            pltpu.VMEM(factor.shape, jnp.float32),
+            pltpu.VMEM(first.shape, jnp.float32),
+            pltpu.SemaphoreType.DMA((5,)),
+        ],
+        compiler_params=pltpu.CompilerParams(vmem_limit_bytes=VMEM_ALONE),
+        name="spectrum_chunks",
+    )(spec, core, factor, first)
+
+
+def core_kernel(_, half_ref, s0_ref, s1_ref, s2_ref, s3_ref, third_ref, out_ref):
+    b = lax.axis_index("my")
+    seconds = jnp.concatenate([ref[...] for ref in (s0_ref, s1_ref, s2_ref, s3_ref)], axis=0)
+    of_t = iota((16, 256), 1) >> 4 == iota((16, 256), 0)
+    of_u = iota((16, 256), 1) & 15 == iota((16, 256), 0)
+    second, third = pick_lanes(seconds, of_t), pick_lanes(third_ref[...], of_u)
+    row = iota((512, 32), 0)
+    by_y = pick(((row >> 7) ^ b) * 8 + ((row & 127) >> 4) == iota((512, 32), 1), second)
+    by_z = pick(iota((512, 16), 0) & 15 == iota((512, 16), 1), third)
+    mat_high, mat_low = split(by_y * by_z)
+    for pair in range(4):
+        high, low = half_ref[pair, 0], half_ref[pair, 1]
         out = dot(mat_high, high) + dot(mat_high, low) + dot(mat_low, high)
         for half in range(2):
             for r in range(4):
@@ -104,20 +127,16 @@
                 ]
 
 
-def send_chunks(spec, core, *factors):
+def core_chunks(chunks, halves, seconds, third):
     whole = pl.BlockSpec(memory_space=pltpu.VMEM)
     return pl.pallas_call(
-        send_kernel,
-        in_specs=[pl.BlockSpec(memory_space=pl.ANY)] * 2 + [whole] * 4,
+        core_kernel,
+        in_specs=[pl.BlockSpec(memory_space=pl.ANY)] + [whole] * 6,
         out_shape=pltpu.VMEM((128 * CHUNK, LANES), jnp.float32),
-        scratch_shapes=[
-            pltpu.VMEM(spec.shape, jnp.float32),
-            pltpu.VMEM(core.shape, jnp.float32),
-            pltpu.SemaphoreType.DMA((6,)),
-        ],
-        compiler_params=pltpu.CompilerParams(vmem_limit_bytes=VMEM_ALONE),
-        name="send_chunks",
-    )(spec, core, *factors)
+        input_output_aliases={0: 0},
+        compiler_params=pltpu.CompilerParams(vmem_limit_bytes=VMEM_SMALL),
+        name="core_chunks",
+    )(chunks, halves, *seconds, third)
 
 
 def mode_kernel(got, out_ref, w_ref):
@@ -218,10 +237,15 @@
     spectrum, core_tensor, input_factor, output_factor, first_factor, second_factor, third_factor
 ):
     everyone = ("mx", "my", "col")
-    second = lax.all_gather(second_factor, "my", axis=0, tiled=True)
+    count = lax.axis_size("my")
+    seconds = [second_factor]
+    for k in range(1, 4):
+        pairs = [(b, b ^ k) for b in range(count)]
+        seconds.append(lax.ppermute(second_factor, "my", pairs))
     core = jnp.transpose(core_tensor, (0, 1, 3, 4, 5, 2)).reshape(2, 8, 256, 64)
     spec = spectrum.reshape(2, 2, 1024, LANES)
-    chunks = send_chunks(spec, core, input_factor.T, first_factor, second, third_factor)
+    chunks, halves = spectrum_chunks(spec, core, input_factor.T, first_factor)
+    chunks = core_chunks(chunks, halves, seconds, third_factor)
     got = swap(chunks.reshape(128, 1, CHUNK * LANES), everyone)
     values = mode_products(got.reshape(128 * CHUNK, LANES))
     values = swap(values.reshape(128, 16, LANES), everyone)

time: 94.4 us -> 91.2 us (0.966)
  blocking collectives: 84.6 us -> 74.8 us
  starting transfers between devices: 0 us -> 4.69 us
  waiting for transfers between devices: 0 us -> 1.39 us
    all_gather x1 -> x0, blocking collectives: 9.59 us -> none  [per_device(): second = lax.all_gather(second_factor, 'my', axis=0, tiled=True)]
    ppermute x0 -> x3, starting transfers between devices: none -> 4.69 us  [per_device(): seconds.append(lax.ppermute(second_factor, 'my', pairs))]
    ppermute x0 -> x3, waiting for transfers between devices: none -> 1.39 us  [per_device(): seconds.append(lax.ppermute(second_factor, 'my', pairs))]
    pallas_call x1 -> x2, Pallas kernels: 4.25 us -> 4.86 us  [the longest x1 3.33 us: spectrum_chunks(): pl.pallas_call(spectrum_kernel, in_specs=[pl.BlockSpec(memory_space=pl.AN...]
  transfers between devices with their start and end apart: 0 -> 3, of which waited for: 0 -> 1; matrix products, arithmetic and copies ran while one was open for 0% -> 0% of each run, Pallas kernels for 0% -> 4%
where the time goes in v8:
time: 91.2 us; the launch traced here: 91.1 us
  blocking collectives  74.8 us (82%)
  Pallas kernels  10.1 us (11%)
  starting transfers between devices  4.69 us (5%)
  waiting for transfers between devices  1.39 us (2%)
    all_to_all x2, blocking collectives, swap(): return lax.all_to_all(chunks, axes, split_axis=0, concat_axis=0, tiled=True)  74.8 us
    ppermute x3, starting transfers between devices, per_device(): seconds.append(lax.ppermute(second_factor, 'my', pairs))  4.69 us
    pallas_call x1, Pallas kernels, spectrum_chunks(): pl.pallas_call(spectrum_kernel, in_specs=[pl.BlockSpec(memory_space=pl.AN...  3.33 us
    pallas_call x1, Pallas kernels, mode_products(): pl.pallas_call(mode_kernel, out_shape=jax.ShapeDtypeStruct((128 * 16, LAN...  3.06 us
    pallas_call x1, Pallas kernels, output_modes(): pl.pallas_call(output_kernel, grid=(2,), in_specs=[pl.BlockSpec((2048, LA...  2.2 us
  transfers between devices with their start and end apart: 3, of which 1 were waited for; matrix products, arithmetic and copies ran while one was open for 0% of the time, Pallas kernels for 4%

profile of v8, /device:TPU:1, one launch (start us, length us, event | category | flops | bytes accessed | tf_op | source)
XLA Modules:
  0.0 91.1 jit_solution(7123003893405969427)
XLA Ops:
  0.0 0.0 copy-start.2
  0.0 0.0 copy-start.1
  0.0 3.7 %collective-permute-start.1 = (f32[8,16]{1,0:T(8,128)}, f32[8,16]{1,0:T(8,128)S(1)}, u32[]{:S(2)}, u32[]{:S(2)}) collective-permute-start(f32[8,16]{1,0:T(8,128)} %s0_ref.1), channel_id=1, source_target_pairs={{0,16},{8,24},{16,0},{24,8},{1,17},{9,25},{17,1},{25,9},{2,18},{10... | collective-permute-start | bytes 1544 | tf_op jit(solution)/shard_map/ppermute | solution.py:244
  3.7 1.0 %collective-permute-start = (f32[8,16]{1,0:T(8,128)}, f32[8,16]{1,0:T(8,128)S(1)}, u32[]{:S(2)}, u32[]{:S(2)}) collective-permute-start(f32[8,16]{1,0:T(8,128)} %s0_ref.1), channel_id=1, source_target_pairs={{0,8},{8,0},{16,24},{24,16},{1,9},{9,1},{17,25},{25,17},{2,10},{10... | collective-permute-start | bytes 1544 | tf_op jit(solution)/shard_map/ppermute | solution.py:244
  4.7 0.0 collective-permute-start.2
  4.7 3.3 %spectrum_chunks.1 = (f32[6272,128]{1,0:T(8,128)S(1)}, bf16[4,2,256,256]{3,2,1,0:T(8,128)(2,1)S(1)}) custom-call(f32[2,2,1024,128]{3,2,1,0:T(8,128)} %bitcast.16, f32[2,8,256,64]{3,2,1,0:T(8,128)} %bitcast.17, f32[64,128]{1,0:T(8,128)} %bitcast.18, f32[8,16]{1,0:T(8,128)} %first_hbm.1), custom_call_target="tpu_custom_call" | custom-call | tf_op jit(solution)/shard_map/spectrum_chunks/pallas_call | solution.py:90
  8.0 0.0 collective-permute-done.1.s2_ref
  8.0 0.0 collective-permute-done.s1_ref
  8.1 1.4 %collective-permute-done.2.s3_ref = f32[8,16]{1,0:T(8,128)S(1)} collective-permute-done((f32[8,16]{1,0:T(8,128)}, f32[8,16]{1,0:T(8,128)S(1)}, u32[]{:S(2)}, u32[]{:S(2)}) %collective-permute-start.2) | collective-permute-done | bytes 544 | tf_op jit(solution)/shard_map/ppermute | solution.py:244
  9.4 0.0 copy-done.2
  9.4 0.0 copy-done.1
  9.4 1.5 %core_chunks.1 = f32[6272,128]{1,0:T(8,128)S(1)} custom-call(f32[6272,128]{1,0:T(8,128)S(1)} %get-tuple-element.7._, bf16[4,2,256,256]{3,2,1,0:T(8,128)(2,1)S(1)} %get-tuple-element.8.half_ref, f32[8,16]{1,0:T(8,128)S(1)} %copy-done.2, f32[8,16]{1,0:T(8,128)S(1)} %collective-permute-done.s1_ref, ...), custom_call_target="tpu_custom_call", output_to_operand_aliasing={{}: (0, {})} | custom-call | tf_op jit(solution)/shard_map/core_chunks/pallas_call | solution.py:132
  11.0 51.0 %all_to_all.10 = f32[128,1,6272]{2,1,0:T(1,128)S(1)} all-to-all(f32[128,1,6272]{2,1,0:T(1,128)S(1)} %bitcast.11), channel_id=1, replica_groups=mesh['mx'=4,'my'=4,'col'=8] {'mx','my','col'}, dimensions={0} | all-to-all | bytes 6422528 | tf_op jit(solution)/shard_map/all_to_all | solution.py:233
  62.0 0.0 copy-start
  62.0 3.1 %mode_products.1 = f32[2048,128]{1,0:T(8,128)S(1)} custom-call(f32[6272,128]{1,0:T(8,128)S(1)} %bitcast.12), custom_call_target="tpu_custom_call" | custom-call | tf_op jit(solution)/shard_map/mode_products/pallas_call | solution.py:196
  65.1 23.8 %all_to_all.11 = f32[128,16,128]{2,1,0:T(8,128)S(1)} all-to-all(f32[128,16,128]{2,1,0:T(8,128)S(1)} %bitcast.14), channel_id=1, replica_groups=mesh['mx'=4,'my'=4,'col'=8] {'mx','my','col'}, dimensions={0} | all-to-all | bytes 2097152 | tf_op jit(solution)/shard_map/all_to_all | solution.py:233
  88.9 0.0 copy-done
  88.9 2.2 %output_modes.1 = f32[2,2,1024,128]{3,2,1,0:T(8,128)} custom-call(f32[2048,128]{1,0:T(8,128)S(1)} %bitcast.13, f32[64,128]{1,0:T(8,128)S(1)} %bitcast.15), custom_call_target="tpu_custom_call" | custom-call | tf_op jit(solution)/shard_map/output_modes/pallas_call | solution.py:218
Async XLA Ops:
  0.0 9.4 %copy-start.2 = (f32[8,16]{1,0:T(8,128)S(1)}, f32[8,16]{1,0:T(8,128)}, u32[]{:S(2)}) copy-start(f32[8,16]{1,0:T(8,128)} %s0_ref.1) | copy-start | bytes 1540
  0.0 9.4 %copy-start.1 = (f32[16,16]{1,0:T(8,128)S(1)}, f32[16,16]{1,0:T(8,128)}, u32[]{:S(2)}) copy-start(f32[16,16]{1,0:T(8,128)} %third_ref.1) | copy-start | bytes 3076
  0.0 8.0 %collective-permute-start.1 = (f32[8,16]{1,0:T(8,128)}, f32[8,16]{1,0:T(8,128)S(1)}, u32[]{:S(2)}, u32[]{:S(2)}) collective-permute-start(f32[8,16]{1,0:T(8,128)} %s0_ref.1), channel_id=1, source_target_pairs={{0,16},{8,24},{16,0},{24,8},{1,17},{9,25},{17,1},{25,9},{2,18},{10... | collective-permute-start | bytes 1544 | tf_op jit(solution)/shard_map/ppermute | solution.py:244
  3.7 4.3 %collective-permute-start = (f32[8,16]{1,0:T(8,128)}, f32[8,16]{1,0:T(8,128)S(1)}, u32[]{:S(2)}, u32[]{:S(2)}) collective-permute-start(f32[8,16]{1,0:T(8,128)} %s0_ref.1), channel_id=1, source_target_pairs={{0,8},{8,0},{16,24},{24,16},{1,9},{9,1},{17,25},{25,17},{2,10},{10... | collective-permute-start | bytes 1544 | tf_op jit(solution)/shard_map/ppermute | solution.py:244
  4.7 4.7 %collective-permute-start.2 = (f32[8,16]{1,0:T(8,128)}, f32[8,16]{1,0:T(8,128)S(1)}, u32[]{:S(2)}, u32[]{:S(2)}) collective-permute-start(f32[8,16]{1,0:T(8,128)} %s0_ref.1), channel_id=1, source_target_pairs={{0,24},{8,16},{16,8},{24,0},{1,25},{9,17},{17,9},{25,1},{2,26},{10... | collective-permute-start | bytes 1544 | tf_op jit(solution)/shard_map/ppermute | solution.py:244
  62.0 26.8 %copy-start = (f32[128,64]{0,1:T(8,128)S(1)}, f32[128,64]{0,1:T(8,128)}, u32[]{:S(2)}) copy-start(f32[128,64]{0,1:T(8,128)} %param.10) | copy-start | bytes 98308

commit v9 on v8

v9 whole, which is shorter than its diff:
```python
import jax
import jax.numpy as jnp
from jax import lax
from jax.experimental import pallas as pl
from jax.experimental.pallas import tpu as pltpu
from jax.sharding import PartitionSpec as P


LANES = 128
SHARE = 65
WIDE = 72
VMEM_SMALL = 16 * 2**20
VMEM_ALONE = 56 * 2**20
VMEM_LARGE = 32 * 2**20


def dot(a, b):
    return jnp.dot(a, b, preferred_element_type=jnp.float32)


def split(x):
    high = x.astype(jnp.bfloat16)
    return high, (x - high.astype(jnp.float32)).astype(jnp.bfloat16)


def split3(x):
    high = x.astype(jnp.bfloat16)
    return (high, *split(x - high.astype(jnp.float32)))


def iota(shape, dim):
    return lax.broadcasted_iota(jnp.int32, shape, dim)


def pick(chosen, table):
    one = chosen.astype(jnp.bfloat16)
    high, mid, low = split3(table)
    return (dot(one, high) + dot(one, mid)) + dot(one, low)


def pick_lanes(table, chosen):
    one = chosen.astype(jnp.bfloat16)
    high, mid, low = split3(table)
    return (dot(high, one) + dot(mid, one)) + dot(low, one)


def spectrum_kernel(spec_hbm, in_hbm, first_hbm, out_ref, spec_ref, in_ref, first_ref, sems):
    def copy(source, target, n):
        made = pltpu.make_async_copy(source, target, sems.at[n])
        made.start()
        return made

    small = [copy(first_hbm, first_ref, 0), copy(in_hbm, in_ref, 1)]
    parts = [copy(spec_hbm.at[:, b], spec_ref.at[:, b], 2 + b) for b in range(2)]

    for made in small:
        made.wait()
    of_s = iota((16, 128), 1) & 15 == iota((16, 128), 0)
    mine = pick_lanes(first_ref[...], of_s)
    mine = jnp.where(iota((8, 128), 1) >> 4 == iota((8, 128), 0), mine, 0.0)
    mine = jnp.sum(mine, axis=0, keepdims=True)
    out_ref[pl.ds(64, 32, stride=SHARE), :] = jnp.broadcast_to(mine, (32, LANES))

    high, low = split(in_ref[...])
    rows = jnp.concatenate(
        [jnp.concatenate([high, high], axis=1), jnp.concatenate([low, low], axis=1)], axis=0
    )
    for made in parts:
        made.wait()
    for b in range(2):
        for k in range(8):
            both = jnp.concatenate(
                [spec_ref[part, b, pl.ds(k, 128, stride=8), :] for part in range(2)], axis=1
            )
            out = dot(rows, jnp.concatenate(split(both), axis=0))
            out = out[:64] + out[64:]
            turned = jnp.concatenate([out[:, :LANES], out[:, LANES:]], axis=0).T
            for r in range(4):
                row = 8 * k + 2 * r + b
                out_ref[pl.ds(row, 32, stride=SHARE), :] = turned[r * 32 : (r + 1) * 32]


def spectrum_chunks(spec, factor, first):
    return pl.pallas_call(
        spectrum_kernel,
        in_specs=[pl.BlockSpec(memory_space=pl.ANY)] * 3,
        out_shape=jax.ShapeDtypeStruct((32 * SHARE, LANES), jnp.float32),
        scratch_shapes=[
            pltpu.VMEM(spec.shape, jnp.float32),
            pltpu.VMEM(factor.shape, jnp.float32),
            pltpu.VMEM(first.shape, jnp.float32),
            pltpu.SemaphoreType.DMA((4,)),
        ],
        compiler_params=pltpu.CompilerParams(vmem_limit_bytes=VMEM_ALONE),
        name="spectrum_chunks",
    )(spec, factor, first)


def half_kernel(core_ref, half_ref):
    for pair in range(4):
        both = jnp.concatenate(
            [core_ref[part, 2 * pair + half] for half in range(2) for part in range(2)], axis=1
        )
        half_ref[pair, 0], half_ref[pair, 1] = split(both)


def core_halves(core):
    return pl.pallas_call(
        half_kernel,
        out_shape=pltpu.VMEM((4, 2, 256, 256), jnp.bfloat16),
        compiler_params=pltpu.CompilerParams(vmem_limit_bytes=VMEM_SMALL),
        name="core_halves",
    )(core)


def core_kernel(half_ref, s0_ref, s1_ref, s2_ref, s3_ref, third_ref, out_ref):
    own = lax.axis_index("my")
    seconds = jnp.concatenate([ref[...] for ref in (s0_ref, s1_ref, s2_ref, s3_ref)], axis=0)

    def place(width):
        row, col = iota((512, width), 0), iota((512, width), 1)
        c, b, a, r = row & 7, (row >> 3) & 3, (row >> 5) & 3, row >> 7
        return col, (b ^ own) * 8 + 2 * r + (a >> 1), (a & 1) * 8 + c

    of_t = iota((16, 256), 1) >> 4 == iota((16, 256), 0)
    of_u = iota((16, 256), 1) & 15 == iota((16, 256), 0)
    second, third = pick_lanes(seconds, of_t), pick_lanes(third_ref[...], of_u)
    col, ky, _ = place(32)
    by_y = pick(col == ky, second)
    col, _, kz = place(16)
    mat_high, mat_low = split(by_y * pick(col == kz, third))
    for pair in range(4):
        high, low = half_ref[pair, 0], half_ref[pair, 1]
        out = dot(mat_high, high) + dot(mat_high, low) + dot(mat_low, high)
        for half in range(2):
            for r in range(4):
                row = (2 * pair + half) * 4 + r
                out_ref[pl.ds(row, 128, stride=32), :] = out[
                    r * 128 : (r + 1) * 128, half * LANES : (half + 1) * LANES
                ]


def core_chunks(halves, seconds, third):
    return pl.pallas_call(
        core_kernel,
        out_shape=pltpu.VMEM((128 * 32, LANES), jnp.float32),
        compiler_params=pltpu.CompilerParams(vmem_limit_bytes=VMEM_SMALL),
        name="core_chunks",
    )(halves, *seconds, third)


def mode_kernel(core, spec, out_ref, w_ref):
    row, col = iota((256, 128), 0), iota((256, 128), 1)
    first = jnp.concatenate([spec[pl.ds(a * 8 * SHARE + 64, 1), :] for a in range(4)] * 2, axis=0)
    first = pick((iota((256, 8), 0) >> 5) & 3 == iota((256, 8), 1), first)
    first = jnp.where(col >> 4 == (row >> 2) & 7, first, 0.0)
    first = pick_lanes(first, iota((128, 128), 0) & 15 == iota((128, 128), 1) >> 3)
    same = ((row >> 7) == ((col >> 2) & 1)) & ((row & 3) == (col & 3))
    high, low = split(jnp.where(same, first, 0.0))
    expand = jnp.concatenate(
        [jnp.concatenate([high, high], axis=1), jnp.concatenate([low, low], axis=1)], axis=0
    )

    for src in range(8):
        for two in range(2):
            blocks = [
                jnp.concatenate(
                    [
                        core[pl.ds((s * 8 + src) * 32 + 8 * pair, 8), :]
                        for s in range(16)
                    ],
                    axis=0,
                )
                for pair in (2 * two, 2 * two + 1)
            ]
            out = dot(expand, jnp.concatenate(split(jnp.concatenate(blocks, axis=1)), axis=0))
            out = out[:256] + out[256:]
            for pair in range(2):
                for half in range(2):
                    p = src * 8 + (2 * two + pair) * 2 + half
                    w_ref[pl.ds(p, 128, stride=WIDE), :] = out[
                        half * 128 : (half + 1) * 128, pair * LANES : (pair + 1) * LANES
                    ]

    left = iota((16, LANES), 1) < 64

    out_ref[pl.ds(64, 32, stride=SHARE), :] = jnp.zeros((32, LANES), jnp.float32)
    for a in range(4):
        for kr in range(32):
            start = a * 8 * SHARE + 2 * kr
            x = jnp.concatenate(
                [spec[pl.ds(start + b, 8, stride=SHARE), :] for b in range(2)], axis=0
            )
            swapped = pltpu.roll(x, 64, 1)
            real, imag = jnp.where(left, x, swapped), jnp.where(left, swapped, x)
            rows = jnp.concatenate([*split(real), *split(imag)], axis=0)
            w = w_ref[pl.ds((a * 32 + kr) * WIDE, 64), :]
            out = dot(rows, jnp.concatenate(split(w), axis=0))
            by_real, by_imag = out[:16] + out[16:32], out[32:48] + out[48:]
            swapped = pltpu.roll(by_imag, 64, 1)
            value = by_real + jnp.where(left, -swapped, swapped)
            for b in range(2):
                out_ref[pl.ds(start + b, 8, stride=SHARE), :] = value[b * 8 : (b + 1) * 8]


def mode_products(core, spec):
    return pl.pallas_call(
        mode_kernel,
        out_shape=pltpu.VMEM((32 * SHARE, LANES), jnp.float32),
        scratch_shapes=[pltpu.VMEM((128 * WIDE, LANES), jnp.float32)],
        compiler_params=pltpu.CompilerParams(vmem_limit_bytes=VMEM_LARGE),
        name="mode_products",
    )(core, spec)


def output_kernel(value_ref, factor_ref, out_ref):
    high, low = split(factor_ref[...].T)
    factor = jnp.concatenate([high, high, low, low], axis=1)
    step = pl.program_id(0)
    for k in range(8):
        rows = [value_ref[pl.ds(8 * k + 2 * r + step, 32, stride=SHARE), :] for r in range(4)]
        turned = jnp.concatenate(rows, axis=0).T
        high, low = split(jnp.concatenate([turned[:64], turned[64:]], axis=1))
        out = dot(factor, jnp.concatenate([high, low, high, low], axis=0))
        for part in range(2):
            out_ref[part, 0, pl.ds(k, 128, stride=8), :] = out[:, part * LANES : (part + 1) * LANES]


def output_modes(values, factor):
    return pl.pallas_call(
        output_kernel,
        grid=(2,),
        in_specs=[
            pl.BlockSpec((32 * SHARE, LANES), lambda i: (0, 0)),
            pl.BlockSpec((64, 128), lambda i: (0, 0)),
        ],
        out_specs=pl.BlockSpec((2, 1, 1024, LANES), lambda i: (0, i, 0, 0)),
        out_shape=jax.ShapeDtypeStruct((2, 2, 1024, LANES), jnp.float32),
        compiler_params=pltpu.CompilerParams(vmem_limit_bytes=VMEM_SMALL),
        name="output_modes",
    )(values, factor)


def swap(chunks, axes):
    return lax.all_to_all(chunks, axes, split_axis=0, concat_axis=0, tiled=True)


def per_device(
    spectrum, core_tensor, input_factor, output_factor, first_factor, second_factor, third_factor
):
    count = lax.axis_size("my")
    spec = spectrum.reshape(2, 2, 1024, LANES)
    spec = spectrum_chunks(spec, input_factor.T, first_factor)
    spec = swap(spec.reshape(32, 1, SHARE * LANES), ("mx", "col"))
    seconds = [second_factor]
    for k in range(1, 4):
        pairs = [(b, b ^ k) for b in range(count)]
        seconds.append(lax.ppermute(second_factor, "my", pairs))
    core = jnp.transpose(core_tensor, (0, 1, 3, 4, 5, 2)).reshape(2, 8, 256, 64)
    halves = core_halves(core)
    core = core_chunks(halves, seconds, third_factor)
    core = swap(core.reshape(128, 32, LANES), ("mx", "my", "col"))
    values = mode_products(core.reshape(128 * 32, LANES), spec.reshape(32 * SHARE, LANES))
    values = swap(values.reshape(32, 1, SHARE * LANES), ("mx", "col"))
    out = output_modes(values.reshape(32 * SHARE, LANES), output_factor.T)
    return out.reshape(spectrum.shape)


def solution(mesh):
    placed = (
        P(None, "col", None, "mx", "my"),
        P(None, "col", None, ("mx", "my"), None, None),
        P(),
        P(),
        P("mx", None),
        P("my", None),
        P(),
    )
    return jax.shard_map(
        per_device,
        mesh=mesh,
        in_specs=placed,
        out_specs=P(None, "col", None, "mx", "my"),
        check_vma=False,
    )
```

time: 91.2 us -> 94.9 us (1.041); the launches traced: 91.1 us -> 93.7 us
  blocking collectives: 74.8 us -> 59.6 us
  starting transfers between devices: 4.69 us -> 13.9 us
  waiting for transfers between devices: 1.39 us -> 8.58 us
  Pallas kernels: 10.1 us -> 11.6 us
    all_to_all x2, blocking collectives: 74.8 us -> 59.6 us  [swap(): return lax.all_to_all(chunks, axes, split_axis=0, concat_axis=0, tiled=True)]
    all_to_all x0 -> x1, starting transfers between devices: none -> 9.73 us  [swap(): return lax.all_to_all(chunks, axes, split_axis=0, concat_axis=0, tiled=True)]
    ppermute x3, waiting for transfers between devices: 1.39 us -> 6.76 us  [per_device(): seconds.append(lax.ppermute(second_factor, 'my', pairs))]
    all_to_all x0 -> x1, waiting for transfers between devices: none -> 1.82 us  [swap(): return lax.all_to_all(chunks, axes, split_axis=0, concat_axis=0, tiled=True)]
    pallas_call x3 -> x4, Pallas kernels: 6.8 us -> 8.14 us  [the longest x1 3.09 us: mode_products(): pl.pallas_call(mode_kernel, out_shape=pltpu.VMEM((32 * SHARE, LANES), jnp...]
  transfers between devices with their start and end apart: 3 -> 4, of which waited for: 1 -> 3; matrix products, arithmetic and copies ran while one was open for 0% -> 0% of each run, Pallas kernels for 4% -> 3%
where the time goes in v9:
time: 94.9 us; the launch traced here: 93.7 us
  blocking collectives  59.6 us (63%)
  starting transfers between devices  13.9 us (15%)
  Pallas kernels  11.6 us (12%)
  waiting for transfers between devices  8.58 us (9%)
    all_to_all x2, blocking collectives, swap(): return lax.all_to_all(chunks, axes, split_axis=0, concat_axis=0, tiled=True)  59.6 us
    all_to_all x1, starting transfers between devices, swap(): return lax.all_to_all(chunks, axes, split_axis=0, concat_axis=0, tiled=True)  9.73 us
    ppermute x3, waiting for transfers between devices, per_device(): seconds.append(lax.ppermute(second_factor, 'my', pairs))  6.76 us
    ppermute x3, starting transfers between devices, per_device(): seconds.append(lax.ppermute(second_factor, 'my', pairs))  4.17 us
    pallas_call x1, Pallas kernels, spectrum_chunks(): pl.pallas_call(spectrum_kernel, in_specs=[pl.BlockSpec(memory_space=pl.AN...  3.43 us
    pallas_call x1, Pallas kernels, mode_products(): pl.pallas_call(mode_kernel, out_shape=pltpu.VMEM((32 * SHARE, LANES), jnp...  3.09 us
    pallas_call x1, Pallas kernels, core_chunks(): pl.pallas_call(core_kernel, out_shape=pltpu.VMEM((128 * 32, LANES), jnp.f...  2.51 us
    pallas_call x1, Pallas kernels, output_modes(): pl.pallas_call(output_kernel, grid=(2,), in_specs=[pl.BlockSpec((32 * SHA...  2.2 us
  transfers between devices with their start and end apart: 4, of which 3 were waited for; matrix products, arithmetic and copies ran while one was open for 0% of the time, Pallas kernels for 3%

profile of v9, /device:TPU:1, one launch (start us, length us, event | category | flops | bytes accessed | tf_op | source)
XLA Modules:
  0.0 93.7 jit_solution(2460713375409400277)
XLA Ops:
  0.0 0.0 copy-start.3
  0.0 0.0 copy-start
  0.0 3.4 %spectrum_chunks.1 = f32[2080,128]{1,0:T(8,128)} custom-call(f32[2,2,1024,128]{3,2,1,0:T(8,128)} %bitcast.21, f32[64,128]{1,0:T(8,128)} %bitcast.22, f32[8,16]{1,0:T(8,128)} %first_hbm.1), custom_call_target="tpu_custom_call" | custom-call | tf_op jit(solution)/shard_map/spectrum_chunks/pallas_call | solution.py:84
  3.4 9.7 %all-to-all-start.1 = ((f32[32,1,8320]{2,1,0:T(1,128)}), f32[32,1,8320]{2,1,0:T(1,128)S(1)}, u32[]{:S(2)}, u32[]{:S(2)}) async-start(f32[32,1,8320]{2,1,0:T(1,128)} %bitcast.20), calls=%async_computation.1 | async-start | bytes 2129920 | tf_op jit(solution)/shard_map/all_to_all | solution.py:245
  13.2 0.0 copy-done.3
  13.2 0.0 copy-start.2
  13.2 2.7 %collective-permute-start.1 = (f32[8,16]{1,0:T(8,128)S(1)}, f32[8,16]{1,0:T(8,128)S(1)}, u32[]{:S(2)}, u32[]{:S(2)}) collective-permute-start(f32[8,16]{1,0:T(8,128)S(1)} %copy-done.3), channel_id=1, source_target_pairs={{0,16},{8,24},{16,0},{24,8},{1,17},{9,25},{17,1},{25,9},{2,18},{10... | collective-permute-start | bytes 1544 | tf_op jit(solution)/shard_map/ppermute | solution.py:258
  15.9 1.2 %collective-permute-start = (f32[8,16]{1,0:T(8,128)S(1)}, f32[8,16]{1,0:T(8,128)S(1)}, u32[]{:S(2)}, u32[]{:S(2)}) collective-permute-start(f32[8,16]{1,0:T(8,128)S(1)} %copy-done.3), channel_id=1, source_target_pairs={{0,8},{8,0},{16,24},{24,16},{1,9},{9,1},{17,25},{25,17},{2,10},{10... | collective-permute-start | bytes 1544 | tf_op jit(solution)/shard_map/ppermute | solution.py:258
  17.1 0.2 collective-permute-start.2
  17.4 0.0 copy-done
  17.4 0.3 core_halves.1.half_ref
  17.7 4.0 %collective-permute-done.1.s2_ref = f32[8,16]{1,0:T(8,128)S(1)} collective-permute-done((f32[8,16]{1,0:T(8,128)S(1)}, f32[8,16]{1,0:T(8,128)S(1)}, u32[]{:S(2)}, u32[]{:S(2)}) %collective-permute-start.1) | collective-permute-done | bytes 544 | tf_op jit(solution)/shard_map/ppermute | solution.py:258
  21.7 0.0 collective-permute-done.s1_ref
  21.7 2.8 %collective-permute-done.2.s3_ref = f32[8,16]{1,0:T(8,128)S(1)} collective-permute-done((f32[8,16]{1,0:T(8,128)S(1)}, f32[8,16]{1,0:T(8,128)S(1)}, u32[]{:S(2)}, u32[]{:S(2)}) %collective-permute-start.2) | collective-permute-done | bytes 544 | tf_op jit(solution)/shard_map/ppermute | solution.py:258
  24.5 0.0 copy-done.2
  24.5 2.5 %core_chunks.1 = f32[4096,128]{1,0:T(8,128)S(1)} custom-call(bf16[4,2,256,256]{3,2,1,0:T(8,128)(2,1)S(1)} %core_halves.1.half_ref, f32[8,16]{1,0:T(8,128)S(1)} %copy-done.3, f32[8,16]{1,0:T(8,128)S(1)} %collective-permute-done.s1_ref, f32[8,16]{1,0:T(8,128)S(1)} %collective-permute-done.1.s2_ref, f32[8,16]{1,0:T(8,128)S(1)} %collective-permute-done.2.s3_ref, ...), custom_call_target="tpu_custom_call" | custom-call | tf_op jit(solution)/shard_map/core_chunks/pallas_call | solution.py:144
  27.0 1.8 %all-to-all-done.1 = f32[32,1,8320]{2,1,0:T(1,128)S(1)} async-done(((f32[32,1,8320]{2,1,0:T(1,128)}), f32[32,1,8320]{2,1,0:T(1,128)S(1)}, u32[]{:S(2)}, u32[]{:S(2)}) %all-to-all-start.1) | async-done | bytes 1064992 | tf_op jit(solution)/shard_map/all_to_all | solution.py:245
  28.8 39.6 %all_to_all.15 = f32[128,32,128]{2,1,0:T(8,128)S(1)} all-to-all(f32[128,32,128]{2,1,0:T(8,128)S(1)} %bitcast.13), channel_id=1, replica_groups=mesh['mx'=4,'my'=4,'col'=8] {'mx','my','col'}, dimensions={0} | all-to-all | bytes 4194304 | tf_op jit(solution)/shard_map/all_to_all | solution.py:245
  68.4 3.1 %mode_products.1 = f32[2080,128]{1,0:T(8,128)S(1)} custom-call(f32[4096,128]{1,0:T(8,128)S(1)} %bitcast.14, f32[2080,128]{1,0:T(8,128)S(1)} %bitcast.16), custom_call_target="tpu_custom_call" | custom-call | tf_op jit(solution)/shard_map/mode_products/pallas_call | solution.py:207
  71.5 0.0 copy-start.1
  71.5 20.0 %all_to_all.16 = f32[32,1,8320]{2,1,0:T(1,128)S(1)} all-to-all(f32[32,1,8320]{2,1,0:T(1,128)S(1)} %bitcast.17), channel_id=1, replica_groups=mesh['mx'=4,'my'=4,'col'=8] {'mx','col'}, dimensions={0} | all-to-all | bytes 2129920 | tf_op jit(solution)/shard_map/all_to_all | solution.py:245
  91.5 0.0 copy-done.1
  91.5 2.2 %output_modes.1 = f32[2,2,1024,128]{3,2,1,0:T(8,128)} custom-call(f32[2080,128]{1,0:T(8,128)S(1)} %bitcast.15, f32[64,128]{1,0:T(8,128)S(1)} %bitcast.19), custom_call_target="tpu_custom_call" | custom-call | tf_op jit(solution)/shard_map/output_modes/pallas_call | solution.py:230
Async XLA Ops:
  0.0 13.2 %copy-start.3 = (f32[8,16]{1,0:T(8,128)S(1)}, f32[8,16]{1,0:T(8,128)}, u32[]{:S(2)}) copy-start(f32[8,16]{1,0:T(8,128)} %s0_ref.1) | copy-start | bytes 1540
  0.0 17.4 %copy-start = (f32[2,8,64,1,16,16]{2,5,4,3,1,0:T(8,128)S(1)}, f32[2,8,64,1,16,16]{2,5,4,3,1,0:T(8,128)}, u32[]{:S(2)}) copy-start(f32[2,8,64,1,16,16]{2,5,4,3,1,0:T(8,128)} %param.8) | copy-start | bytes 3145732
  3.4 25.4 %all-to-all-start.1 = ((f32[32,1,8320]{2,1,0:T(1,128)}), f32[32,1,8320]{2,1,0:T(1,128)S(1)}, u32[]{:S(2)}, u32[]{:S(2)}) async-start(f32[32,1,8320]{2,1,0:T(1,128)} %bitcast.20), calls=%async_computation.1 | async-start | bytes 2129920 | tf_op jit(solution)/shard_map/all_to_all | solution.py:245
  13.2 11.3 %copy-start.2 = (f32[16,16]{1,0:T(8,128)S(1)}, f32[16,16]{1,0:T(8,128)}, u32[]{:S(2)}) copy-start(f32[16,16]{1,0:T(8,128)} %third_ref.1) | copy-start | bytes 3076
  13.2 8.5 %collective-permute-start.1 = (f32[8,16]{1,0:T(8,128)S(1)}, f32[8,16]{1,0:T(8,128)S(1)}, u32[]{:S(2)}, u32[]{:S(2)}) collective-permute-start(f32[8,16]{1,0:T(8,128)S(1)} %copy-done.3), channel_id=1, source_target_pairs={{0,16},{8,24},{16,0},{24,8},{1,17},{9,25},{17,1},{25,9},{2,18},{10... | collective-permute-start | bytes 1544 | tf_op jit(solution)/shard_map/ppermute | solution.py:258
  15.9 5.8 %collective-permute-start = (f32[8,16]{1,0:T(8,128)S(1)}, f32[8,16]{1,0:T(8,128)S(1)}, u32[]{:S(2)}, u32[]{:S(2)}) collective-permute-start(f32[8,16]{1,0:T(8,128)S(1)} %copy-done.3), channel_id=1, source_target_pairs={{0,8},{8,0},{16,24},{24,16},{1,9},{9,1},{17,25},{25,17},{2,10},{10... | collective-permute-start | bytes 1544 | tf_op jit(solution)/shard_map/ppermute | solution.py:258
  17.1 7.4 %collective-permute-start.2 = (f32[8,16]{1,0:T(8,128)S(1)}, f32[8,16]{1,0:T(8,128)S(1)}, u32[]{:S(2)}, u32[]{:S(2)}) collective-permute-start(f32[8,16]{1,0:T(8,128)S(1)} %copy-done.3), channel_id=1, source_target_pairs={{0,24},{8,16},{16,8},{24,0},{1,25},{9,17},{17,9},{25,1},{2,26},{10... | collective-permute-start | bytes 1544 | tf_op jit(solution)/shard_map/ppermute | solution.py:258
  71.5 20.0 %copy-start.1 = (f32[128,64]{0,1:T(8,128)S(1)}, f32[128,64]{0,1:T(8,128)}, u32[]{:S(2)}) copy-start(f32[128,64]{0,1:T(8,128)} %param.10) | copy-start | bytes 98308

commit v10 on v8

--- a/solution.py
+++ b/solution.py
@@ -45,16 +45,17 @@
 
 
 def spectrum_kernel(
-    spec_hbm, core_hbm, in_hbm, first_hbm, out_ref, half_ref, spec_ref, core_ref, in_ref, first_ref, sems
+    spec_hbm, core_hbm, in_hbm, first_hbm, third_hbm, out_ref, half_ref, by_z_ref,
+    spec_ref, core_ref, in_ref, first_ref, third_ref, sems,
 ):
     def copy(source, target, n):
         made = pltpu.make_async_copy(source, target, sems.at[n])
         made.start()
         return made
 
-    small = [copy(first_hbm, first_ref, 0), copy(in_hbm, in_ref, 1)]
-    parts = [copy(spec_hbm.at[:, b], spec_ref.at[:, b], 2 + b) for b in range(2)]
-    parts.append(copy(core_hbm, core_ref, 4))
+    small = [copy(first_hbm, first_ref, 0), copy(in_hbm, in_ref, 1), copy(third_hbm, third_ref, 2)]
+    parts = [copy(spec_hbm.at[:, b], spec_ref.at[:, b], 3 + b) for b in range(2)]
+    parts.append(copy(core_hbm, core_ref, 5))
 
     for made in small:
         made.wait()
@@ -68,9 +69,11 @@
     rows = jnp.concatenate(
         [jnp.concatenate([high, high], axis=1), jnp.concatenate([low, low], axis=1)], axis=0
     )
-    for made in parts:
-        made.wait()
+    of_u = iota((16, 256), 1) & 15 == iota((16, 256), 0)
+    third = pick_lanes(third_ref[...], of_u)
+    by_z_ref[...] = pick(iota((128, 16), 0) & 15 == iota((128, 16), 1), third)
     for b in range(2):
+        parts[b].wait()
         for k in range(8):
             both = jnp.concatenate(
                 [spec_ref[part, b, pl.ds(k, 128, stride=8), :] for part in range(2)], axis=1
@@ -79,6 +82,7 @@
             out = out[:64] + out[64:]
             turned = jnp.concatenate([out[:, :LANES], out[:, LANES:]], axis=0).T
             out_ref[pl.ds(2 * k + b, 128, stride=CHUNK), :] = turned
+    parts[2].wait()
     for pair in range(4):
         both = jnp.concatenate(
             [core_ref[part, 2 * pair + half] for half in range(2) for part in range(2)], axis=1
@@ -86,35 +90,36 @@
         half_ref[pair, 0], half_ref[pair, 1] = split(both)
 
 
-def spectrum_chunks(spec, core, factor, first):
+def spectrum_chunks(spec, core, factor, first, third):
     return pl.pallas_call(
         spectrum_kernel,
-        in_specs=[pl.BlockSpec(memory_space=pl.ANY)] * 4,
+        in_specs=[pl.BlockSpec(memory_space=pl.ANY)] * 5,
         out_shape=(
             pltpu.VMEM((128 * CHUNK, LANES), jnp.float32),
             pltpu.VMEM((4, 2, 256, 256), jnp.bfloat16),
+            pltpu.VMEM((128, 256), jnp.float32),
         ),
         scratch_shapes=[
             pltpu.VMEM(spec.shape, jnp.float32),
             pltpu.VMEM(core.shape, jnp.float32),
             pltpu.VMEM(factor.shape, jnp.float32),
             pltpu.VMEM(first.shape, jnp.float32),
-            pltpu.SemaphoreType.DMA((5,)),
+            pltpu.VMEM(third.shape, jnp.float32),
+            pltpu.SemaphoreType.DMA((6,)),
         ],
         compiler_params=pltpu.CompilerParams(vmem_limit_bytes=VMEM_ALONE),
         name="spectrum_chunks",
-    )(spec, core, factor, first)
-
-
-def core_kernel(_, half_ref, s0_ref, s1_ref, s2_ref, s3_ref, third_ref, out_ref):
+    )(spec, core, factor, first, third)
+
+
+def core_kernel(_, half_ref, by_z_ref, s0_ref, s1_ref, s2_ref, s3_ref, out_ref):
     b = lax.axis_index("my")
     seconds = jnp.concatenate([ref[...] for ref in (s0_ref, s1_ref, s2_ref, s3_ref)], axis=0)
     of_t = iota((16, 256), 1) >> 4 == iota((16, 256), 0)
-    of_u = iota((16, 256), 1) & 15 == iota((16, 256), 0)
-    second, third = pick_lanes(seconds, of_t), pick_lanes(third_ref[...], of_u)
+    second = pick_lanes(seconds, of_t)
     row = iota((512, 32), 0)
     by_y = pick(((row >> 7) ^ b) * 8 + ((row & 127) >> 4) == iota((512, 32), 1), second)
-    by_z = pick(iota((512, 16), 0) & 15 == iota((512, 16), 1), third)
+    by_z = jnp.concatenate([by_z_ref[...]] * 4, axis=0)
     mat_high, mat_low = split(by_y * by_z)
     for pair in range(4):
         high, low = half_ref[pair, 0], half_ref[pair, 1]
@@ -127,7 +132,7 @@
                 ]
 
 
-def core_chunks(chunks, halves, seconds, third):
+def core_chunks(chunks, halves, by_z, seconds):
     whole = pl.BlockSpec(memory_space=pltpu.VMEM)
     return pl.pallas_call(
         core_kernel,
@@ -136,41 +141,39 @@
         input_output_aliases={0: 0},
         compiler_params=pltpu.CompilerParams(vmem_limit_bytes=VMEM_SMALL),
         name="core_chunks",
-    )(chunks, halves, *seconds, third)
+    )(chunks, halves, by_z, *seconds)
 
 
 def mode_kernel(got, out_ref, w_ref):
-    row, col = iota((256, 128), 0), iota((256, 128), 1)
+    row, col = iota((128, 128), 0), iota((128, 128), 1)
     first = jnp.concatenate([got[pl.ds(a * 32 * CHUNK + 48, 1), :] for a in range(4)] * 2, axis=0)
-    first = pick((iota((256, 8), 0) >> 5) & 3 == iota((256, 8), 1), first)
+    first = pick(iota((128, 8), 0) >> 5 == iota((128, 8), 1), first)
     first = jnp.where(col >> 4 == row & 7, first, 0.0)
-    first = pick_lanes(first, iota((128, 128), 0) & 15 == iota((128, 128), 1) >> 3)
-    same = ((row >> 7) == ((col >> 2) & 1)) & (((row >> 3) & 3) == (col & 3))
-    high, low = split(jnp.where(same, first, 0.0))
-    expand = jnp.concatenate(
-        [jnp.concatenate([high, high], axis=1), jnp.concatenate([low, low], axis=1)], axis=0
-    )
-
-    for src in range(8):
-        for two in range(2):
-            blocks = [
+    first = pick_lanes(first, row & 15 == col & 15)
+    high, low = split(jnp.where((row >> 3) & 3 == (col >> 4) & 3, first, 0.0))
+    expand = jnp.concatenate([high, low], axis=1)
+
+    for pair in range(32):
+        src, two = pair // 4, pair % 4
+        block = jnp.concatenate(
+            [
                 jnp.concatenate(
                     [
-                        got[pl.ds((s * 8 + src) * CHUNK + 16 + 8 * pair, 8), :]
-                        for s in range(16)
+                        got[pl.ds(src * CHUNK + 16 + (2 * two + half) * 4 + r, 16, stride=8 * CHUNK), :]
+                        for r in range(4)
                     ],
                     axis=0,
                 )
-                for pair in (2 * two, 2 * two + 1)
+                for half in range(2)
+            ],
+            axis=1,
+        )
+        high, low = split(block)
+        out = dot(expand, jnp.concatenate([high, low, high, low], axis=0))
+        for half in range(2):
+            w_ref[pl.ds(src * 8 + 2 * two + half, 128, stride=WIDE), :] = out[
+                :, half * LANES : (half + 1) * LANES
             ]
-            out = dot(expand, jnp.concatenate(split(jnp.concatenate(blocks, axis=1)), axis=0))
-            out = out[:256] + out[256:]
-            for pair in range(2):
-                for half in range(2):
-                    p = src * 8 + (2 * two + pair) * 2 + half
-                    w_ref[pl.ds(p, 128, stride=WIDE), :] = out[
-                        half * 128 : (half + 1) * 128, pair * LANES : (pair + 1) * LANES
-                    ]
 
     left = iota((16, LANES), 1) < 64
 
@@ -244,8 +247,8 @@
         seconds.append(lax.ppermute(second_factor, "my", pairs))
     core = jnp.transpose(core_tensor, (0, 1, 3, 4, 5, 2)).reshape(2, 8, 256, 64)
     spec = spectrum.reshape(2, 2, 1024, LANES)
-    chunks, halves = spectrum_chunks(spec, core, input_factor.T, first_factor)
-    chunks = core_chunks(chunks, halves, seconds, third_factor)
+    chunks, halves, by_z = spectrum_chunks(spec, core, input_factor.T, first_factor, third_factor)
+    chunks = core_chunks(chunks, halves, by_z, seconds)
     got = swap(chunks.reshape(128, 1, CHUNK * LANES), everyone)
     values = mode_products(got.reshape(128 * CHUNK, LANES))
     values = swap(values.reshape(128, 16, LANES), everyone)

time: 91.2 us -> 90.1 us (0.988)
  Pallas kernels: 10.1 us -> 9.03 us
  transfers between devices with their start and end apart: 3 -> 3, of which waited for: 1 -> 1; matrix products, arithmetic and copies ran while one was open for 0% -> 0% of each run, Pallas kernels for 4% -> 3%
where the time goes in v10:
time: 90.1 us; the launch traced here: 90 us
  blocking collectives  74.2 us (82%)
  Pallas kernels  9.03 us (10%)
  starting transfers between devices  4.69 us (5%)
  waiting for transfers between devices  2.05 us (2%)
    all_to_all x2, blocking collectives, swap(): return lax.all_to_all(chunks, axes, split_axis=0, concat_axis=0, tiled=True)  74.2 us
    ppermute x3, starting transfers between devices, per_device(): seconds.append(lax.ppermute(second_factor, 'my', pairs))  4.69 us
    pallas_call x1, Pallas kernels, mode_products(): pl.pallas_call(mode_kernel, out_shape=jax.ShapeDtypeStruct((128 * 16, LAN...  2.78 us
    pallas_call x1, Pallas kernels, spectrum_chunks(): pl.pallas_call(spectrum_kernel, in_specs=[pl.BlockSpec(memory_space=pl.AN...  2.67 us
    pallas_call x1, Pallas kernels, output_modes(): pl.pallas_call(output_kernel, grid=(2,), in_specs=[pl.BlockSpec((2048, LA...  2.2 us
    ppermute x3, waiting for transfers between devices, per_device(): seconds.append(lax.ppermute(second_factor, 'my', pairs))  2.05 us
  transfers between devices with their start and end apart: 3, of which 1 were waited for; matrix products, arithmetic and copies ran while one was open for 0% of the time, Pallas kernels for 3%

profile of v10, /device:TPU:1, one launch (start us, length us, event | category | flops | bytes accessed | tf_op | source)
XLA Modules:
  0.0 90.0 jit_solution(8265600270110796727)
XLA Ops:
  0.0 0.0 copy-start.1
  0.0 3.7 %collective-permute-start.1 = (f32[8,16]{1,0:T(8,128)}, f32[8,16]{1,0:T(8,128)S(1)}, u32[]{:S(2)}, u32[]{:S(2)}) collective-permute-start(f32[8,16]{1,0:T(8,128)} %s0_ref.1), channel_id=1, source_target_pairs={{0,16},{8,24},{16,0},{24,8},{1,17},{9,25},{17,1},{25,9},{2,18},{10... | collective-permute-start | bytes 1544 | tf_op jit(solution)/shard_map/ppermute | solution.py:247
  3.7 1.0 %collective-permute-start = (f32[8,16]{1,0:T(8,128)}, f32[8,16]{1,0:T(8,128)S(1)}, u32[]{:S(2)}, u32[]{:S(2)}) collective-permute-start(f32[8,16]{1,0:T(8,128)} %s0_ref.1), channel_id=1, source_target_pairs={{0,8},{8,0},{16,24},{24,16},{1,9},{9,1},{17,25},{25,17},{2,10},{10... | collective-permute-start | bytes 1544 | tf_op jit(solution)/shard_map/ppermute | solution.py:247
  4.7 0.0 collective-permute-start.2
  4.7 2.7 %spectrum_chunks.1 = (f32[6272,128]{1,0:T(8,128)S(1)}, bf16[4,2,256,256]{3,2,1,0:T(8,128)(2,1)S(1)}, f32[128,256]{1,0:T(8,128)S(1)}) custom-call(f32[2,2,1024,128]{3,2,1,0:T(8,128)} %bitcast.16, f32[2,8,256,64]{3,2,1,0:T(8,128)} %bitcast.17, f32[64,128]{1,0:T(8,128)} %bitcast.18, f32[8,16]{1,0:T(8,128)} %first_hbm.1, f32[16,16]{1,0:T(8,128)} %third_hbm.1), custom_call_target="tpu_custom_call" | custom-call | tf_op jit(solution)/shard_map/spectrum_chunks/pallas_call | solution.py:94
  7.4 0.0 collective-permute-done.1.s2_ref
  7.4 0.0 collective-permute-done.s1_ref
  7.4 2.0 %collective-permute-done.2.s3_ref = f32[8,16]{1,0:T(8,128)S(1)} collective-permute-done((f32[8,16]{1,0:T(8,128)}, f32[8,16]{1,0:T(8,128)S(1)}, u32[]{:S(2)}, u32[]{:S(2)}) %collective-permute-start.2) | collective-permute-done | bytes 544 | tf_op jit(solution)/shard_map/ppermute | solution.py:247
  9.4 0.0 copy-done.1
  9.4 1.4 %core_chunks.1 = f32[6272,128]{1,0:T(8,128)S(1)} custom-call(f32[6272,128]{1,0:T(8,128)S(1)} %get-tuple-element.8._, bf16[4,2,256,256]{3,2,1,0:T(8,128)(2,1)S(1)} %get-tuple-element.9.half_ref, f32[128,256]{1,0:T(8,128)S(1)} %get-tuple-element.10.by_z_ref, f32[8,16]{1,0:T(8,128)S(1)} %copy-done.1, ...), custom_call_target="tpu_custom_call", output_to_operand_aliasing={{}: (0, {})} | custom-call | tf_op jit(solution)/shard_map/core_chunks/pallas_call | solution.py:137
  10.8 50.4 %all_to_all.10 = f32[128,1,6272]{2,1,0:T(1,128)S(1)} all-to-all(f32[128,1,6272]{2,1,0:T(1,128)S(1)} %bitcast.12), channel_id=1, replica_groups=mesh['mx'=4,'my'=4,'col'=8] {'mx','my','col'}, dimensions={0} | all-to-all | bytes 6422528 | tf_op jit(solution)/shard_map/all_to_all | solution.py:236
  61.2 0.0 copy-start
  61.2 2.8 %mode_products.1 = f32[2048,128]{1,0:T(8,128)S(1)} custom-call(f32[6272,128]{1,0:T(8,128)S(1)} %bitcast.11), custom_call_target="tpu_custom_call" | custom-call | tf_op jit(solution)/shard_map/mode_products/pallas_call | solution.py:199
  64.0 23.8 %all_to_all.11 = f32[128,16,128]{2,1,0:T(8,128)S(1)} all-to-all(f32[128,16,128]{2,1,0:T(8,128)S(1)} %bitcast.14), channel_id=1, replica_groups=mesh['mx'=4,'my'=4,'col'=8] {'mx','my','col'}, dimensions={0} | all-to-all | bytes 2097152 | tf_op jit(solution)/shard_map/all_to_all | solution.py:236
  87.8 0.0 copy-done
  87.8 2.2 %output_modes.1 = f32[2,2,1024,128]{3,2,1,0:T(8,128)} custom-call(f32[2048,128]{1,0:T(8,128)S(1)} %bitcast.13, f32[64,128]{1,0:T(8,128)S(1)} %bitcast.15), custom_call_target="tpu_custom_call" | custom-call | tf_op jit(solution)/shard_map/output_modes/pallas_call | solution.py:221
Async XLA Ops:
  0.0 9.4 %copy-start.1 = (f32[8,16]{1,0:T(8,128)S(1)}, f32[8,16]{1,0:T(8,128)}, u32[]{:S(2)}) copy-start(f32[8,16]{1,0:T(8,128)} %s0_ref.1) | copy-start | bytes 1540
  0.0 7.4 %collective-permute-start.1 = (f32[8,16]{1,0:T(8,128)}, f32[8,16]{1,0:T(8,128)S(1)}, u32[]{:S(2)}, u32[]{:S(2)}) collective-permute-start(f32[8,16]{1,0:T(8,128)} %s0_ref.1), channel_id=1, source_target_pairs={{0,16},{8,24},{16,0},{24,8},{1,17},{9,25},{17,1},{25,9},{2,18},{10... | collective-permute-start | bytes 1544 | tf_op jit(solution)/shard_map/ppermute | solution.py:247
  3.7 3.6 %collective-permute-start = (f32[8,16]{1,0:T(8,128)}, f32[8,16]{1,0:T(8,128)S(1)}, u32[]{:S(2)}, u32[]{:S(2)}) collective-permute-start(f32[8,16]{1,0:T(8,128)} %s0_ref.1), channel_id=1, source_target_pairs={{0,8},{8,0},{16,24},{24,16},{1,9},{9,1},{17,25},{25,17},{2,10},{10... | collective-permute-start | bytes 1544 | tf_op jit(solution)/shard_map/ppermute | solution.py:247
  4.7 4.7 %collective-permute-start.2 = (f32[8,16]{1,0:T(8,128)}, f32[8,16]{1,0:T(8,128)S(1)}, u32[]{:S(2)}, u32[]{:S(2)}) collective-permute-start(f32[8,16]{1,0:T(8,128)} %s0_ref.1), channel_id=1, source_target_pairs={{0,24},{8,16},{16,8},{24,0},{1,25},{9,17},{17,9},{25,1},{2,26},{10... | collective-permute-start | bytes 1544 | tf_op jit(solution)/shard_map/ppermute | solution.py:247
  61.2 26.6 %copy-start = (f32[128,64]{0,1:T(8,128)S(1)}, f32[128,64]{0,1:T(8,128)}, u32[]{:S(2)}) copy-start(f32[128,64]{0,1:T(8,128)} %param.10) | copy-start | bytes 98308

commit v11 on v10

--- a/solution.py
+++ b/solution.py
@@ -8,7 +8,7 @@
 
 LANES = 128
 CHUNK = 49
-WIDE = 72
+WIDE = 65
 VMEM_SMALL = 16 * 2**20
 VMEM_ALONE = 56 * 2**20
 VMEM_LARGE = 32 * 2**20
@@ -176,6 +176,7 @@
             ]
 
     left = iota((16, LANES), 1) < 64
+    sign = jnp.where(left, -1.0, 1.0)
 
     for g in range(16):
         for k in range(8):
@@ -190,7 +191,7 @@
             out = dot(rows, jnp.concatenate(split(w), axis=0))
             by_real, by_imag = out[:16] + out[16:32], out[32:48] + out[48:]
             swapped = pltpu.roll(by_imag, 64, 1)
-            value = by_real + jnp.where(left, -swapped, swapped)
+            value = by_real + sign * swapped
             for b in range(2):
                 out_ref[pl.ds(g * 128 + 2 * k + b, 8, stride=16), :] = value[b * 8 : (b + 1) * 8]
 
@@ -205,28 +206,33 @@
     )(got)
 
 
-def output_kernel(value_ref, factor_ref, out_ref):
+def output_kernel(value_ref, factor_ref, out_hbm, out_ref, sems):
     high, low = split(factor_ref[...].T)
     factor = jnp.concatenate([high, high, low, low], axis=1)
-    step = pl.program_id(0)
-    for k in range(8):
-        turned = value_ref[pl.ds(2 * k + step, 128, stride=16), :].T
-        high, low = split(jnp.concatenate([turned[:64], turned[64:]], axis=1))
-        out = dot(factor, jnp.concatenate([high, low, high, low], axis=0))
-        for part in range(2):
-            out_ref[part, 0, pl.ds(k, 128, stride=8), :] = out[:, part * LANES : (part + 1) * LANES]
+    copies = [
+        pltpu.make_async_copy(out_ref.at[:, b], out_hbm.at[:, b], sems.at[b]) for b in range(2)
+    ]
+    for b in range(2):
+        for k in range(8):
+            turned = value_ref[pl.ds(2 * k + b, 128, stride=16), :].T
+            high, low = split(jnp.concatenate([turned[:64], turned[64:]], axis=1))
+            out = dot(factor, jnp.concatenate([high, low, high, low], axis=0))
+            for part in range(2):
+                out_ref[part, b, pl.ds(k, 128, stride=8), :] = out[
+                    :, part * LANES : (part + 1) * LANES
+                ]
+        copies[b].start()
+    for copy in copies:
+        copy.wait()
 
 
 def output_modes(values, factor):
+    whole = (2, 2, 1024, LANES)
     return pl.pallas_call(
         output_kernel,
-        grid=(2,),
-        in_specs=[
-            pl.BlockSpec((2048, LANES), lambda i: (0, 0)),
-            pl.BlockSpec((64, 128), lambda i: (0, 0)),
-        ],
-        out_specs=pl.BlockSpec((2, 1, 1024, LANES), lambda i: (0, i, 0, 0)),
-        out_shape=jax.ShapeDtypeStruct((2, 2, 1024, LANES), jnp.float32),
+        out_specs=pl.BlockSpec(memory_space=pl.ANY),
+        out_shape=jax.ShapeDtypeStruct(whole, jnp.float32),
+        scratch_shapes=[pltpu.VMEM(whole, jnp.float32), pltpu.SemaphoreType.DMA((2,))],
         compiler_params=pltpu.CompilerParams(vmem_limit_bytes=VMEM_SMALL),
         name="output_modes",
     )(values, factor)

time: 90.1 us -> 89.6 us (level)
  no operation moved by 1% of the time
where the time goes in v11:
time: 89.6 us; the launch traced here: 89.4 us
  blocking collectives  74.2 us (83%)
  Pallas kernels  8.47 us (9%)
  starting transfers between devices  4.69 us (5%)
  waiting for transfers between devices  2.05 us (2%)
    all_to_all x2, blocking collectives, swap(): return lax.all_to_all(chunks, axes, split_axis=0, concat_axis=0, tiled=True)  74.2 us
    ppermute x3, starting transfers between devices, per_device(): seconds.append(lax.ppermute(second_factor, 'my', pairs))  4.69 us
    pallas_call x1, Pallas kernels, spectrum_chunks(): pl.pallas_call(spectrum_kernel, in_specs=[pl.BlockSpec(memory_space=pl.AN...  2.67 us
    pallas_call x1, Pallas kernels, mode_products(): pl.pallas_call(mode_kernel, out_shape=jax.ShapeDtypeStruct((128 * 16, LAN...  2.43 us
    ppermute x3, waiting for transfers between devices, per_device(): seconds.append(lax.ppermute(second_factor, 'my', pairs))  2.05 us
    pallas_call x1, Pallas kernels, output_modes(): pl.pallas_call(output_kernel, out_specs=pl.BlockSpec(memory_space=pl.ANY)...  1.99 us
  transfers between devices with their start and end apart: 3, of which 1 were waited for; matrix products, arithmetic and copies ran while one was open for 0% of the time, Pallas kernels for 3%

profile of v11, /device:TPU:1, one launch (start us, length us, event | category | flops | bytes accessed | tf_op | source)
XLA Modules:
  0.0 89.4 jit_solution(16585084147936088711)
XLA Ops:
  0.0 0.0 copy-start.1
  0.0 3.7 %collective-permute-start.1 = (f32[8,16]{1,0:T(8,128)}, f32[8,16]{1,0:T(8,128)S(1)}, u32[]{:S(2)}, u32[]{:S(2)}) collective-permute-start(f32[8,16]{1,0:T(8,128)} %s0_ref.1), channel_id=1, source_target_pairs={{0,16},{8,24},{16,0},{24,8},{1,17},{9,25},{17,1},{25,9},{2,18},{10... | collective-permute-start | bytes 1544 | tf_op jit(solution)/shard_map/ppermute | solution.py:253
  3.7 1.0 %collective-permute-start = (f32[8,16]{1,0:T(8,128)}, f32[8,16]{1,0:T(8,128)S(1)}, u32[]{:S(2)}, u32[]{:S(2)}) collective-permute-start(f32[8,16]{1,0:T(8,128)} %s0_ref.1), channel_id=1, source_target_pairs={{0,8},{8,0},{16,24},{24,16},{1,9},{9,1},{17,25},{25,17},{2,10},{10... | collective-permute-start | bytes 1544 | tf_op jit(solution)/shard_map/ppermute | solution.py:253
  4.7 0.0 collective-permute-start.2
  4.7 2.7 %spectrum_chunks.1 = (f32[6272,128]{1,0:T(8,128)S(1)}, bf16[4,2,256,256]{3,2,1,0:T(8,128)(2,1)S(1)}, f32[128,256]{1,0:T(8,128)S(1)}) custom-call(f32[2,2,1024,128]{3,2,1,0:T(8,128)} %bitcast.16, f32[2,8,256,64]{3,2,1,0:T(8,128)} %bitcast.17, f32[64,128]{1,0:T(8,128)} %bitcast.18, f32[8,16]{1,0:T(8,128)} %first_hbm.1, f32[16,16]{1,0:T(8,128)} %third_hbm.1), custom_call_target="tpu_custom_call" | custom-call | tf_op jit(solution)/shard_map/spectrum_chunks/pallas_call | solution.py:94
  7.4 0.0 collective-permute-done.1.s2_ref
  7.4 0.0 collective-permute-done.s1_ref
  7.4 2.0 %collective-permute-done.2.s3_ref = f32[8,16]{1,0:T(8,128)S(1)} collective-permute-done((f32[8,16]{1,0:T(8,128)}, f32[8,16]{1,0:T(8,128)S(1)}, u32[]{:S(2)}, u32[]{:S(2)}) %collective-permute-start.2) | collective-permute-done | bytes 544 | tf_op jit(solution)/shard_map/ppermute | solution.py:253
  9.4 0.0 copy-done.1
  9.4 1.4 %core_chunks.1 = f32[6272,128]{1,0:T(8,128)S(1)} custom-call(f32[6272,128]{1,0:T(8,128)S(1)} %get-tuple-element.8._, bf16[4,2,256,256]{3,2,1,0:T(8,128)(2,1)S(1)} %get-tuple-element.9.half_ref, f32[128,256]{1,0:T(8,128)S(1)} %get-tuple-element.10.by_z_ref, f32[8,16]{1,0:T(8,128)S(1)} %copy-done.1, ...), custom_call_target="tpu_custom_call", output_to_operand_aliasing={{}: (0, {})} | custom-call | tf_op jit(solution)/shard_map/core_chunks/pallas_call | solution.py:137
  10.8 50.4 %all_to_all.10 = f32[128,1,6272]{2,1,0:T(1,128)S(1)} all-to-all(f32[128,1,6272]{2,1,0:T(1,128)S(1)} %bitcast.12), channel_id=1, replica_groups=mesh['mx'=4,'my'=4,'col'=8] {'mx','my','col'}, dimensions={0} | all-to-all | bytes 6422528 | tf_op jit(solution)/shard_map/all_to_all | solution.py:242
  61.2 0.0 copy-start
  61.2 2.4 %mode_products.1 = f32[2048,128]{1,0:T(8,128)S(1)} custom-call(f32[6272,128]{1,0:T(8,128)S(1)} %bitcast.11), custom_call_target="tpu_custom_call" | custom-call | tf_op jit(solution)/shard_map/mode_products/pallas_call | solution.py:200
  63.6 23.8 %all_to_all.11 = f32[128,16,128]{2,1,0:T(8,128)S(1)} all-to-all(f32[128,16,128]{2,1,0:T(8,128)S(1)} %bitcast.14), channel_id=1, replica_groups=mesh['mx'=4,'my'=4,'col'=8] {'mx','my','col'}, dimensions={0} | all-to-all | bytes 2097152 | tf_op jit(solution)/shard_map/all_to_all | solution.py:242
  87.4 0.0 copy-done
  87.4 2.0 %output_modes.1 = f32[2,2,1024,128]{3,2,1,0:T(8,128)} custom-call(f32[2048,128]{1,0:T(8,128)S(1)} %bitcast.13, f32[64,128]{1,0:T(8,128)S(1)} %bitcast.15), custom_call_target="tpu_custom_call" | custom-call | tf_op jit(solution)/shard_map/output_modes/pallas_call | solution.py:231
Async XLA Ops:
  0.0 9.4 %copy-start.1 = (f32[8,16]{1,0:T(8,128)S(1)}, f32[8,16]{1,0:T(8,128)}, u32[]{:S(2)}) copy-start(f32[8,16]{1,0:T(8,128)} %s0_ref.1) | copy-start | bytes 1540
  0.0 7.4 %collective-permute-start.1 = (f32[8,16]{1,0:T(8,128)}, f32[8,16]{1,0:T(8,128)S(1)}, u32[]{:S(2)}, u32[]{:S(2)}) collective-permute-start(f32[8,16]{1,0:T(8,128)} %s0_ref.1), channel_id=1, source_target_pairs={{0,16},{8,24},{16,0},{24,8},{1,17},{9,25},{17,1},{25,9},{2,18},{10... | collective-permute-start | bytes 1544 | tf_op jit(solution)/shard_map/ppermute | solution.py:253
  3.7 3.6 %collective-permute-start = (f32[8,16]{1,0:T(8,128)}, f32[8,16]{1,0:T(8,128)S(1)}, u32[]{:S(2)}, u32[]{:S(2)}) collective-permute-start(f32[8,16]{1,0:T(8,128)} %s0_ref.1), channel_id=1, source_target_pairs={{0,8},{8,0},{16,24},{24,16},{1,9},{9,1},{17,25},{25,17},{2,10},{10... | collective-permute-start | bytes 1544 | tf_op jit(solution)/shard_map/ppermute | solution.py:253
  4.7 4.7 %collective-permute-start.2 = (f32[8,16]{1,0:T(8,128)}, f32[8,16]{1,0:T(8,128)S(1)}, u32[]{:S(2)}, u32[]{:S(2)}) collective-permute-start(f32[8,16]{1,0:T(8,128)} %s0_ref.1), channel_id=1, source_target_pairs={{0,24},{8,16},{16,8},{24,0},{1,25},{9,17},{17,9},{25,1},{2,26},{10... | collective-permute-start | bytes 1544 | tf_op jit(solution)/shard_map/ppermute | solution.py:253
  61.2 26.2 %copy-start = (f32[128,64]{0,1:T(8,128)S(1)}, f32[128,64]{0,1:T(8,128)}, u32[]{:S(2)}) copy-start(f32[128,64]{0,1:T(8,128)} %param.10) | copy-start | bytes 98308

commit v12 on v11

--- a/solution.py
+++ b/solution.py
@@ -32,16 +32,16 @@
     return lax.broadcasted_iota(jnp.int32, shape, dim)
 
 
-def pick(chosen, table):
-    one = chosen.astype(jnp.bfloat16)
-    high, mid, low = split3(table)
-    return (dot(one, high) + dot(one, mid)) + dot(one, low)
-
-
-def pick_lanes(table, chosen):
-    one = chosen.astype(jnp.bfloat16)
-    high, mid, low = split3(table)
-    return (dot(high, one) + dot(mid, one)) + dot(low, one)
+def pick(rows, chosen, table):
+    shape = (rows, 3 * table.shape[0])
+    one = chosen(iota(shape, 0), iota(shape, 1) & (table.shape[0] - 1)).astype(jnp.bfloat16)
+    return dot(one, jnp.concatenate(split3(table), axis=0))
+
+
+def pick_lanes(table, lanes, chosen):
+    shape = (3 * table.shape[1], lanes)
+    one = chosen(iota(shape, 0) & (table.shape[1] - 1), iota(shape, 1)).astype(jnp.bfloat16)
+    return dot(jnp.concatenate(split3(table), axis=1), one)
 
 
 def spectrum_kernel(
@@ -59,8 +59,7 @@
 
     for made in small:
         made.wait()
-    of_s = iota((16, 128), 1) & 15 == iota((16, 128), 0)
-    mine = pick_lanes(first_ref[...], of_s)
+    mine = pick_lanes(first_ref[...], 128, lambda row, col: col & 15 == row)
     mine = jnp.where(iota((8, 128), 1) >> 4 == iota((8, 128), 0), mine, 0.0)
     mine = jnp.sum(mine, axis=0, keepdims=True)
     out_ref[pl.ds(48, 128, stride=CHUNK), :] = jnp.broadcast_to(mine, (128, LANES))
@@ -69,9 +68,8 @@
     rows = jnp.concatenate(
         [jnp.concatenate([high, high], axis=1), jnp.concatenate([low, low], axis=1)], axis=0
     )
-    of_u = iota((16, 256), 1) & 15 == iota((16, 256), 0)
-    third = pick_lanes(third_ref[...], of_u)
-    by_z_ref[...] = pick(iota((128, 16), 0) & 15 == iota((128, 16), 1), third)
+    third = pick_lanes(third_ref[...], 256, lambda row, col: col & 15 == row)
+    by_z_ref[...] = pick(128, lambda row, col: row & 15 == col, third)
     for b in range(2):
         parts[b].wait()
         for k in range(8):
@@ -115,10 +113,10 @@
 def core_kernel(_, half_ref, by_z_ref, s0_ref, s1_ref, s2_ref, s3_ref, out_ref):
     b = lax.axis_index("my")
     seconds = jnp.concatenate([ref[...] for ref in (s0_ref, s1_ref, s2_ref, s3_ref)], axis=0)
-    of_t = iota((16, 256), 1) >> 4 == iota((16, 256), 0)
-    second = pick_lanes(seconds, of_t)
-    row = iota((512, 32), 0)
-    by_y = pick(((row >> 7) ^ b) * 8 + ((row & 127) >> 4) == iota((512, 32), 1), second)
+    second = pick_lanes(seconds, 256, lambda row, col: col >> 4 == row)
+    by_y = pick(
+        512, lambda row, col: ((row >> 7) ^ b) * 8 + ((row & 127) >> 4) == col, second
+    )
     by_z = jnp.concatenate([by_z_ref[...]] * 4, axis=0)
     mat_high, mat_low = split(by_y * by_z)
     for pair in range(4):
@@ -147,9 +145,9 @@
 def mode_kernel(got, out_ref, w_ref):
     row, col = iota((128, 128), 0), iota((128, 128), 1)
     first = jnp.concatenate([got[pl.ds(a * 32 * CHUNK + 48, 1), :] for a in range(4)] * 2, axis=0)
-    first = pick(iota((128, 8), 0) >> 5 == iota((128, 8), 1), first)
+    first = pick(128, lambda row, col: row >> 5 == col, first)
     first = jnp.where(col >> 4 == row & 7, first, 0.0)
-    first = pick_lanes(first, row & 15 == col & 15)
+    first = pick_lanes(first, 128, lambda row, col: row & 15 == col & 15)
     high, low = split(jnp.where((row >> 3) & 3 == (col >> 4) & 3, first, 0.0))
     expand = jnp.concatenate([high, low], axis=1)
 

time: 89.6 us -> 89.4 us (level)
  no operation moved by 1% of the time
where the time goes in v12:
time: 89.4 us; the launch traced here: 89.3 us
  blocking collectives  74.1 us (83%)
  Pallas kernels  8.33 us (9%)
  starting transfers between devices  4.69 us (5%)
  waiting for transfers between devices  2.05 us (2%)
    all_to_all x2, blocking collectives, swap(): return lax.all_to_all(chunks, axes, split_axis=0, concat_axis=0, tiled=True)  74.1 us
    ppermute x3, starting transfers between devices, per_device(): seconds.append(lax.ppermute(second_factor, 'my', pairs))  4.69 us
    pallas_call x1, Pallas kernels, spectrum_chunks(): pl.pallas_call(spectrum_kernel, in_specs=[pl.BlockSpec(memory_space=pl.AN...  2.67 us
    pallas_call x1, Pallas kernels, mode_products(): pl.pallas_call(mode_kernel, out_shape=jax.ShapeDtypeStruct((128 * 16, LAN...  2.38 us
    ppermute x3, waiting for transfers between devices, per_device(): seconds.append(lax.ppermute(second_factor, 'my', pairs))  2.05 us
    pallas_call x1, Pallas kernels, output_modes(): pl.pallas_call(output_kernel, out_specs=pl.BlockSpec(memory_space=pl.ANY)...  1.99 us
  transfers between devices with their start and end apart: 3, of which 1 were waited for; matrix products, arithmetic and copies ran while one was open for 0% of the time, Pallas kernels for 3%

profile of v12, /device:TPU:1, one launch (start us, length us, event | category | flops | bytes accessed | tf_op | source)
XLA Modules:
  0.0 89.3 jit_solution(2968109989278857246)
XLA Ops:
  0.0 0.0 copy-start.1
  0.0 3.7 %collective-permute-start.1 = (f32[8,16]{1,0:T(8,128)}, f32[8,16]{1,0:T(8,128)S(1)}, u32[]{:S(2)}, u32[]{:S(2)}) collective-permute-start(f32[8,16]{1,0:T(8,128)} %s0_ref.1), channel_id=1, source_target_pairs={{0,16},{8,24},{16,0},{24,8},{1,17},{9,25},{17,1},{25,9},{2,18},{10... | collective-permute-start | bytes 1544 | tf_op jit(solution)/shard_map/ppermute | solution.py:251
  3.7 1.0 %collective-permute-start = (f32[8,16]{1,0:T(8,128)}, f32[8,16]{1,0:T(8,128)S(1)}, u32[]{:S(2)}, u32[]{:S(2)}) collective-permute-start(f32[8,16]{1,0:T(8,128)} %s0_ref.1), channel_id=1, source_target_pairs={{0,8},{8,0},{16,24},{24,16},{1,9},{9,1},{17,25},{25,17},{2,10},{10... | collective-permute-start | bytes 1544 | tf_op jit(solution)/shard_map/ppermute | solution.py:251
  4.7 0.0 collective-permute-start.2
  4.7 2.7 %spectrum_chunks.1 = (f32[6272,128]{1,0:T(8,128)S(1)}, bf16[4,2,256,256]{3,2,1,0:T(8,128)(2,1)S(1)}, f32[128,256]{1,0:T(8,128)S(1)}) custom-call(f32[2,2,1024,128]{3,2,1,0:T(8,128)} %bitcast.16, f32[2,8,256,64]{3,2,1,0:T(8,128)} %bitcast.17, f32[64,128]{1,0:T(8,128)} %bitcast.18, f32[8,16]{1,0:T(8,128)} %first_hbm.1, f32[16,16]{1,0:T(8,128)} %third_hbm.1), custom_call_target="tpu_custom_call" | custom-call | tf_op jit(solution)/shard_map/spectrum_chunks/pallas_call | solution.py:92
  7.4 0.0 collective-permute-done.1.s2_ref
  7.4 0.0 collective-permute-done.s1_ref
  7.4 2.0 %collective-permute-done.2.s3_ref = f32[8,16]{1,0:T(8,128)S(1)} collective-permute-done((f32[8,16]{1,0:T(8,128)}, f32[8,16]{1,0:T(8,128)S(1)}, u32[]{:S(2)}, u32[]{:S(2)}) %collective-permute-start.2) | collective-permute-done | bytes 544 | tf_op jit(solution)/shard_map/ppermute | solution.py:251
  9.4 0.0 copy-done.1
  9.4 1.3 %core_chunks.1 = f32[6272,128]{1,0:T(8,128)S(1)} custom-call(f32[6272,128]{1,0:T(8,128)S(1)} %get-tuple-element.8._, bf16[4,2,256,256]{3,2,1,0:T(8,128)(2,1)S(1)} %get-tuple-element.9.half_ref, f32[128,256]{1,0:T(8,128)S(1)} %get-tuple-element.10.by_z_ref, f32[8,16]{1,0:T(8,128)S(1)} %copy-done.1, ...), custom_call_target="tpu_custom_call", output_to_operand_aliasing={{}: (0, {})} | custom-call | tf_op jit(solution)/shard_map/core_chunks/pallas_call | solution.py:135
  10.7 50.4 %all_to_all.10 = f32[128,1,6272]{2,1,0:T(1,128)S(1)} all-to-all(f32[128,1,6272]{2,1,0:T(1,128)S(1)} %bitcast.12), channel_id=1, replica_groups=mesh['mx'=4,'my'=4,'col'=8] {'mx','my','col'}, dimensions={0} | all-to-all | bytes 6422528 | tf_op jit(solution)/shard_map/all_to_all | solution.py:240
  61.1 0.0 copy-start
  61.1 2.4 %mode_products.1 = f32[2048,128]{1,0:T(8,128)S(1)} custom-call(f32[6272,128]{1,0:T(8,128)S(1)} %bitcast.11), custom_call_target="tpu_custom_call" | custom-call | tf_op jit(solution)/shard_map/mode_products/pallas_call | solution.py:198
  63.5 23.8 %all_to_all.11 = f32[128,16,128]{2,1,0:T(8,128)S(1)} all-to-all(f32[128,16,128]{2,1,0:T(8,128)S(1)} %bitcast.14), channel_id=1, replica_groups=mesh['mx'=4,'my'=4,'col'=8] {'mx','my','col'}, dimensions={0} | all-to-all | bytes 2097152 | tf_op jit(solution)/shard_map/all_to_all | solution.py:240
  87.3 0.0 copy-done
  87.3 2.0 %output_modes.1 = f32[2,2,1024,128]{3,2,1,0:T(8,128)} custom-call(f32[2048,128]{1,0:T(8,128)S(1)} %bitcast.13, f32[64,128]{1,0:T(8,128)S(1)} %bitcast.15), custom_call_target="tpu_custom_call" | custom-call | tf_op jit(solution)/shard_map/output_modes/pallas_call | solution.py:229
Async XLA Ops:
  0.0 9.4 %copy-start.1 = (f32[8,16]{1,0:T(8,128)S(1)}, f32[8,16]{1,0:T(8,128)}, u32[]{:S(2)}) copy-start(f32[8,16]{1,0:T(8,128)} %s0_ref.1) | copy-start | bytes 1540
  0.0 7.4 %collective-permute-start.1 = (f32[8,16]{1,0:T(8,128)}, f32[8,16]{1,0:T(8,128)S(1)}, u32[]{:S(2)}, u32[]{:S(2)}) collective-permute-start(f32[8,16]{1,0:T(8,128)} %s0_ref.1), channel_id=1, source_target_pairs={{0,16},{8,24},{16,0},{24,8},{1,17},{9,25},{17,1},{25,9},{2,18},{10... | collective-permute-start | bytes 1544 | tf_op jit(solution)/shard_map/ppermute | solution.py:251
  3.7 3.6 %collective-permute-start = (f32[8,16]{1,0:T(8,128)}, f32[8,16]{1,0:T(8,128)S(1)}, u32[]{:S(2)}, u32[]{:S(2)}) collective-permute-start(f32[8,16]{1,0:T(8,128)} %s0_ref.1), channel_id=1, source_target_pairs={{0,8},{8,0},{16,24},{24,16},{1,9},{9,1},{17,25},{25,17},{2,10},{10... | collective-permute-start | bytes 1544 | tf_op jit(solution)/shard_map/ppermute | solution.py:251
  4.7 4.7 %collective-permute-start.2 = (f32[8,16]{1,0:T(8,128)}, f32[8,16]{1,0:T(8,128)S(1)}, u32[]{:S(2)}, u32[]{:S(2)}) collective-permute-start(f32[8,16]{1,0:T(8,128)} %s0_ref.1), channel_id=1, source_target_pairs={{0,24},{8,16},{16,8},{24,0},{1,25},{9,17},{17,9},{25,1},{2,26},{10... | collective-permute-start | bytes 1544 | tf_op jit(solution)/shard_map/ppermute | solution.py:251
  61.1 26.1 %copy-start = (f32[128,64]{0,1:T(8,128)S(1)}, f32[128,64]{0,1:T(8,128)}, u32[]{:S(2)}) copy-start(f32[128,64]{0,1:T(8,128)} %param.10) | copy-start | bytes 98308

commit v13 on v12

--- a/solution.py
+++ b/solution.py
@@ -10,7 +10,6 @@
 CHUNK = 49
 WIDE = 65
 VMEM_SMALL = 16 * 2**20
-VMEM_ALONE = 56 * 2**20
 VMEM_LARGE = 32 * 2**20
 
 
@@ -45,20 +44,8 @@
 
 
 def spectrum_kernel(
-    spec_hbm, core_hbm, in_hbm, first_hbm, third_hbm, out_ref, half_ref, by_z_ref,
-    spec_ref, core_ref, in_ref, first_ref, third_ref, sems,
+    spec_ref, core_ref, in_ref, first_ref, third_ref, out_ref, half_ref, by_z_ref
 ):
-    def copy(source, target, n):
-        made = pltpu.make_async_copy(source, target, sems.at[n])
-        made.start()
-        return made
-
-    small = [copy(first_hbm, first_ref, 0), copy(in_hbm, in_ref, 1), copy(third_hbm, third_ref, 2)]
-    parts = [copy(spec_hbm.at[:, b], spec_ref.at[:, b], 3 + b) for b in range(2)]
-    parts.append(copy(core_hbm, core_ref, 5))
-
-    for made in small:
-        made.wait()
     mine = pick_lanes(first_ref[...], 128, lambda row, col: col & 15 == row)
     mine = jnp.where(iota((8, 128), 1) >> 4 == iota((8, 128), 0), mine, 0.0)
     mine = jnp.sum(mine, axis=0, keepdims=True)
@@ -71,7 +58,6 @@
     third = pick_lanes(third_ref[...], 256, lambda row, col: col & 15 == row)
     by_z_ref[...] = pick(128, lambda row, col: row & 15 == col, third)
     for b in range(2):
-        parts[b].wait()
         for k in range(8):
             both = jnp.concatenate(
                 [spec_ref[part, b, pl.ds(k, 128, stride=8), :] for part in range(2)], axis=1
@@ -80,7 +66,6 @@
             out = out[:64] + out[64:]
             turned = jnp.concatenate([out[:, :LANES], out[:, LANES:]], axis=0).T
             out_ref[pl.ds(2 * k + b, 128, stride=CHUNK), :] = turned
-    parts[2].wait()
     for pair in range(4):
         both = jnp.concatenate(
             [core_ref[part, 2 * pair + half] for half in range(2) for part in range(2)], axis=1
@@ -91,32 +76,36 @@
 def spectrum_chunks(spec, core, factor, first, third):
     return pl.pallas_call(
         spectrum_kernel,
-        in_specs=[pl.BlockSpec(memory_space=pl.ANY)] * 5,
         out_shape=(
             pltpu.VMEM((128 * CHUNK, LANES), jnp.float32),
             pltpu.VMEM((4, 2, 256, 256), jnp.bfloat16),
             pltpu.VMEM((128, 256), jnp.float32),
         ),
-        scratch_shapes=[
-            pltpu.VMEM(spec.shape, jnp.float32),
-            pltpu.VMEM(core.shape, jnp.float32),
-            pltpu.VMEM(factor.shape, jnp.float32),
-            pltpu.VMEM(first.shape, jnp.float32),
-            pltpu.VMEM(third.shape, jnp.float32),
-            pltpu.SemaphoreType.DMA((6,)),
-        ],
-        compiler_params=pltpu.CompilerParams(vmem_limit_bytes=VMEM_ALONE),
+        compiler_params=pltpu.CompilerParams(vmem_limit_bytes=VMEM_SMALL),
         name="spectrum_chunks",
     )(spec, core, factor, first, third)
 
 
-def core_kernel(_, half_ref, by_z_ref, s0_ref, s1_ref, s2_ref, s3_ref, out_ref):
+def choice_kernel(out_ref):
     b = lax.axis_index("my")
+    row, col = iota((512, 96), 0), iota((512, 96), 1) & 31
+    out_ref[...] = (((row >> 7) ^ b) * 8 + ((row & 127) >> 4) == col).astype(jnp.bfloat16)
+
+
+def choices():
+    return pl.pallas_call(
+        choice_kernel,
+        out_shape=pltpu.VMEM((512, 96), jnp.bfloat16),
+        compiler_params=pltpu.CompilerParams(vmem_limit_bytes=VMEM_SMALL),
+        cost_estimate=pl.CostEstimate(flops=10**10, bytes_accessed=98304, transcendentals=0),
+        name="choices",
+    )()
+
+
+def core_kernel(_, half_ref, by_z_ref, one_ref, s0_ref, s1_ref, s2_ref, s3_ref, out_ref):
     seconds = jnp.concatenate([ref[...] for ref in (s0_ref, s1_ref, s2_ref, s3_ref)], axis=0)
     second = pick_lanes(seconds, 256, lambda row, col: col >> 4 == row)
-    by_y = pick(
-        512, lambda row, col: ((row >> 7) ^ b) * 8 + ((row & 127) >> 4) == col, second
-    )
+    by_y = dot(one_ref[...], jnp.concatenate(split3(second), axis=0))
     by_z = jnp.concatenate([by_z_ref[...]] * 4, axis=0)
     mat_high, mat_low = split(by_y * by_z)
     for pair in range(4):
@@ -130,16 +119,16 @@
                 ]
 
 
-def core_chunks(chunks, halves, by_z, seconds):
+def core_chunks(chunks, halves, by_z, one, seconds):
     whole = pl.BlockSpec(memory_space=pltpu.VMEM)
     return pl.pallas_call(
         core_kernel,
-        in_specs=[pl.BlockSpec(memory_space=pl.ANY)] + [whole] * 6,
+        in_specs=[pl.BlockSpec(memory_space=pl.ANY)] + [whole] * 7,
         out_shape=pltpu.VMEM((128 * CHUNK, LANES), jnp.float32),
         input_output_aliases={0: 0},
         compiler_params=pltpu.CompilerParams(vmem_limit_bytes=VMEM_SMALL),
         name="core_chunks",
-    )(chunks, halves, by_z, *seconds)
+    )(chunks, halves, by_z, one, *seconds)
 
 
 def mode_kernel(got, out_ref, w_ref):
@@ -245,6 +234,7 @@
 ):
     everyone = ("mx", "my", "col")
     count = lax.axis_size("my")
+    one = choices()
     seconds = [second_factor]
     for k in range(1, 4):
         pairs = [(b, b ^ k) for b in range(count)]
@@ -252,7 +242,7 @@
     core = jnp.transpose(core_tensor, (0, 1, 3, 4, 5, 2)).reshape(2, 8, 256, 64)
     spec = spectrum.reshape(2, 2, 1024, LANES)
     chunks, halves, by_z = spectrum_chunks(spec, core, input_factor.T, first_factor, third_factor)
-    chunks = core_chunks(chunks, halves, by_z, seconds)
+    chunks = core_chunks(chunks, halves, by_z, one, seconds)
     got = swap(chunks.reshape(128, 1, CHUNK * LANES), everyone)
     values = mode_products(got.reshape(128 * CHUNK, LANES))
     values = swap(values.reshape(128, 16, LANES), everyone)

time: 89.4 us -> 89.1 us (level)
  Pallas kernels: 8.33 us -> 6.85 us
  waiting for transfers between devices: 2.05 us -> 3.48 us
    pallas_call x1 -> x2, Pallas kernels: 2.67 us -> 1.2 us  [the longest x1 1.1 us: spectrum_chunks(): pl.pallas_call(spectrum_kernel, out_shape=(pltpu.VMEM((128 * CHUNK, LANES...]
    ppermute x3, waiting for transfers between devices: 2.05 us -> 3.48 us  [per_device(): seconds.append(lax.ppermute(second_factor, 'my', pairs))]
  transfers between devices with their start and end apart: 3 -> 3, of which waited for: 1 -> 1; matrix products, arithmetic and copies ran while one was open for 0% -> 0% of each run, Pallas kernels for 3% -> 1%
where the time goes in v13:
time: 89.1 us; the launch traced here: 88.9 us
  blocking collectives  73.7 us (83%)
  Pallas kernels  6.85 us (8%)
  starting transfers between devices  4.77 us (5%)
  waiting for transfers between devices  3.48 us (4%)
    all_to_all x2, blocking collectives, swap(): return lax.all_to_all(chunks, axes, split_axis=0, concat_axis=0, tiled=True)  73.7 us
    ppermute x3, starting transfers between devices, per_device(): seconds.append(lax.ppermute(second_factor, 'my', pairs))  4.77 us
    ppermute x3, waiting for transfers between devices, per_device(): seconds.append(lax.ppermute(second_factor, 'my', pairs))  3.48 us
    pallas_call x1, Pallas kernels, mode_products(): pl.pallas_call(mode_kernel, out_shape=jax.ShapeDtypeStruct((128 * 16, LAN...  2.38 us
    pallas_call x1, Pallas kernels, output_modes(): pl.pallas_call(output_kernel, out_specs=pl.BlockSpec(memory_space=pl.ANY)...  1.99 us
  transfers between devices with their start and end apart: 3, of which 1 were waited for; matrix products, arithmetic and copies ran while one was open for 0% of the time, Pallas kernels for 1%

profile of v13, /device:TPU:1, one launch (start us, length us, event | category | flops | bytes accessed | tf_op | source)
XLA Modules:
  0.0 88.9 jit_solution(16115777016583617201)
XLA Ops:
  0.0 0.0 copy-start.4
  0.0 0.0 copy-start.1
  0.0 0.0 copy-start
  0.0 3.8 %collective-permute-start.1 = (f32[8,16]{1,0:T(8,128)}, f32[8,16]{1,0:T(8,128)S(1)}, u32[]{:S(2)}, u32[]{:S(2)}) collective-permute-start(f32[8,16]{1,0:T(8,128)} %s0_ref.1), channel_id=1, source_target_pairs={{0,16},{8,24},{16,0},{24,8},{1,17},{9,25},{17,1},{25,9},{2,18},{10... | collective-permute-start | bytes 1544 | tf_op jit(solution)/shard_map/ppermute | solution.py:241
  3.8 1.0 %collective-permute-start = (f32[8,16]{1,0:T(8,128)}, f32[8,16]{1,0:T(8,128)S(1)}, u32[]{:S(2)}, u32[]{:S(2)}) collective-permute-start(f32[8,16]{1,0:T(8,128)} %s0_ref.1), channel_id=1, source_target_pairs={{0,8},{8,0},{16,24},{24,16},{1,9},{9,1},{17,25},{25,17},{2,10},{10... | collective-permute-start | bytes 1544 | tf_op jit(solution)/shard_map/ppermute | solution.py:241
  4.8 0.0 collective-permute-start.2
  4.8 0.1 choices.1.one_ref
  4.9 0.0 copy-start.6
  4.9 0.0 copy-done.4
  4.9 0.0 copy-done.5
  4.9 0.0 copy-done.2
  4.9 0.0 copy-done.1
  4.9 0.0 copy-done
  5.0 1.1 %spectrum_chunks.1 = (f32[6272,128]{1,0:T(8,128)S(1)}, bf16[4,2,256,256]{3,2,1,0:T(8,128)(2,1)S(1)}, f32[128,256]{1,0:T(8,128)S(1)}) custom-call(f32[2,2,1024,128]{3,2,1,0:T(8,128)S(1)} %bitcast.15, f32[2,8,256,64]{3,2,1,0:T(8,128)S(1)} %bitcast.16, f32[64,128]{1,0:T(8,128)S(1)} %bitcast.17, f32[8,16]{1,0:T(8,128)S(1)} %copy-done.5, f32[16,16]{1,0:T(8,128)S(1)} %copy-done.4), custom_call_target="tpu_custom_call" | custom-call | tf_op jit(solution)/shard_map/spectrum_chunks/pallas_call | solution.py:77
  6.1 0.0 collective-permute-done.1.s2_ref
  6.1 0.0 collective-permute-done.s1_ref
  6.1 3.5 %collective-permute-done.2.s3_ref = f32[8,16]{1,0:T(8,128)S(1)} collective-permute-done((f32[8,16]{1,0:T(8,128)}, f32[8,16]{1,0:T(8,128)S(1)}, u32[]{:S(2)}, u32[]{:S(2)}) %collective-permute-start.2) | collective-permute-done | bytes 544 | tf_op jit(solution)/shard_map/ppermute | solution.py:241
  9.5 0.0 copy-done.6
  9.5 1.3 %core_chunks.1 = f32[6272,128]{1,0:T(8,128)S(1)} custom-call(f32[6272,128]{1,0:T(8,128)S(1)} %get-tuple-element.8._, bf16[4,2,256,256]{3,2,1,0:T(8,128)(2,1)S(1)} %get-tuple-element.9.half_ref, f32[128,256]{1,0:T(8,128)S(1)} %get-tuple-element.10.by_z_ref, bf16[512,96]{1,0:T(8,128)(2,1)S(1)} %choices.1.one_ref, ...), custom_call_target="tpu_custom_call", output_to_operand_aliasing={{}: (0, {})} | custom-call | tf_op jit(solution)/shard_map/core_chunks/pallas_call | solution.py:124
  10.8 49.9 %all_to_all.10 = f32[128,1,6272]{2,1,0:T(1,128)S(1)} all-to-all(f32[128,1,6272]{2,1,0:T(1,128)S(1)} %bitcast.12), channel_id=1, replica_groups=mesh['mx'=4,'my'=4,'col'=8] {'mx','my','col'}, dimensions={0} | all-to-all | bytes 6422528 | tf_op jit(solution)/shard_map/all_to_all | solution.py:229
  60.8 2.4 %mode_products.1 = f32[2048,128]{1,0:T(8,128)S(1)} custom-call(f32[6272,128]{1,0:T(8,128)S(1)} %bitcast.11), custom_call_target="tpu_custom_call" | custom-call | tf_op jit(solution)/shard_map/mode_products/pallas_call | solution.py:187
  63.2 23.8 %all_to_all.11 = f32[128,16,128]{2,1,0:T(8,128)S(1)} all-to-all(f32[128,16,128]{2,1,0:T(8,128)S(1)} %bitcast.14), channel_id=1, replica_groups=mesh['mx'=4,'my'=4,'col'=8] {'mx','my','col'}, dimensions={0} | all-to-all | bytes 2097152 | tf_op jit(solution)/shard_map/all_to_all | solution.py:229
  86.9 0.0 copy-done.3
  86.9 2.0 %output_modes.1 = f32[2,2,1024,128]{3,2,1,0:T(8,128)} custom-call(f32[2048,128]{1,0:T(8,128)S(1)} %bitcast.13, f32[64,128]{1,0:T(8,128)S(1)} %bitcast.18), custom_call_target="tpu_custom_call" | custom-call | tf_op jit(solution)/shard_map/output_modes/pallas_call | solution.py:218
  (3 shorter events, 0.0 us)
Async XLA Ops:
  0.0 4.9 %copy-start.4 = (f32[16,16]{1,0:T(8,128)S(1)}, f32[16,16]{1,0:T(8,128)}, u32[]{:S(2)}) copy-start(f32[16,16]{1,0:T(8,128)} %third_ref.1) | copy-start | bytes 3076
  0.0 4.9 %copy-start.5 = (f32[8,16]{1,0:T(8,128)S(1)}, f32[8,16]{1,0:T(8,128)}, u32[]{:S(2)}) copy-start(f32[8,16]{1,0:T(8,128)} %first_ref.1) | copy-start | bytes 1540
  0.0 4.9 %copy-start.2 = (f32[128,64]{0,1:T(8,128)S(1)}, f32[128,64]{0,1:T(8,128)}, u32[]{:S(2)}) copy-start(f32[128,64]{0,1:T(8,128)} %param.9) | copy-start | bytes 98308
  0.0 4.9 %copy-start.1 = (f32[2,8,64,1,16,16]{2,5,4,3,1,0:T(8,128)S(1)}, f32[2,8,64,1,16,16]{2,5,4,3,1,0:T(8,128)}, u32[]{:S(2)}) copy-start(f32[2,8,64,1,16,16]{2,5,4,3,1,0:T(8,128)} %param.8) | copy-start | bytes 3145732
  0.0 4.9 %copy-start = (f32[2,2,128,8,128]{4,3,2,1,0:T(8,128)S(1)}, f32[2,2,128,8,128]{4,3,2,1,0:T(8,128)}, u32[]{:S(2)}) copy-start(f32[2,2,128,8,128]{4,3,2,1,0:T(8,128)} %param.7) | copy-start | bytes 6291460
  0.0 6.0 %collective-permute-start.1 = (f32[8,16]{1,0:T(8,128)}, f32[8,16]{1,0:T(8,128)S(1)}, u32[]{:S(2)}, u32[]{:S(2)}) collective-permute-start(f32[8,16]{1,0:T(8,128)} %s0_ref.1), channel_id=1, source_target_pairs={{0,16},{8,24},{16,0},{24,8},{1,17},{9,25},{17,1},{25,9},{2,18},{10... | collective-permute-start | bytes 1544 | tf_op jit(solution)/shard_map/ppermute | solution.py:241
  3.8 2.2 %collective-permute-start = (f32[8,16]{1,0:T(8,128)}, f32[8,16]{1,0:T(8,128)S(1)}, u32[]{:S(2)}, u32[]{:S(2)}) collective-permute-start(f32[8,16]{1,0:T(8,128)} %s0_ref.1), channel_id=1, source_target_pairs={{0,8},{8,0},{16,24},{24,16},{1,9},{9,1},{17,25},{25,17},{2,10},{10... | collective-permute-start | bytes 1544 | tf_op jit(solution)/shard_map/ppermute | solution.py:241
  4.8 4.7 %collective-permute-start.2 = (f32[8,16]{1,0:T(8,128)}, f32[8,16]{1,0:T(8,128)S(1)}, u32[]{:S(2)}, u32[]{:S(2)}) collective-permute-start(f32[8,16]{1,0:T(8,128)} %s0_ref.1), channel_id=1, source_target_pairs={{0,24},{8,16},{16,8},{24,0},{1,25},{9,17},{17,9},{25,1},{2,26},{10... | collective-permute-start | bytes 1544 | tf_op jit(solution)/shard_map/ppermute | solution.py:241
  4.9 4.7 %copy-start.6 = (f32[8,16]{1,0:T(8,128)S(1)}, f32[8,16]{1,0:T(8,128)}, u32[]{:S(2)}) copy-start(f32[8,16]{1,0:T(8,128)} %s0_ref.1) | copy-start | bytes 1540
  60.8 26.2 %copy-start.3 = (f32[128,64]{0,1:T(8,128)S(1)}, f32[128,64]{0,1:T(8,128)}, u32[]{:S(2)}) copy-start(f32[128,64]{0,1:T(8,128)} %param.10) | copy-start | bytes 98308
